TPU v7x, 256 devices: a whole 4x4x8 slice. The times are simulated.
256 devices in a mesh: band: 32 (over y_hi, z, core), fft: 8 (over x, y_lo).
Axes of the slice: x: 4, y: 4 (y_hi: 2, y_lo: 2; y = y_hi * 2 + y_lo), z: 8, core: 2. Of those that a mesh axis runs over, the one named last changes fastest.
Arguments:
- coefficients: float32 [32, 2, 72, 5184], P('band', None, None, 'fft'), may hold values from -0.009765625 to 0.009765625
- col_index: int32 [5184], replicated, may hold values from 0 to 5183, each once
- occupation: int32 [32], P('band'), may hold values from 1 to 4
Outputs:
- density: float32 [288, 288, 288], P('band', 'fft')
Inputs may be any that keep to these rules, and one draw needn't show every extreme that they name: `col_index`: each number of the range appears once.
All inputs are finite; a program needn't handle non-finite values.
Results may differ from a plain program's by a relative error of at most 0.0003.
Values sent between devices are 32-bit elements; how exact they have to be, the bound alone decides.
A program may use at most 64 MiB of HBM per device.

v0:
```python
import math

import jax
import jax.numpy as jnp
from jax import lax
from jax.sharding import PartitionSpec as P

NC = 144
NF = 288
KZ = 72
NCOLS = 5184


def split_up(value, dim, count):
    before, after = (value.shape[:dim], value.shape[dim + 1 :])
    return jnp.moveaxis(value.reshape(*before, count, -1, *after), dim, 0)


def sum_at_owner(value, axis, dim):
    parts = split_up(value, dim, lax.axis_size(axis))
    arrived = lax.all_to_all(parts, axis, split_axis=0, concat_axis=0, tiled=True)
    return arrived.sum(axis=0)


def product(pattern, operand_a, operand_b):
    return jnp.einsum(pattern, operand_a, operand_b, precision=lax.Precision.HIGHEST)


def phase_tables(wave_count, offset, points):
    wave_index = jnp.arange(wave_count, dtype=jnp.int32) - offset
    grid_index = jnp.arange(points, dtype=jnp.int32)
    phases = jnp.mod(wave_index[:, None] * grid_index[None, :], points)
    angles = phases.astype(jnp.float32) * (2.0 * math.pi / points)
    return (jnp.cos(angles), jnp.sin(angles))


def interpolation_matrix(coarse_len, fine_len):
    fine_index = jnp.arange(fine_len, dtype=jnp.int32)
    coarse_index = jnp.arange(coarse_len, dtype=jnp.int32)
    wave_index = jnp.arange(1, coarse_len // 2, dtype=jnp.int32)
    offsets = fine_index[:, None] - 2 * coarse_index[None, :]
    phases = jnp.mod(offsets[:, :, None] * wave_index[None, None, :], fine_len)
    angles = phases.astype(jnp.float32) * (2.0 * math.pi / fine_len)
    return (1.0 + 2.0 * jnp.sum(jnp.cos(angles), axis=2)) / coarse_len


def rotate(pattern, real_part, imag_part, cos_table, sin_table):
    out_real = product(pattern, real_part, cos_table) - product(pattern, imag_part, sin_table)
    out_imag = product(pattern, real_part, sin_table) + product(pattern, imag_part, cos_table)
    return (out_real, out_imag)


def local(coefficients, col_index, occupation):
    band_here = coefficients.shape[0]
    col_count = coefficients.shape[3]
    band_total = band_here * lax.axis_size("band")
    radius = KZ // 2
    col_start = lax.axis_index("fft") * col_count
    local_cols = lax.dynamic_slice_in_dim(col_index, col_start, col_count)
    first_wave = local_cols // KZ - radius
    second_wave = local_cols % KZ - radius
    third_wave = jnp.arange(KZ, dtype=jnp.int32) - radius
    radial = (first_wave * first_wave + second_wave * second_wave)[None, :] + (
        third_wave * third_wave
    )[:, None]
    inside = (radial <= radius * radius).astype(jnp.float32)
    masked = coefficients * inside
    cos_table, sin_table = phase_tables(KZ, radius, NC)
    line_real, line_imag = rotate("bkc,kz->bzc", masked[:, 0], masked[:, 1], cos_table, sin_table)
    z_lines = jnp.stack([line_real, line_imag], axis=1)
    inverse = jnp.zeros((NCOLS,), jnp.int32).at[col_index].set(jnp.arange(NCOLS, dtype=jnp.int32))
    block_in = lax.all_to_all(z_lines, "fft", split_axis=2, concat_axis=3, tiled=True)
    box_grid = jnp.take(block_in, inverse, axis=3)
    box_grid = box_grid.reshape(block_in.shape[0], 2, block_in.shape[2], KZ, KZ)
    half_real, half_imag = rotate(
        "bzak,kr->bzar", box_grid[:, 0], box_grid[:, 1], cos_table, sin_table
    )
    full_real, full_imag = rotate("bzar,as->bzsr", half_real, half_imag, cos_table, sin_table)
    moduli = full_real * full_real + full_imag * full_imag
    weights = occupation.astype(jnp.float32) / band_total
    partial_value = product("b,bzxy->zxy", weights, moduli)
    interpolation = interpolation_matrix(NC, NF)
    section_one = product("zab,ga->zgb", partial_value, interpolation)
    shared = sum_at_owner(section_one, "band", 1)
    reduced = product("zgb,fb->zgf", shared, interpolation)
    return product(
        "rgf,hr->gfh",
        lax.all_to_all(reduced, "fft", split_axis=2, concat_axis=0, tiled=True),
        interpolation,
    )


def solution(mesh):
    return jax.shard_map(
        local,
        mesh=mesh,
        in_specs=(P("band", None, None, "fft"), P(), P("band")),
        out_specs=P("band", "fft", None),
        check_vma=False,
    )
```

profile of v0, /device:TPU:32, one launch (start us, length us, event | category | flops | bytes accessed | tf_op | source)
XLA Modules:
  0.0 300.1 jit_solution(10613181250059869739)
XLA Ops:
  0.0 0.8 fusion.110
  0.8 0.1 fusion.15
  0.9 1.1 broadcast_multiply_fusion
  2.0 0.8 fusion.17
  2.8 0.8 fusion.16
  3.6 0.8 fusion.8
  4.4 0.8 fusion.7
  5.2 0.0 copy-start
  5.2 0.1 pad_maximum_fusion
  5.3 1.6 copy.37
  6.9 5.3 %all-to-all-start = ((f32[1,2,144,648]{3,1,0,2:T(2,128)}), f32[1,2,144,648]{3,1,0,2:T(2,128)S(1)}, u32[]{:S(2)}, u32[]{:S(2)}) async-start(f32[1,2,144,648]{3,1,0,2:T(2,128)} %copy.37), calls=%async_computation | async-start | bytes 1769472 | tf_op jit(solution)/shard_map/all_to_all | solution.py:72
  12.2 0.0 copy-done
  12.2 25.5 %scatter_custom_fusion = s32[5184]{0:T(1024)S(1)} fusion(s32[5184]{0:T(1024)S(1)} %compare_select_fusion.1, s32[5184]{0:T(1024)S(1)} %iota.59, s32[]{:T(128)} %constant.51.clone.1), kind=kCustom, calls=%fused_computation.107 | custom fusion | bytes 20740 | tf_op jit(solution)/shard_map/scatter | solution.py:71
  37.8 0.1 broadcast_in_dim.27
  38.5 0.1 iota_subtract_fusion
  38.6 61.0 %fusion.3 = f32[288,144]{0,1:T(8,128)S(1)} fusion(s32[71]{0:T(128)S(1)} %iota_add_fusion.1, s32[288,144]{0,1:T(8,128)S(1)} %iota_subtract_fusion), kind=kLoop, calls=%fused_computation.6 | loop fusion | flops 29403648 | bytes 332060 | tf_op jit(solution)/shard_map/reduce_sum | solution.py:44
  99.6 0.0 all-to-all-done
  99.6 4.8 %copy.56 = f32[1,2,18,8,648]{2,1,4,3,0:T(2,128)} copy(f32[1,2,18,8,648]{4,1,2,3,0:T(2,128)S(1)} %bitcast.93) | data formatting | bytes 1492992 | tf_op jit(solution)/shard_map/all_to_all | solution.py:72
  104.4 19.3 %gather_fusion = f32[5184,2,18]{2,1,0:T(2,128)} fusion(f32[2,18,5184]{1,0,2:T(2,128)} %bitcast.92, s32[6144]{0:T(1024)S(1)} %pad_clamp_fusion), kind=kCustom, calls=%fused_computation | custom fusion | bytes 1513728 | tf_op jit(solution)/shard_map/jit(_take)/gather | solution.py:73
  123.7 7.0 %copy.41 = f32[1,2,18,72,72]{4,3,2,1,0:T(8,128)S(1)} copy(f32[1,2,18,72,72]{2,1,4,3,0:T(2,128)} %bitcast.91) | data formatting | bytes 1492992 | tf_op jit(solution)/shard_map/jit(_take)/gather | solution.py:73
  130.7 0.1 broadcast_select_fusion
  130.8 1.5 fusion.9
  132.3 1.5 fusion.10
  133.8 1.5 convolution_subtract_fusion
  135.3 2.5 fusion.39
  137.8 2.5 fusion.31
  140.3 1.5 convolution_add_fusion
  141.9 2.7 fusion.33
  144.6 3.2 %multiply_bitcast_fusion = f32[18,144,144]{2,1,0:T(8,128)S(1)} fusion(f32[144,18,144]{2,0,1:T(8,128)S(1)} %fusion.31, f32[144,18,144]{2,0,1:T(8,128)S(1)} %fusion.39, f32[144,18,144]{2,0,1:T(8,128)S(1)} %fusion.33, f32[18,72,144]{2,1,0:T(8,128)S(1)} %convolution_add_fusion, f32[]{:T(128)} %bitcast, s32[72]{0:T(128)S(1)} %iota_add_fusion), kind=kOutput, calls=%fused_computation.11 | convolution fusion | flops 324819072 | bytes 6718756 | tf_op jit(solution)/shard_map/bzar,as->bzsr/dot_general | solution.py:26
  147.8 2.6 copy.46
  150.4 8.1 %fusion.18 = f32[288,2592]{0,1} fusion(f32[144,2592]{0,1:T(8,128)} %bitcast.88, f32[288,144]{0,1:T(8,128)S(1)} %fusion.3), kind=kOutput, calls=%fused_computation.37 | convolution fusion | flops 1290069504 | bytes 4644864
  158.4 8.5 %copy.47 = f32[18,288,144]{2,0,1:T(8,128)} copy(f32[18,288,144]{1,2,0:T(8,128)} %bitcast.87) | data formatting | bytes 5971968 | tf_op jit(solution)/shard_map/zab,ga->zgb/transpose | solution.py:26
  166.9 8.6 %reshape.196 = f32[32,1,23328]{2,1,0:T(1,128)} reshape(f32[32,9,18,144]{3,2,1,0:T(8,128)} %bitcast.86) | data formatting | bytes 5971968
  175.5 83.3 %all_to_all.41 = f32[32,1,23328]{2,1,0:T(1,128)S(1)} all-to-all(f32[32,1,23328]{2,1,0:T(1,128)} %reshape.196), channel_id=1, replica_groups=mesh['band'=32,'fft'=8] {'band'}, dimensions={0} | all-to-all | bytes 5971968 | tf_op jit(solution)/shard_map/all_to_all | solution.py:21
  258.8 0.5 broadcast.120
  259.3 10.2 %reduce = f32[32,23328]{1,0:T(8,128)} reduce(f32[32,1,23328]{2,1,0:T(1,128)S(1)} %all_to_all.41, f32[]{:T(128)} %broadcast.120), dimensions={1}, to_apply=%all_to_all.33.reduce_sub_computation | reduce | bytes 5971972 | tf_op jit(solution)/shard_map/all_to_all | solution.py:21
  269.5 7.1 %reshape.197 = f32[32,9,18,144]{3,2,1,0:T(8,128)} reshape(f32[32,23328]{1,0:T(8,128)} %reduce) | data formatting | bytes 5971968
  276.6 3.5 %bitcast_reduce_fusion = f32[18,9,144]{2,0,1:T(8,128)S(1)} fusion(f32[32,9,18,144]{3,2,1,0:T(8,128)} %reshape.197), kind=kLoop, calls=%fused_computation.168 | loop fusion | flops 723168 | bytes 3079296 | tf_op jit(solution)/shard_map/reduce_sum | solution.py:22
  280.1 0.5 fusion.13
  280.7 1.4 copy.48
  282.1 0.9 reshape.198
  283.0 11.5 %all_to_all.42 = f32[8,1,5832]{2,1,0:T(1,128)S(1)} all-to-all(f32[8,1,5832]{2,1,0:T(1,128)S(1)} %reshape.198), channel_id=1, replica_groups=mesh['band'=32,'fft'=8] {'fft'}, dimensions={0} | all-to-all | bytes 373248 | tf_op jit(solution)/shard_map/all_to_all | solution.py:88
  294.5 1.1 reduce.1
  295.6 0.8 reshape.199
  296.4 1.0 copy.49
  297.4 0.1 all_to_all.37
  297.4 2.4 fusion.11
  (9 shorter events, 0.1 us)
Async XLA Ops:
  5.2 7.0 %copy-start = (s32[5184]{0:T(1024)S(1)}, s32[5184]{0:T(1024)}, u32[]{:S(2)}) copy-start(s32[5184]{0:T(1024)} %param.4) | copy-start | bytes 62212
  6.9 92.7 %all-to-all-start = ((f32[1,2,144,648]{3,1,0,2:T(2,128)}), f32[1,2,144,648]{3,1,0,2:T(2,128)S(1)}, u32[]{:S(2)}, u32[]{:S(2)}) async-start(f32[1,2,144,648]{3,1,0,2:T(2,128)} %copy.37), calls=%async_computation | async-start | bytes 1769472 | tf_op jit(solution)/shard_map/all_to_all | solution.py:72
where the time goes:
time: 305 us; the launch traced here: 300 us
  blocking collectives  94.8 us (31%)
  local copies, waits for them, and re-layouts  89.6 us (29%)
  other arithmetic  78.1 us (26%)
  matrix products  31.1 us (10%)
  starting transfers between devices  5.3 us (2%)
    all_to_all x1, blocking collectives, sum_at_owner(): lax.all_to_all(parts, axis, split_axis=0, concat_axis=0, tiled=True)  83.3 us
    reduce_sum x1, other arithmetic, interpolation_matrix(): return (1.0 + 2.0 * jnp.sum(jnp.cos(angles), axis=2)) / coarse_len  61 us
    gather x2, local copies, waits for them, and re-layouts, local(): box_grid = jnp.take(block_in, inverse, axis=3)  26.2 us
    scatter x1, local copies, waits for them, and re-layouts, local(): jnp.zeros((NCOLS,), jnp.int32).at[col_index]  25.5 us
    dot_general x14, matrix products, product(): jnp.einsum(pattern, operand_a, operand_b, precision=lax.Precision.HIGHEST)  23 us
    unnamed x6, local copies, waits for them, and re-layouts  17.3 us
    all_to_all x1, blocking collectives, local(): lax.all_to_all(reduced, 'fft', split_axis=2, concat_axis=0, tiled=True)  11.5 us
    all_to_all x1, other arithmetic, sum_at_owner(): lax.all_to_all(parts, axis, split_axis=0, concat_axis=0, tiled=True)  10.2 us
  transfers between devices with their start and end apart: 1, of which 0 were waited for; matrix products, arithmetic and copies ran while one was open for 29% of the time, Pallas kernels for 0%

commit v1 on v0

v1 whole, which is shorter than its diff:
```python
import functools
import math

import jax
import jax.numpy as jnp
import numpy as np
from jax import lax
from jax.experimental import pallas as pl
from jax.experimental.pallas import tpu as pltpu
from jax.sharding import PartitionSpec as P

NC = 144
NF = 288
KZ = 72
R = 36
NCOLS = 5184
LC = 648
NP = 18
HALF = 1408
BF16 = jnp.bfloat16
F32 = jnp.float32
MESH = pl.DeviceIdType.MESH


def hi_lo(table):
    table = np.asarray(table, np.float64)
    hi = table.astype(np.float32).astype(jnp.bfloat16)
    lo = (table - hi.astype(np.float64)).astype(np.float32).astype(jnp.bfloat16)
    return hi, lo


def phases(points):
    k = np.arange(KZ) - R
    ang = 2.0 * np.pi * ((k[:, None] * np.arange(points)[None, :]) % points) / points
    return np.cos(ang), np.sin(ang)


def interpolation():
    d = np.arange(NF)[:, None] - 2 * np.arange(NC)[None, :]
    k = np.arange(1, NC // 2)
    ang = 2.0 * np.pi * ((d[:, :, None] * k) % NF) / NF
    return (1.0 + 2.0 * np.cos(ang).sum(axis=2)) / NC


def line_table():
    cos, sin = phases(NC)
    w = np.zeros((2, KZ, 8, 128))
    for j in range(8):
        c, s = cos[:, NP * j : NP * j + NP], sin[:, NP * j : NP * j + NP]
        w[0, :, j, :NP] = c
        w[1, :, j, :NP] = -s
        w[0, :, j, NP : 2 * NP] = s
        w[1, :, j, NP : 2 * NP] = c
    return hi_lo(w.reshape(2 * KZ, 1024))


def stacked(table):
    hi, lo = hi_lo(table)
    return np.concatenate([hi, hi, lo], axis=1)


def first_table():
    cos, sin = phases(NC)
    return stacked(np.block([[cos.T, -sin.T], [sin.T, cos.T]]))


def second_tables():
    cos, sin = phases(NC)
    ch, cl = hi_lo(cos)
    sh, sl = hi_lo(sin)
    return ch, cl, sh, sl


def owner_rows():
    m = interpolation()
    rows = np.zeros((8, 5, 8, NC))
    for zc in range(8):
        for y in range(2):
            for c in range(2):
                g = NC * y + 18 * zc + 9 * c
                rows[zc, 2 * y + c] = m[g : g + 8]
                rows[zc, 4, 2 * y + c] = m[g + 8]
    return stacked(rows.reshape(320, NC))


def split(x):
    hi = x.astype(BF16)
    lo = (x - hi.astype(F32)).astype(BF16)
    return hi, lo


def dot(a, b):
    return jnp.dot(a, b, preferred_element_type=F32)


def lines_kernel(coef_ref, radial_ref, wh_ref, wl_ref, out_ref):
    k = lax.broadcasted_iota(jnp.int32, (KZ, LC), 0).astype(F32) - R
    inside = k * k + radial_ref[...] <= float(R * R)
    x = jnp.concatenate(
        [jnp.where(inside, coef_ref[0, 0], 0.0), jnp.where(inside, coef_ref[0, 1], 0.0)], axis=0
    )
    xt = x.T
    hi, lo = split(xt)
    for j in range(8):
        cols = slice(128 * j, 128 * j + 128)
        wh, wl = wh_ref[:, cols], wl_ref[:, cols]
        y = dot(hi, wh) + dot(lo, wh) + dot(hi, wl)
        out_ref[j] = (
            y[0:216] + pltpu.roll(y[216:432], 36, 1) + pltpu.roll(y[432:648], 72, 1)
        )


def lines(coefficients, radial):
    wh, wl = line_table()
    return pl.pallas_call(
        lines_kernel,
        out_shape=jax.ShapeDtypeStruct((8, 216, 128), F32),
        in_specs=[pl.BlockSpec(memory_space=pltpu.VMEM)] * 4,
        out_specs=pl.BlockSpec(memory_space=pltpu.VMEM),
        compiler_params=pltpu.CompilerParams(vmem_limit_bytes=40 * 2**20),
    )(coefficients, radial, jnp.asarray(wh), jnp.asarray(wl))


def planes_kernel(
    recv_ref, cols_ref, occ_ref, ch_ref, cl_ref, sh_ref, sl_ref, t2_ref, m3_ref,
    out_ref, rows_ref, grid_ref, g_ref, hall_ref,
):
    def unpack(s, carry):
        block = recv_ref[s]
        base = s * LC
        rows_ref[pl.ds(base, 216), :] = block
        rows_ref[pl.ds(base + 216, 216), :] = pltpu.roll(block, 128 - 36, 1)
        rows_ref[pl.ds(base + 432, 216), :] = pltpu.roll(block, 128 - 72, 1)
        return carry

    lax.fori_loop(0, 8, unpack, 0)

    def scatter(i, carry):
        for u in range(16):
            n = i * 16 + u
            grid_ref[pl.ds(cols_ref[n], 1), :] = rows_ref[pl.ds(n, 1), :]
        return carry

    lax.fori_loop(0, NCOLS // 16, scatter, 0)

    def turn(k0, carry):
        block = grid_ref[pl.ds(k0 * KZ, 128), :]
        t = block.T
        g_ref[pl.ds(k0, 36, stride=KZ), :] = t[0:36]
        return carry

    lax.fori_loop(0, KZ, turn, 0)

    ch, cl, sh, sl = ch_ref[...], cl_ref[...], sh_ref[...], sl_ref[...]
    for h in range(2):
        hall_ref[:, HALF * h + 9 * NC : HALF * (h + 1)] = jnp.zeros((NC, HALF - 9 * NC), F32)
    for part in range(6):
        rows = 3 * KZ
        re_h, re_l = split(g_ref[rows * part : rows * (part + 1), 0:KZ])
        im_h, im_l = split(g_ref[NP * KZ + rows * part : NP * KZ + rows * (part + 1), 0:KZ])
        half_re = (dot(re_h, ch) + dot(re_l, ch) + dot(re_h, cl)) - (
            dot(im_h, sh) + dot(im_l, sh) + dot(im_h, sl)
        )
        half_im = (dot(re_h, sh) + dot(re_l, sh) + dot(re_h, sl)) + (
            dot(im_h, ch) + dot(im_l, ch) + dot(im_h, cl)
        )
        for u in range(3):
            z = 3 * part + u
            lane = HALF * (z // 9) + NC * (z % 9)
            hall_ref[0:KZ, lane : lane + NC] = half_re[KZ * u : KZ * (u + 1)]
            hall_ref[KZ : 2 * KZ, lane : lane + NC] = half_im[KZ * u : KZ * (u + 1)]

    weight = occ_ref[0].astype(F32) * (1.0 / 32.0)
    for h in range(2):
        for start in range(0, HALF, 256):
            width = min(256, HALF - start)
            lane = slice(HALF * h + start, HALF * h + start + width)
            hh, hl = split(hall_ref[:, lane])
            hst = jnp.concatenate([hh, hl, hh], axis=0)
            psi = dot(t2_ref[...], hst)
            re, im = psi[0:NC], psi[NC : 2 * NC]
            dh, dl = split((re * re + im * im) * weight)
            dst = jnp.concatenate([dh, dl, dh], axis=0)
            s1 = dot(m3_ref[...], dst)
            out_ref[h, :, :, :, start : start + width] = s1.reshape(8, 5, 8, width)


def planes(recv, cols, occ):
    ch, cl, sh, sl = second_tables()
    smem = pl.BlockSpec(memory_space=pltpu.SMEM)
    vmem = pl.BlockSpec(memory_space=pltpu.VMEM)
    return pl.pallas_call(
        planes_kernel,
        out_shape=jax.ShapeDtypeStruct((2, 8, 5, 8, HALF), F32),
        in_specs=[vmem, smem, smem] + [vmem] * 6,
        out_specs=vmem,
        scratch_shapes=[
            pltpu.VMEM((NCOLS, 128), F32),
            pltpu.VMEM((NCOLS + 56, 128), F32),
            pltpu.VMEM((36 * KZ, 128), F32),
            pltpu.VMEM((NC, 2 * HALF), F32),
        ],
        compiler_params=pltpu.CompilerParams(vmem_limit_bytes=56 * 2**20),
    )(recv, cols, occ, *(jnp.asarray(t) for t in (ch, cl, sh, sl, first_table(), owner_rows())))


ALONE = {0: (3, 4), 1: (0, 1, 2)}


def sums_kernel(
    part_ref, mh_ref, ml_ref, out_ref,
    pair, held, sent, acc, other, tot, fin, left, fine, packed, given, got, turned,
    pair_s, pair_r, ring_s, ring_r, other_s, other_r, fin_s, fin_r, got_s, got_r,
):
    band = lax.axis_index("band")
    me = lax.axis_index("fft")
    y, zc, c = band // 16, (band // 2) % 8, band % 2

    def at(yy, zz, cc):
        return {"band": yy * 16 + zz * 2 + cc, "fft": me}

    partner = at(y, zc, 1 - c)
    ring_to = (at(y, (zc + 7) % 8, c), at(y, (zc + 1) % 8, c))
    across = at(1 - y, zc, c)
    peers = [{"band": band, "fft": (me + k) % 8} for k in range(1, 8)]

    barrier = pltpu.get_barrier_semaphore()
    everyone = [partner, *ring_to, across, *peers]
    for device in everyone:
        pl.semaphore_signal(barrier, inc=1, device_id=device, device_id_type=MESH)
    pl.semaphore_wait(barrier, len(everyone))

    def copy(src, dst, send, recv, device):
        made = pltpu.make_async_remote_copy(
            src_ref=src, dst_ref=dst, send_sem=send, recv_sem=recv, device_id=device, device_id_type=MESH
        )
        made.start()
        return made

    started = []
    pairs = {}
    for rel in (4, 5, 3, 6, 2, 7, 1, 0):
        pairs[rel] = copy(
            part_ref.at[1 - c, (zc + rel) % 8], pair.at[rel], pair_s.at[rel], pair_r.at[rel], partner
        )
        started.append(pairs[rel])

    group = (2 * (1 - y), 2 * (1 - y) + 1, 4, 2 * y, 2 * y + 1)
    ready = set()

    def own(rel, lg):
        if rel not in ready:
            pairs[rel].wait_recv()
            ready.add(rel)
        return part_ref[c, (zc + rel) % 8, group[lg]] + pair[rel, group[lg]]

    ring = {}
    for step in range(4):
        away = 4 - step
        for lg in range(5):
            for way in range(2):
                if step == 0 and lg not in ALONE[way]:
                    continue
                rel = (8 - away) % 8 if way == 0 else away
                value = own(rel, lg)
                before = ring.get((way, step - 1, lg))
                if before is not None:
                    before.wait_recv()
                    value = value + held[way, step - 1, lg]
                sent[way, step, lg] = value
                ring[way, step, lg] = copy(
                    sent.at[way, step, lg], held.at[way, step, lg],
                    ring_s.at[way, step, lg], ring_r.at[way, step, lg], ring_to[way],
                )
                started.append(ring[way, step, lg])
    over = []
    for lg in range(5):
        value = own(0, lg)
        for way in range(2):
            ring[way, 3, lg].wait_recv()
            value = value + held[way, 3, lg]
        acc[lg] = value
        if lg < 3:
            over.append(copy(acc.at[lg], other.at[lg], other_s.at[lg], other_r.at[lg], across))
    started += over
    for lg in range(3):
        over[lg].wait_recv()
    tot[0] = acc[3] + other[0]
    tot[1] = acc[4] + other[1]
    tot[2] = acc[2] + other[2]
    last = [
        copy(tot.at[1 - c], fin.at[c, 0], fin_s.at[0], fin_r.at[0], partner),
        copy(tot.at[2], fin.at[c, 1], fin_s.at[1], fin_r.at[1], partner),
    ]
    started += last
    fin[c, 0] = tot[c]
    fin[c, 1] = tot[2]
    for one in last:
        one.wait_recv()

    for h in range(2):
        ninth = fin[h, 1, pl.ds(2 * y + c, 1), :]
        for u in range(9):
            z = 9 * h + u
            left[8 * z : 8 * z + 8, :] = fin[h, 0, :, NC * u : NC * (u + 1)]
            left[NC + z : NC + z + 1, :] = ninth[:, NC * u : NC * (u + 1)]
    lh, ll = split(left[...])
    mh, ml = mh_ref[...], ml_ref[...]
    value = dot(lh, mh) + dot(ll, mh) + dot(lh, ml)
    for t in range(3):
        fine[t, :, 0 : min(128, NF - 128 * t)] = value[:, 128 * t : min(128 * (t + 1), NF)]
    for g in range(9):
        here = pl.ds(g, NP, stride=8) if g < 8 else pl.ds(NC, NP)
        rows = jnp.concatenate([fine[t, here, :] for t in range(3)], axis=1)
        for j in range(8):
            packed[j, 0:NP, 36 * g : 36 * g + 36] = rows[:, 36 * j : 36 * j + 36]
    for j in range(8):
        for t in range(3):
            given[j, NP * t : NP * (t + 1), :] = packed[j, 0:NP, 128 * t : 128 * (t + 1)]
    moves = []
    for k in range(1, 8):
        moves.append(
            copy(given.at[(me + k) % 8], got.at[me], got_s.at[k], got_r.at[k], peers[k - 1])
        )
    started += moves
    got[me] = given[me]
    for one in moves:
        one.wait_recv()
    for j in range(8):
        for t in range(3):
            turned[NP * j : NP * (j + 1), 128 * t : 128 * (t + 1)] = got[j, NP * t : NP * (t + 1), :]
    rh, rl = split(turned[...].T)
    for g in range(9):
        a, b = rh[36 * g : 36 * g + 36], rl[36 * g : 36 * g + 36]
        out_ref[g] = dot(a, mh) + dot(b, mh) + dot(a, ml)
    for one in started:
        one.wait_send()


def sums(part):
    mh, ml = hi_lo(interpolation().T)
    vmem = pl.BlockSpec(memory_space=pltpu.VMEM)
    dma = pltpu.SemaphoreType.DMA
    block = (5, 8, HALF)
    return pl.pallas_call(
        sums_kernel,
        out_shape=jax.ShapeDtypeStruct((9, 36, NF), F32),
        in_specs=[vmem] * 3,
        out_specs=vmem,
        scratch_shapes=[
            pltpu.VMEM((8, *block), F32),
            pltpu.VMEM((2, 4, *block), F32),
            pltpu.VMEM((2, 4, *block), F32),
            pltpu.VMEM(block, F32),
            pltpu.VMEM((3, 8, HALF), F32),
            pltpu.VMEM((3, 8, HALF), F32),
            pltpu.VMEM((2, 2, 8, HALF), F32),
            pltpu.VMEM((168, NC), F32),
            pltpu.VMEM((3, 168, 128), F32),
            pltpu.VMEM((8, 24, 384), F32),
            pltpu.VMEM((8, 56, 128), F32),
            pltpu.VMEM((8, 56, 128), F32),
            pltpu.VMEM((NC, 384), F32),
            dma((8,)), dma((8,)),
            dma((2, 4, 5)), dma((2, 4, 5)),
            dma((3,)), dma((3,)),
            dma((2,)), dma((2,)),
            dma((8,)), dma((8,)),
        ],
        compiler_params=pltpu.CompilerParams(
            collective_id=0, has_side_effects=True, vmem_limit_bytes=40 * 2**20
        ),
    )(part, jnp.asarray(mh), jnp.asarray(ml))


def local(coefficients, col_index, occupation):
    mine = lax.dynamic_slice_in_dim(col_index, lax.axis_index("fft") * LC, LC)
    k0, k1 = mine // KZ - R, mine % KZ - R
    radial = (k0 * k0 + k1 * k1).astype(F32)[None, :]
    packed = lines(coefficients, radial)
    recv = lax.all_to_all(packed, "fft", 0, 0)
    return sums(planes(recv, col_index, occupation))


def solution(mesh):
    return jax.shard_map(
        local,
        mesh=mesh,
        in_specs=(P("band", None, None, "fft"), P(), P("band")),
        out_specs=P("band", "fft", None),
        check_vma=False,
    )
```

time: 305 us -> 90 us (0.30)
  the two profiles are of different devices: /device:TPU:32 before, /device:TPU:1 now
where the time goes in v1:
time: 90 us; the launch traced here: 89.6 us
  Pallas kernels  63.1 us (70%)
  waiting for transfers between devices  12.4 us (14%)
  local copies, waits for them, and re-layouts  6.67 us (7%)
  starting transfers between devices  5.99 us (7%)
    pallas_call x1, Pallas kernels, sums(): pl.pallas_call(sums_kernel, out_shape=jax.ShapeDtypeStruct((9, 36, NF), F...  39.3 us
    pallas_call x1, Pallas kernels, planes(): pl.pallas_call(planes_kernel, out_shape=jax.ShapeDtypeStruct((2, 8, 5, 8,...  20.4 us
    all_to_all x1, waiting for transfers between devices, local(): recv = lax.all_to_all(packed, 'fft', 0, 0)  12.4 us
    unnamed x15, local copies, waits for them, and re-layouts  6.66 us
    all_to_all x1, starting transfers between devices, local(): recv = lax.all_to_all(packed, 'fft', 0, 0)  5.99 us
    pallas_call x1, Pallas kernels, lines(): pl.pallas_call(lines_kernel, out_shape=jax.ShapeDtypeStruct((8, 216, 128)...  3.41 us
  transfers between devices with their start and end apart: 1, of which 1 were waited for; matrix products, arithmetic and copies ran while one was open for 0% of the time, Pallas kernels for 0%

profile of v1, /device:TPU:1, one launch (start us, length us, event | category | flops | bytes accessed | tf_op | source)
XLA Modules:
  0.0 89.6 jit_solution(18186337488698409573)
XLA Ops:
  0.0 0.8 fusion.3
  0.8 0.0 copy-start.1
  0.8 1.0 %copy-done.1 = f32[1,2,72,648]{3,2,1,0:T(8,128)S(1)} copy-done((f32[1,2,72,648]{3,2,1,0:T(8,128)S(1)}, f32[1,2,72,648]{3,2,1,0:T(8,128)}, u32[]{:S(2)}) %copy-start.1) | copy-done | bytes 373272
  1.8 0.0 copy-start.2
  1.8 1.0 %copy-done.2 = bf16[144,1024]{1,0:T(8,128)(2,1)S(1)} copy-done((bf16[144,1024]{1,0:T(8,128)(2,1)S(1)}, bf16[144,1024]{1,0:T(8,128)(2,1)}, u32[]{:S(2)}) %copy-start.2) | copy-done | bytes 294936
  2.8 0.0 copy-start.3
  2.8 1.0 %copy-done.3 = bf16[144,1024]{1,0:T(8,128)(2,1)S(1)} copy-done((bf16[144,1024]{1,0:T(8,128)(2,1)S(1)}, bf16[144,1024]{1,0:T(8,128)(2,1)}, u32[]{:S(2)}) %copy-start.3) | copy-done | bytes 294936
  3.7 3.4 %shard_map.127 = f32[8,216,128]{2,1,0:T(8,128)} custom-call(f32[1,2,72,648]{3,2,1,0:T(8,128)S(1)} %copy-done.1, f32[1,648]{1,0:T(1,128)S(1)} %broadcast_in_dim.3.radial_ref, bf16[144,1024]{1,0:T(8,128)(2,1)S(1)} %copy-done.3, bf16[144,1024]{1,0:T(8,128)(2,1)S(1)} %copy-done.2), custom_call_target="tpu_custom_call" | custom-call | tf_op jit(solution)/shard_map/pallas_call | solution.py:115
  7.1 0.0 copy-start.4
  7.1 0.0 copy-start.5
  7.2 6.0 %all-to-all-start = ((f32[8,216,128]{2,1,0:T(8,128)}), f32[8,216,128]{2,1,0:T(8,128)S(1)}, u32[]{:S(2)}, u32[]{:S(2)}) async-start(f32[8,216,128]{2,1,0:T(8,128)} %shard_map.127), calls=%async_computation | async-start | bytes 1769472 | tf_op jit(solution)/shard_map/all_to_all | solution.py:381
  13.8 12.4 %all-to-all-done.recv_ref = f32[8,216,128]{2,1,0:T(8,128)S(1)} async-done(((f32[8,216,128]{2,1,0:T(8,128)}), f32[8,216,128]{2,1,0:T(8,128)S(1)}, u32[]{:S(2)}, u32[]{:S(2)}) %all-to-all-start) | async-done | bytes 884768 | tf_op jit(solution)/shard_map/all_to_all | solution.py:381
  26.1 0.0 copy-start.6
  26.1 0.9 %copy-done.6 = f32[8,216,128]{2,1,0:T(8,128)} copy-done((f32[8,216,128]{2,1,0:T(8,128)}, f32[8,216,128]{2,1,0:T(8,128)S(1)}, u32[]{:S(2)}) %copy-start.6) | copy-done | bytes 884760
  27.0 20.4 %shard_map.128.part_ref = f32[2,8,5,8,1408]{4,3,2,1,0:T(8,128)} custom-call(f32[8,216,128]{2,1,0:T(8,128)} %copy-done.6, s32[5184]{0:T(1024)} %cols_ref.1, s32[1]{0:T(128)S(6)} %copy.15.occ_ref, bf16[72,144]{1,0:T(8,128)(2,1)} %constant.55.clone.ch_ref, bf16[72,144]{1,0:T(8,128)(2,1)} %constant.56.clone.cl_ref, bf16[72,144]{1,0:T(8,128)(2,1)} %constant.57.clone.sh_ref, ...), custom_call_target="tpu_custom_call" | custom-call | tf_op jit(solution)/shard_map/pallas_call | solution.py:192
  47.5 0.0 copy-done.4
  47.5 0.0 copy-done.5
  47.5 0.0 copy-start
  47.5 2.0 %copy-done = f32[2,8,5,8,1408]{4,3,2,1,0:T(8,128)S(1)} copy-done((f32[2,8,5,8,1408]{4,3,2,1,0:T(8,128)S(1)}, f32[2,8,5,8,1408]{4,3,2,1,0:T(8,128)}, u32[]{:S(2)}) %copy-start) | copy-done | bytes 3604504
  49.5 39.3 %shard_map.129 = f32[9,36,288]{2,1,0:T(8,128)S(1)} custom-call(f32[2,8,5,8,1408]{4,3,2,1,0:T(8,128)S(1)} %copy-done, bf16[144,288]{1,0:T(8,128)(2,1)S(1)} %copy-done.5, bf16[144,288]{1,0:T(8,128)(2,1)S(1)} %copy-done.4), custom_call_target="tpu_custom_call" | custom-call | tf_op jit(solution)/shard_map/pallas_call | solution.py:345
  88.8 0.8 copy.16
  (1 shorter events, 0.0 us)
Async XLA Ops:
  0.8 1.0 %copy-start.1 = (f32[1,2,72,648]{3,2,1,0:T(8,128)S(1)}, f32[1,2,72,648]{3,2,1,0:T(8,128)}, u32[]{:S(2)}) copy-start(f32[1,2,72,648]{3,2,1,0:T(8,128)} %coef_ref.1) | copy-start | bytes 1119748
  1.8 1.0 %copy-start.2 = (bf16[144,1024]{1,0:T(8,128)(2,1)S(1)}, bf16[144,1024]{1,0:T(8,128)(2,1)}, u32[]{:S(2)}) copy-start(bf16[144,1024]{1,0:T(8,128)(2,1)} %constant.54.clone.wl_ref) | copy-start | bytes 884740
  2.8 1.0 %copy-start.3 = (bf16[144,1024]{1,0:T(8,128)(2,1)S(1)}, bf16[144,1024]{1,0:T(8,128)(2,1)}, u32[]{:S(2)}) copy-start(bf16[144,1024]{1,0:T(8,128)(2,1)} %constant.53.clone.wh_ref) | copy-start | bytes 884740
  7.1 40.3 %copy-start.4 = (bf16[144,288]{1,0:T(8,128)(2,1)S(1)}, bf16[144,288]{1,0:T(8,128)(2,1)}, u32[]{:S(2)}) copy-start(bf16[144,288]{1,0:T(8,128)(2,1)} %constant.62.clone.ml_ref) | copy-start | bytes 248836
  7.1 40.3 %copy-start.5 = (bf16[144,288]{1,0:T(8,128)(2,1)S(1)}, bf16[144,288]{1,0:T(8,128)(2,1)}, u32[]{:S(2)}) copy-start(bf16[144,288]{1,0:T(8,128)(2,1)} %constant.61.clone.mh_ref) | copy-start | bytes 248836
  7.2 19.0 %all-to-all-start = ((f32[8,216,128]{2,1,0:T(8,128)}), f32[8,216,128]{2,1,0:T(8,128)S(1)}, u32[]{:S(2)}, u32[]{:S(2)}) async-start(f32[8,216,128]{2,1,0:T(8,128)} %shard_map.127), calls=%async_computation | async-start | bytes 1769472 | tf_op jit(solution)/shard_map/all_to_all | solution.py:381
  26.1 0.9 %copy-start.6 = (f32[8,216,128]{2,1,0:T(8,128)}, f32[8,216,128]{2,1,0:T(8,128)S(1)}, u32[]{:S(2)}) copy-start(f32[8,216,128]{2,1,0:T(8,128)S(1)} %all-to-all-done.recv_ref) | copy-start | bytes 2654212
  47.5 2.0 %copy-start = (f32[2,8,5,8,1408]{4,3,2,1,0:T(8,128)S(1)}, f32[2,8,5,8,1408]{4,3,2,1,0:T(8,128)}, u32[]{:S(2)}) copy-start(f32[2,8,5,8,1408]{4,3,2,1,0:T(8,128)} %shard_map.128.part_ref) | copy-start | bytes 10813444

commit v2 on v1

v2 whole, which is shorter than its diff:
```python
import functools
import math

import jax
import jax.numpy as jnp
import numpy as np
from jax import lax
from jax.experimental import pallas as pl
from jax.experimental.pallas import tpu as pltpu
from jax.sharding import PartitionSpec as P

NC = 144
NF = 288
KZ = 72
R = 36
NCOLS = 5184
LC = 648
NP = 18
HALF = 1408
BF16 = jnp.bfloat16
F32 = jnp.float32
MESH = pl.DeviceIdType.MESH


def hi_lo(table):
    table = np.asarray(table, np.float64)
    hi = table.astype(np.float32).astype(jnp.bfloat16)
    lo = (table - hi.astype(np.float64)).astype(np.float32).astype(jnp.bfloat16)
    return hi, lo


def phases(points):
    k = np.arange(KZ) - R
    ang = 2.0 * np.pi * ((k[:, None] * np.arange(points)[None, :]) % points) / points
    return np.cos(ang), np.sin(ang)


def interpolation():
    d = np.arange(NF)[:, None] - 2 * np.arange(NC)[None, :]
    k = np.arange(1, NC // 2)
    ang = 2.0 * np.pi * ((d[:, :, None] * k) % NF) / NF
    return (1.0 + 2.0 * np.cos(ang).sum(axis=2)) / NC


def line_table():
    cos, sin = phases(NC)
    w = np.zeros((2, KZ, 3, 128))
    for d in range(16):
        c, s = cos[:, 9 * d : 9 * d + 9], sin[:, 9 * d : 9 * d + 9]
        t, lane = d // 7, 18 * (d % 7)
        w[0, :, t, lane : lane + 9] = c
        w[1, :, t, lane : lane + 9] = -s
        w[0, :, t, lane + 9 : lane + 18] = s
        w[1, :, t, lane + 9 : lane + 18] = c
    return hi_lo(w.reshape(2 * KZ, 384))


def stacked(table):
    hi, lo = hi_lo(table)
    return np.concatenate([hi, hi, lo], axis=1)


def first_table():
    cos, sin = phases(NC)
    return stacked(np.block([[cos.T, -sin.T], [sin.T, cos.T]]))


def second_tables():
    cos, sin = phases(NC)
    ch, cl = hi_lo(cos)
    sh, sl = hi_lo(sin)
    return ch, cl, sh, sl


def owner_rows():
    m = interpolation()
    rows = np.zeros((8, 5, 8, NC))
    for zc in range(8):
        for y in range(2):
            for c in range(2):
                g = NC * y + 18 * zc + 9 * c
                rows[zc, 2 * y + c] = m[g : g + 8]
                rows[zc, 4, 2 * y + c] = rows[zc, 4, 4 + 2 * y + c] = m[g + 8]
    return stacked(rows.reshape(320, NC))


def split(x):
    hi = x.astype(BF16)
    lo = (x - hi.astype(F32)).astype(BF16)
    return hi, lo


def dot(a, b):
    return jnp.dot(a, b, preferred_element_type=F32)


FAR = ((2, 1), (2, 0), (1, 1), (3, 1), (1, 0), (3, 0), (0, 1), (0, 0))


def lines_kernel(
    coef_hbm, radial_ref, occ_ref, wh_hbm, wl_hbm, out_ref,
    coef, wh, wl, lanes, given, got, load, give_s, got_r,
):
    loads = [
        pltpu.make_async_copy(src, dst, load.at[i])
        for i, (src, dst) in enumerate(((coef_hbm, coef), (wh_hbm, wh), (wl_hbm, wl)))
    ]
    for one in loads:
        one.start()
    band, me = lax.axis_index("band"), lax.axis_index("fft")
    c, x, y = band % 2, me // 2, me % 2
    targets = []
    for dx, dy in FAR:
        for dc in (1, 0):
            if (dx, dy, dc) != (0, 0, 0):
                f, cc = ((x + dx) % 4) * 2 + (y + dy) % 2, (c + dc) % 2
                targets.append((f, cc, {"band": band - c + cc, "fft": f}))
    barrier = pltpu.get_barrier_semaphore()
    for _, _, device in targets:
        pl.semaphore_signal(barrier, inc=1, device_id=device, device_id_type=MESH)

    k = lax.broadcasted_iota(jnp.int32, (KZ, LC), 0).astype(F32) - R
    inside = k * k + radial_ref[...] <= float(R * R)
    scale = jnp.sqrt(jnp.full((1, LC), occ_ref[0].astype(F32) * (1.0 / 32.0)))
    scale = jnp.where(inside, scale, 0.0)
    for one in loads:
        one.wait()
    xt = jnp.concatenate([coef[0, 0] * scale, coef[0, 1] * scale], axis=0).T
    hi, lo = split(xt)
    value = dot(hi, wh[...]) + dot(lo, wh[...]) + dot(hi, wl[...])
    for t in range(3):
        lanes[t] = value[:, 128 * t : 128 * (t + 1)]
    lane = lax.broadcasted_iota(jnp.int32, (96, 128), 1)

    def packed(d):
        t, e = d // 7, d % 7
        tile = lanes.at[t]
        result = pltpu.roll(tile[0:96, :], lax.rem(7 * 128 - 18 * e, 128), 1)
        for q in range(1, 7):
            n = 96 if q < 6 else 72
            turned = pltpu.roll(tile[96 * q : 96 * q + n, :], lax.rem(7 * 128 + 18 * q - 18 * e, 128), 1)
            if n < 96:
                turned = jnp.concatenate([turned, jnp.zeros((96 - n, 128), F32)], axis=0)
            result = jnp.where(lane >= 18 * q, turned, result)
        return result

    moves = []
    for i, (f, cc, device) in enumerate(targets):
        given[i] = packed(2 * f + cc)
        if i == 0:
            pl.semaphore_wait(barrier, len(targets))
        move = pltpu.make_async_remote_copy(
            src_ref=given.at[i], dst_ref=got.at[2 * me + c],
            send_sem=give_s.at[i], recv_sem=got_r.at[i], device_id=device, device_id_type=MESH,
        )
        move.start()
        moves.append(move)
    got[2 * me + c] = packed(2 * me + c)

    def unpack(f):
        base = f * LC
        for q in range(7):
            n = 96 if q < 6 else 72
            first = pltpu.roll(got[2 * f, 0:n, :], (128 - 18 * q) % 128, 1) if q else got[2 * f, 0:n, :]
            second = pltpu.roll(got[2 * f + 1, 0:n, :], (128 + 18 - 18 * q) % 128, 1)
            out_ref[pl.ds(base + 96 * q, n), :] = jnp.where(lane[0:n] < 18, first, second)

    for i in reversed(range(8)):
        dx, dy = FAR[i]
        for move in moves[2 * i : 2 * i + 2]:
            move.wait_recv()
        unpack(((x + 4 - dx) % 4) * 2 + (y + dy) % 2)
    for move in moves:
        move.wait_send()


def lines(coefficients, radial, occ):
    wh, wl = line_table()
    vmem = pl.BlockSpec(memory_space=pltpu.VMEM)
    hbm = pl.BlockSpec(memory_space=pltpu.HBM)
    dma = pltpu.SemaphoreType.DMA
    return pl.pallas_call(
        lines_kernel,
        out_shape=jax.ShapeDtypeStruct((NCOLS, 128), F32),
        in_specs=[hbm, vmem, pl.BlockSpec(memory_space=pltpu.SMEM), hbm, hbm],
        out_specs=vmem,
        scratch_shapes=[
            pltpu.VMEM((1, 2, KZ, LC), F32),
            pltpu.VMEM((2 * KZ, 384), BF16),
            pltpu.VMEM((2 * KZ, 384), BF16),
            pltpu.VMEM((3, LC, 128), F32),
            pltpu.VMEM((15, 96, 128), F32),
            pltpu.VMEM((16, 96, 128), F32),
            dma((3,)), dma((15,)), dma((15,)),
        ],
        compiler_params=pltpu.CompilerParams(
            collective_id=1, has_side_effects=True, vmem_limit_bytes=24 * 2**20
        ),
    )(coefficients, radial, occ, jnp.asarray(wh), jnp.asarray(wl))


def planes_kernel(
    rows_ref, cols_ref, ch_ref, cl_ref, sh_ref, sl_ref, t2_ref, m3_ref,
    out_ref, grid_ref, g_ref, hall_ref,
):
    def scatter(i, carry):
        for u in range(16):
            n = i * 16 + u
            grid_ref[pl.ds(cols_ref[n], 1), :] = rows_ref[pl.ds(n, 1), :]
        return carry

    lax.fori_loop(0, NCOLS // 16, scatter, 0)

    def turn(i, carry):
        for u in range(8):
            k0 = i * 8 + u
            t = grid_ref[pl.ds(k0 * KZ, 128), :].T
            g_ref[pl.ds(k0, 36, stride=KZ), :] = t[0:36]
        return carry

    lax.fori_loop(0, KZ // 8, turn, 0)

    ch, cl, sh, sl = ch_ref[...], cl_ref[...], sh_ref[...], sl_ref[...]
    for h in range(2):
        hall_ref[:, HALF * h + 9 * NC : HALF * (h + 1)] = jnp.zeros((NC, HALF - 9 * NC), F32)
    for part in range(6):
        h, first = part // 3, 3 * (part % 3)
        rows = 3 * KZ
        base = (18 * h + first) * KZ
        re_h, re_l = split(g_ref[base : base + rows, 0:KZ])
        base += 9 * KZ
        im_h, im_l = split(g_ref[base : base + rows, 0:KZ])
        half_re = (dot(re_h, ch) + dot(re_l, ch) + dot(re_h, cl)) - (
            dot(im_h, sh) + dot(im_l, sh) + dot(im_h, sl)
        )
        half_im = (dot(re_h, sh) + dot(re_l, sh) + dot(re_h, sl)) + (
            dot(im_h, ch) + dot(im_l, ch) + dot(im_h, cl)
        )
        for u in range(3):
            at = HALF * h + NC * (first + u)
            hall_ref[0:KZ, at : at + NC] = half_re[KZ * u : KZ * (u + 1)]
            hall_ref[KZ : 2 * KZ, at : at + NC] = half_im[KZ * u : KZ * (u + 1)]

    def interpolated(tiles):
        total = 0.0
        for h in range(2):
            field = [hall_ref[:, HALF * h + 128 * t : HALF * h + 128 * (t + 1)] for t in tiles]
            hh, hl = split(jnp.concatenate(field, axis=1))
            psi = dot(t2_ref[...], jnp.concatenate([hh, hl, hh], axis=0))
            re, im = psi[0:NC], psi[NC : 2 * NC]
            total = total + re * re + im * im
        dh, dl = split(total)
        return dot(m3_ref[...], jnp.concatenate([dh, dl, dh], axis=0))

    row = lax.broadcasted_iota(jnp.int32, (8, 128), 0)
    lane = lax.broadcasted_iota(jnp.int32, (8, 128), 1)
    for t in range(5):
        both = interpolated((t, t + 5))
        left, right = both[:, 0:128].reshape(8, 5, 8, 128), both[:, 128:256].reshape(8, 5, 8, 128)
        for p in range(4):
            out_ref[:, 10 * p + t] = left[:, p]
            out_ref[:, 10 * p + t + 5] = right[:, p]
        out_ref[:, 40 + t] = jnp.where(row[None] < 4, left[:, 4], right[:, 4])
    rest = interpolated((10,)).reshape(8, 5, 8, 128)
    for zc in range(8):
        value = rest[zc, 0]
        for p in range(1, 5):
            value = jnp.where(lane >= 16 * p, pltpu.roll(rest[zc, p], 16 * p, 1), value)
        out_ref[zc, 45] = value


def planes(rows, cols):
    ch, cl, sh, sl = second_tables()
    smem = pl.BlockSpec(memory_space=pltpu.SMEM)
    vmem = pl.BlockSpec(memory_space=pltpu.VMEM)
    return pl.pallas_call(
        planes_kernel,
        out_shape=jax.ShapeDtypeStruct((8, 46, 8, 128), F32),
        in_specs=[vmem, smem] + [vmem] * 6,
        out_specs=vmem,
        scratch_shapes=[
            pltpu.VMEM((NCOLS + 56, 128), F32),
            pltpu.VMEM((36 * KZ, 128), F32),
            pltpu.VMEM((NC, 2 * HALF), F32),
        ],
        compiler_params=pltpu.CompilerParams(vmem_limit_bytes=32 * 2**20),
    )(rows, cols, *(jnp.asarray(t) for t in (ch, cl, sh, sl, first_table(), owner_rows())))


ALONE = {0: (3, 4), 1: (0, 1, 2)}


def sums_kernel(
    part_ref, mh_ref, ml_ref, out_ref,
    held, sent, acc, other, tot, fin, left, fine, packed, given, got, turned,
    ring_s, ring_r, other_s, other_r, fin_s, fin_r, got_s, got_r,
):
    band = lax.axis_index("band")
    me = lax.axis_index("fft")
    y, zc, c = band // 16, (band // 2) % 8, band % 2

    def at(yy, zz, cc):
        return {"band": yy * 16 + zz * 2 + cc, "fft": me}

    partner = at(y, zc, 1 - c)
    ring_to = (at(y, (zc + 7) % 8, c), at(y, (zc + 1) % 8, c))
    across = at(1 - y, zc, c)
    peers = [{"band": band, "fft": (me + k) % 8} for k in range(1, 8)]

    barrier = pltpu.get_barrier_semaphore()
    everyone = [partner, *ring_to, across, *peers]
    for device in everyone:
        pl.semaphore_signal(barrier, inc=1, device_id=device, device_id_type=MESH)
    pl.semaphore_wait(barrier, len(everyone))

    def copy(src, dst, send, recv, device):
        made = pltpu.make_async_remote_copy(
            src_ref=src, dst_ref=dst, send_sem=send, recv_sem=recv, device_id=device, device_id_type=MESH
        )
        made.start()
        return made

    started = []
    theirs, mine = 20 * (1 - y), 20 * y
    group = (pl.ds(theirs, 10), pl.ds(theirs + 10, 10), pl.ds(40, 6), pl.ds(mine, 10), pl.ds(mine + 10, 10))

    ring = {}
    for step in range(4):
        away = 4 - step
        for lg in range(5):
            for way in range(2):
                if step == 0 and lg not in ALONE[way]:
                    continue
                owner = (zc + (8 - away if way == 0 else away)) % 8
                before = ring.get((way, step - 1, lg))
                if before is None:
                    src = part_ref.at[owner, group[lg]]
                else:
                    before.wait_recv()
                    sent[way, step, group[lg]] = part_ref[owner, group[lg]] + held[way, step - 1, group[lg]]
                    src = sent.at[way, step, group[lg]]
                ring[way, step, lg] = copy(
                    src, held.at[way, step, group[lg]],
                    ring_s.at[way, step, lg], ring_r.at[way, step, lg], ring_to[way],
                )
                started.append(ring[way, step, lg])
    over = []
    for lg in range(5):
        for way in range(2):
            ring[way, 3, lg].wait_recv()
        acc[group[lg]] = part_ref[zc, group[lg]] + held[0, 3, group[lg]] + held[1, 3, group[lg]]
        if lg < 3:
            there = (pl.ds(0, 10), pl.ds(10, 10), pl.ds(20, 6))[lg]
            over.append(copy(acc.at[group[lg]], other.at[there], other_s.at[lg], other_r.at[lg], across))
    started += over
    for one in over:
        one.wait_recv()
    tot[pl.ds(0, 10)] = acc[pl.ds(mine, 10)] + other[pl.ds(0, 10)]
    tot[pl.ds(10, 10)] = acc[pl.ds(mine + 10, 10)] + other[pl.ds(10, 10)]
    tot[pl.ds(20, 6)] = acc[pl.ds(40, 6)] + other[pl.ds(20, 6)]
    last = [
        copy(tot.at[pl.ds(10 * (1 - c), 10)], fin.at[c, pl.ds(0, 10)], fin_s.at[0], fin_r.at[0], partner),
        copy(tot.at[pl.ds(20, 6)], fin.at[c, pl.ds(10, 6)], fin_s.at[1], fin_r.at[1], partner),
    ]
    started += last
    fin[c, pl.ds(0, 10)] = tot[pl.ds(10 * c, 10)]
    fin[c, pl.ds(10, 6)] = tot[pl.ds(20, 6)]
    for one in last:
        one.wait_recv()

    which = 2 * y + c
    for h in range(2):
        tail = pltpu.roll(fin[h, 15], lax.rem(128 - 16 * which, 128), 1)
        main = jnp.concatenate([fin[h, t] for t in range(10)] + [tail], axis=1)
        tail = pltpu.roll(fin[h, 15, pl.ds(which, 1), :], 64, 1)
        ninth = jnp.concatenate(
            [fin[h, 10 + t, pl.ds(which, 1), :] for t in range(5)]
            + [fin[h, 10 + t, pl.ds(4 + which, 1), :] for t in range(5)]
            + [tail],
            axis=1,
        )
        for u in range(9):
            z = 9 * h + u
            left[8 * z : 8 * z + 8, :] = main[:, NC * u : NC * (u + 1)]
            left[NC + z : NC + z + 1, :] = ninth[:, NC * u : NC * (u + 1)]
    lh, ll = split(left[...])
    mh, ml = mh_ref[...], ml_ref[...]
    value = dot(lh, mh) + dot(ll, mh) + dot(lh, ml)
    for t in range(3):
        fine[t, :, 0 : min(128, NF - 128 * t)] = value[:, 128 * t : min(128 * (t + 1), NF)]
    for g in range(9):
        here = pl.ds(g, NP, stride=8) if g < 8 else pl.ds(NC, NP)
        rows = jnp.concatenate([fine[t, here, :] for t in range(3)], axis=1)
        for j in range(8):
            packed[j, 0:NP, 36 * g : 36 * g + 36] = rows[:, 36 * j : 36 * j + 36]
    for j in range(8):
        for t in range(3):
            given[j, NP * t : NP * (t + 1), :] = packed[j, 0:NP, 128 * t : 128 * (t + 1)]
    moves = []
    for k in range(1, 8):
        moves.append(
            copy(given.at[(me + k) % 8], got.at[me], got_s.at[k], got_r.at[k], peers[k - 1])
        )
    started += moves
    got[me] = given[me]
    for one in moves:
        one.wait_recv()
    for j in range(8):
        for t in range(3):
            turned[NP * j : NP * (j + 1), 128 * t : 128 * (t + 1)] = got[j, NP * t : NP * (t + 1), :]
    rh, rl = split(turned[...].T)
    for g in range(9):
        a, b = rh[36 * g : 36 * g + 36], rl[36 * g : 36 * g + 36]
        out_ref[g] = dot(a, mh) + dot(b, mh) + dot(a, ml)
    for one in started:
        one.wait_send()


def sums(part):
    mh, ml = hi_lo(interpolation().T)
    vmem = pl.BlockSpec(memory_space=pltpu.VMEM)
    dma = pltpu.SemaphoreType.DMA
    return pl.pallas_call(
        sums_kernel,
        out_shape=jax.ShapeDtypeStruct((9, 36, NF), F32),
        in_specs=[vmem] * 3,
        out_specs=vmem,
        scratch_shapes=[
            pltpu.VMEM((2, 4, 46, 8, 128), F32),
            pltpu.VMEM((2, 4, 46, 8, 128), F32),
            pltpu.VMEM((46, 8, 128), F32),
            pltpu.VMEM((26, 8, 128), F32),
            pltpu.VMEM((26, 8, 128), F32),
            pltpu.VMEM((2, 16, 8, 128), F32),
            pltpu.VMEM((168, NC), F32),
            pltpu.VMEM((3, 168, 128), F32),
            pltpu.VMEM((8, 24, 384), F32),
            pltpu.VMEM((8, 56, 128), F32),
            pltpu.VMEM((8, 56, 128), F32),
            pltpu.VMEM((NC, 384), F32),
            dma((2, 4, 5)), dma((2, 4, 5)),
            dma((3,)), dma((3,)),
            dma((2,)), dma((2,)),
            dma((8,)), dma((8,)),
        ],
        compiler_params=pltpu.CompilerParams(
            collective_id=0, has_side_effects=True, vmem_limit_bytes=24 * 2**20
        ),
    )(part, jnp.asarray(mh), jnp.asarray(ml))


def local(coefficients, col_index, occupation):
    mine = lax.dynamic_slice_in_dim(col_index, lax.axis_index("fft") * LC, LC)
    k0, k1 = mine // KZ - R, mine % KZ - R
    radial = (k0 * k0 + k1 * k1).astype(F32)[None, :]
    rows = lines(coefficients, radial, occupation)
    return sums(planes(rows, col_index))


def solution(mesh):
    return jax.shard_map(
        local,
        mesh=mesh,
        in_specs=(P("band", None, None, "fft"), P(), P("band")),
        out_specs=P("band", "fft", None),
        check_vma=False,
    )
```

time: 90 us -> 72.8 us (0.81)
  waiting for transfers between devices: 12.4 us -> 0 us
  starting transfers between devices: 5.99 us -> 0 us
  Pallas kernels: 63.1 us -> 67.2 us
  local copies, waits for them, and re-layouts: 6.67 us -> 3.66 us
    all_to_all x1 -> x0, waiting for transfers between devices: 12.4 us -> none  [local(): recv = lax.all_to_all(packed, 'fft', 0, 0)]
    pallas_call x2, Pallas kernels: 23.8 us -> 32.4 us  [the longest x1 19.1 us: lines(): pl.pallas_call(lines_kernel, out_shape=jax.ShapeDtypeStruct((NCOLS, 128),...]
    all_to_all x1 -> x0, starting transfers between devices: 5.99 us -> none  [local(): recv = lax.all_to_all(packed, 'fft', 0, 0)]
    pallas_call x1, Pallas kernels: 39.3 us -> 34.8 us  [sums(): pl.pallas_call(sums_kernel, out_shape=jax.ShapeDtypeStruct((9, 36, NF), F...]
    unnamed x15 -> x25, local copies, waits for them, and re-layouts: 6.66 us -> 3.65 us
  transfers between devices with their start and end apart: 1 -> 0, of which waited for: 1 -> 0; matrix products, arithmetic and copies ran while one was open for 0% -> 0% of each run, Pallas kernels for 0% -> 0%
where the time goes in v2:
time: 72.8 us; the launch traced here: 72.5 us
  Pallas kernels  67.2 us (92%)
  local copies, waits for them, and re-layouts  3.66 us (5%)
  between operations  0.8 us (1%)
  other arithmetic  0.79 us (1%)
    pallas_call x1, Pallas kernels, sums(): pl.pallas_call(sums_kernel, out_shape=jax.ShapeDtypeStruct((9, 36, NF), F...  34.8 us
    pallas_call x1, Pallas kernels, lines(): pl.pallas_call(lines_kernel, out_shape=jax.ShapeDtypeStruct((NCOLS, 128),...  19.1 us
    pallas_call x1, Pallas kernels, planes(): pl.pallas_call(planes_kernel, out_shape=jax.ShapeDtypeStruct((8, 46, 8, 1...  13.3 us
    unnamed x25, local copies, waits for them, and re-layouts  3.65 us

profile of v2, /device:TPU:1, one launch (start us, length us, event | category | flops | bytes accessed | tf_op | source)
XLA Modules:
  0.0 72.5 jit_solution(11920933703467298765)
XLA Ops:
  0.0 0.0 copy-start.7
  0.7 0.8 %fusion.3 = f32[648]{0:T(1024)S(1)} fusion(s32[5184]{0:T(1024)} %cols_ref.1, s32[]{:T(128)S(6)} %select_n.15), kind=kLoop, calls=%fused_computation.5 | loop fusion | flops 11664 | bytes 5188 | tf_op jit(solution)/shard_map/convert_element_type | solution.py:455
  1.5 0.0 copy-start
  1.5 1.0 %copy-done = f32[1,2,72,648]{3,2,1,0:T(8,128)S(1)} copy-done((f32[1,2,72,648]{3,2,1,0:T(8,128)S(1)}, f32[1,2,72,648]{3,2,1,0:T(8,128)}, u32[]{:S(2)}) %copy-start) | copy-done | bytes 373272
  2.5 0.0 copy-start.5
  2.5 0.9 %copy-done.5 = bf16[144,384]{1,0:T(8,128)(2,1)S(1)} copy-done((bf16[144,384]{1,0:T(8,128)(2,1)S(1)}, bf16[144,384]{1,0:T(8,128)(2,1)}, u32[]{:S(2)}) %copy-start.5) | copy-done | bytes 110616
  3.4 0.0 copy-start.6
  3.4 0.9 %copy-done.6 = bf16[144,384]{1,0:T(8,128)(2,1)S(1)} copy-done((bf16[144,384]{1,0:T(8,128)(2,1)S(1)}, bf16[144,384]{1,0:T(8,128)(2,1)}, u32[]{:S(2)}) %copy-start.6) | copy-done | bytes 110616
  4.3 0.0 copy-start.1
  4.3 0.0 copy-start.2
  4.3 0.0 copy-start.8
  4.3 0.0 copy-start.9
  4.3 0.0 copy-start.10
  4.3 0.0 copy-start.11
  4.3 19.1 %shard_map.127.rows_ref = f32[5184,128]{1,0:T(8,128)S(1)} custom-call(f32[1,2,72,648]{3,2,1,0:T(8,128)S(1)} %copy-done, f32[1,648]{1,0:T(1,128)S(1)} %broadcast_in_dim.3.radial_ref, s32[1]{0:T(128)S(6)} %copy.15.occ_ref, bf16[144,384]{1,0:T(8,128)(2,1)S(1)} %copy-done.6, bf16[144,384]{1,0:T(8,128)(2,1)S(1)} %copy-done.5), custom_call_target="tpu_custom_call" | custom-call | tf_op jit(solution)/shard_map/pallas_call | solution.py:182
  23.4 0.0 copy-done.7
  23.4 0.0 copy-done.1
  23.4 0.0 copy-done.2
  23.5 0.0 copy-done.8
  23.5 0.0 copy-done.9
  23.5 0.0 copy-done.10
  23.5 0.0 copy-done.11
  23.5 0.0 copy-start.3
  23.5 0.0 copy-start.4
  23.5 13.3 %shard_map.128.part_ref = f32[8,46,8,128]{3,2,1,0:T(8,128)S(1)} custom-call(f32[5184,128]{1,0:T(8,128)S(1)} %shard_map.127.rows_ref, s32[5184]{0:T(1024)S(1)} %copy-done.11, bf16[72,144]{1,0:T(8,128)(2,1)S(1)} %copy-done.10, bf16[72,144]{1,0:T(8,128)(2,1)S(1)} %copy-done.9, bf16[72,144]{1,0:T(8,128)(2,1)S(1)} %copy-done.8, bf16[72,144]{1,0:T(8,128)(2,1)S(1)} %copy-done.7, ...), custom_call_target="tpu_custom_call" | custom-call | tf_op jit(solution)/shard_map/pallas_call | solution.py:276
  36.8 0.0 copy-done.3
  36.8 0.0 copy-done.4
  36.8 34.8 %shard_map.129 = f32[9,36,288]{2,1,0:T(8,128)S(1)} custom-call(f32[8,46,8,128]{3,2,1,0:T(8,128)S(1)} %shard_map.128.part_ref, bf16[144,288]{1,0:T(8,128)(2,1)S(1)} %copy-done.4, bf16[144,288]{1,0:T(8,128)(2,1)S(1)} %copy-done.3), custom_call_target="tpu_custom_call" | custom-call | tf_op jit(solution)/shard_map/pallas_call | solution.py:423
  71.7 0.8 %copy.16 = f32[9,36,288]{2,1,0:T(8,128)} copy(f32[9,36,288]{2,1,0:T(8,128)S(1)} %shard_map.129) | data formatting | bytes 746496
  (1 shorter events, 0.0 us)
Async XLA Ops:
  0.0 23.4 %copy-start.7 = (bf16[72,144]{1,0:T(8,128)(2,1)S(1)}, bf16[72,144]{1,0:T(8,128)(2,1)}, u32[]{:S(2)}) copy-start(bf16[72,144]{1,0:T(8,128)(2,1)} %constant.58.clone.sl_ref) | copy-start | bytes 62212
  1.5 1.0 %copy-start = (f32[1,2,72,648]{3,2,1,0:T(8,128)S(1)}, f32[1,2,72,648]{3,2,1,0:T(8,128)}, u32[]{:S(2)}) copy-start(f32[1,2,72,648]{3,2,1,0:T(8,128)} %coef_hbm.1) | copy-start | bytes 1119748
  2.5 0.9 %copy-start.5 = (bf16[144,384]{1,0:T(8,128)(2,1)S(1)}, bf16[144,384]{1,0:T(8,128)(2,1)}, u32[]{:S(2)}) copy-start(bf16[144,384]{1,0:T(8,128)(2,1)} %constant.54.clone.wl_hbm) | copy-start | bytes 331780
  3.4 0.9 %copy-start.6 = (bf16[144,384]{1,0:T(8,128)(2,1)S(1)}, bf16[144,384]{1,0:T(8,128)(2,1)}, u32[]{:S(2)}) copy-start(bf16[144,384]{1,0:T(8,128)(2,1)} %constant.53.clone.wh_hbm) | copy-start | bytes 331780
  4.3 19.2 %copy-start.1 = (bf16[320,432]{1,0:T(8,128)(2,1)S(1)}, bf16[320,432]{1,0:T(8,128)(2,1)}, u32[]{:S(2)}) copy-start(bf16[320,432]{1,0:T(8,128)(2,1)} %constant.60.clone.m3_ref) | copy-start | bytes 829444
  4.3 19.2 %copy-start.2 = (bf16[288,432]{1,0:T(8,128)(2,1)S(1)}, bf16[288,432]{1,0:T(8,128)(2,1)}, u32[]{:S(2)}) copy-start(bf16[288,432]{1,0:T(8,128)(2,1)} %constant.59.clone.t2_ref) | copy-start | bytes 746500
  4.3 19.2 %copy-start.8 = (bf16[72,144]{1,0:T(8,128)(2,1)S(1)}, bf16[72,144]{1,0:T(8,128)(2,1)}, u32[]{:S(2)}) copy-start(bf16[72,144]{1,0:T(8,128)(2,1)} %constant.57.clone.sh_ref) | copy-start | bytes 62212
  4.3 19.2 %copy-start.9 = (bf16[72,144]{1,0:T(8,128)(2,1)S(1)}, bf16[72,144]{1,0:T(8,128)(2,1)}, u32[]{:S(2)}) copy-start(bf16[72,144]{1,0:T(8,128)(2,1)} %constant.56.clone.cl_ref) | copy-start | bytes 62212
  4.3 19.2 %copy-start.10 = (bf16[72,144]{1,0:T(8,128)(2,1)S(1)}, bf16[72,144]{1,0:T(8,128)(2,1)}, u32[]{:S(2)}) copy-start(bf16[72,144]{1,0:T(8,128)(2,1)} %constant.55.clone.ch_ref) | copy-start | bytes 62212
  4.3 19.2 %copy-start.11 = (s32[5184]{0:T(1024)S(1)}, s32[5184]{0:T(1024)}, u32[]{:S(2)}) copy-start(s32[5184]{0:T(1024)} %cols_ref.1) | copy-start | bytes 62212
  23.5 13.3 %copy-start.3 = (bf16[144,288]{1,0:T(8,128)(2,1)S(1)}, bf16[144,288]{1,0:T(8,128)(2,1)}, u32[]{:S(2)}) copy-start(bf16[144,288]{1,0:T(8,128)(2,1)} %constant.62.clone.ml_ref) | copy-start | bytes 248836
  23.5 13.3 %copy-start.4 = (bf16[144,288]{1,0:T(8,128)(2,1)S(1)}, bf16[144,288]{1,0:T(8,128)(2,1)}, u32[]{:S(2)}) copy-start(bf16[144,288]{1,0:T(8,128)(2,1)} %constant.61.clone.mh_ref) | copy-start | bytes 248836

commit v3 on v2

v3 whole, which is shorter than its diff:
```python
import functools
import math

import jax
import jax.numpy as jnp
import numpy as np
from jax import lax
from jax.experimental import pallas as pl
from jax.experimental.pallas import tpu as pltpu
from jax.sharding import PartitionSpec as P

NC = 144
NF = 288
KZ = 72
R = 36
NCOLS = 5184
LC = 648
NP = 18
HALF = 768
FIRST = (0, 5, 9, 14)
COUNT = (5, 4, 5, 4)
BF16 = jnp.bfloat16
F32 = jnp.float32
MESH = pl.DeviceIdType.MESH


def hi_lo(table):
    table = np.asarray(table, np.float64)
    hi = table.astype(np.float32).astype(jnp.bfloat16)
    lo = (table - hi.astype(np.float64)).astype(np.float32).astype(jnp.bfloat16)
    return hi, lo


def phases(points):
    k = np.arange(KZ) - R
    ang = 2.0 * np.pi * ((k[:, None] * np.arange(points)[None, :]) % points) / points
    return np.cos(ang), np.sin(ang)


def interpolation():
    d = np.arange(NF)[:, None] - 2 * np.arange(NC)[None, :]
    k = np.arange(1, NC // 2)
    ang = 2.0 * np.pi * ((d[:, :, None] * k) % NF) / NF
    return (1.0 + 2.0 * np.cos(ang).sum(axis=2)) / NC


def line_table():
    cos, sin = phases(NC)
    w = np.zeros((2, KZ, 3, 128))
    for d in range(32):
        n, z = COUNT[d % 4], NP * (d // 4) + FIRST[d % 4]
        c, s = cos[:, z : z + n], sin[:, z : z + n]
        t, lane = d // 12, 10 * (d % 12)
        w[0, :, t, lane : lane + n] = c
        w[1, :, t, lane : lane + n] = -s
        w[0, :, t, lane + 5 : lane + 5 + n] = s
        w[1, :, t, lane + 5 : lane + 5 + n] = c
    return hi_lo(w.reshape(2 * KZ, 384))


def stacked(table):
    hi, lo = hi_lo(table)
    return np.concatenate([hi, hi, lo], axis=1)


def first_table():
    cos, sin = phases(NC)
    return stacked(np.block([[cos.T, -sin.T], [sin.T, cos.T]]))


def second_tables():
    cos, sin = phases(NC)
    ch, cl = hi_lo(cos)
    sh, sl = hi_lo(sin)
    return ch, cl, sh, sl


def owner_rows():
    m = interpolation()
    rows = np.zeros((8, 5, 8, NC))
    for zc in range(8):
        for y in range(2):
            for c in range(2):
                g = NC * y + 18 * zc + 9 * c
                rows[zc, 2 * y + c] = m[g : g + 8]
                rows[zc, 4, 2 * y + c] = rows[zc, 4, 4 + 2 * y + c] = m[g + 8]
    return stacked(rows.reshape(320, NC))


def split(x):
    hi = x.astype(BF16)
    lo = (x - hi.astype(F32)).astype(BF16)
    return hi, lo


def dot(a, b):
    return jnp.dot(a, b, preferred_element_type=F32)


CHIPS = sorted(
    ((dx, dy) for dx in range(4) for dy in range(4)),
    key=lambda d: (-min(d[0], 4 - d[0]) - min(d[1], 4 - d[1]), d),
)
TARGETS = [(dx, dy, dc) for dx, dy in CHIPS for dc in (1, 0) if (dx, dy, dc) != (0, 0, 0)]


def load_tables(pairs, sems):
    loads = [pltpu.make_async_copy(src, dst, sems.at[i]) for i, (src, dst) in enumerate(pairs)]
    for one in loads:
        one.start()
    return loads


def lines_kernel(
    coef_hbm, cols_hbm, occ_ref, wh_hbm, wl_hbm, out_ref,
    coef, cols, wh, wl, lanes, given, got, load, give_s, got_r,
):
    loads = load_tables(((cols_hbm, cols), (coef_hbm, coef), (wh_hbm, wh), (wl_hbm, wl)), load)
    band, me = lax.axis_index("band"), lax.axis_index("fft")
    yh, zc, c = band // 16, (band // 2) % 8, band % 2
    x, y = me // 2, 2 * yh + me % 2
    slot = 4 * me + 2 * yh + c

    def device(xx, yy, cc):
        return {"band": (yy // 2) * 16 + zc * 2 + cc, "fft": 2 * xx + yy % 2}

    targets = [((x + dx) % 4, (y + dy) % 4, (c + dc) % 2) for dx, dy, dc in TARGETS]
    barrier = pltpu.get_barrier_semaphore()
    for target in targets:
        pl.semaphore_signal(barrier, inc=1, device_id=device(*target), device_id_type=MESH)

    loads[0].wait()
    window = cols[:, pl.ds(pl.multiple_of(640 * me, 128), 704)]
    window = jnp.concatenate([window, window[:, 0:64]], axis=1)
    box = pltpu.roll(window, lax.rem(768 - 8 * me, 768), 1)[:, 0:LC].astype(F32)
    k0 = jnp.floor((box + 0.5) * (1.0 / KZ))
    k1 = box - KZ * k0 - R
    k0 = k0 - R
    k = lax.broadcasted_iota(jnp.int32, (KZ, LC), 0).astype(F32) - R
    inside = k * k + (k0 * k0 + k1 * k1) <= float(R * R)
    scale = jnp.sqrt(jnp.full((1, LC), occ_ref[0].astype(F32) * (1.0 / 32.0)))
    scale = jnp.where(inside, scale, 0.0)
    for one in loads[1:]:
        one.wait()
    xt = jnp.concatenate([coef[0, 0] * scale, coef[0, 1] * scale], axis=0).T
    hi, lo = split(xt)
    value = dot(hi, wh[...]) + dot(lo, wh[...]) + dot(hi, wl[...])
    for t in range(3):
        lanes[t] = value[:, 128 * t : 128 * (t + 1)]
    lane = lax.broadcasted_iota(jnp.int32, (56, 128), 1)
    pieces = [(q, 56 if q < 11 else 32) for q in range(12)]

    def packed(d):
        t, e = d // 12, d % 12
        tile = lanes.at[t]
        result = None
        for q, n in pieces:
            turned = pltpu.roll(tile[56 * q : 56 * q + n, :], lax.rem(10 * 128 + 10 * q - 10 * e, 128), 1)
            if n < 56:
                turned = jnp.concatenate([turned, jnp.zeros((56 - n, 128), F32)], axis=0)
            result = turned if result is None else jnp.where(lane >= 10 * q, turned, result)
        return result

    moves = {}
    for i, target in enumerate(targets):
        xx, yy, cc = target
        given[i] = packed(4 * (2 * xx + yy % 2) + 2 * (yy // 2) + cc)
        if i == 0:
            pl.semaphore_wait(barrier, len(targets))
        move = pltpu.make_async_remote_copy(
            src_ref=given.at[i], dst_ref=got.at[slot],
            send_sem=give_s.at[i], recv_sem=got_r.at[i], device_id=device(*target), device_id_type=MESH,
        )
        move.start()
        moves[TARGETS[i]] = move
    got[slot] = packed(slot)

    def unpack(f):
        base = pl.multiple_of(f * LC, 8)
        for q, n in pieces:
            result = None
            for i in range(4):
                block = got[4 * f + i, 0:n, :]
                shift = (10 * i - 10 * q) % 128
                block = pltpu.roll(block, shift, 1) if shift else block
                result = block if i == 0 else jnp.where(lane[0:n] >= 10 * i, block, result)
            out_ref[pl.ds(base + 56 * q, n), :] = result

    for dx, odd in ((0, 1), (0, 0), (1, 1), (3, 1), (1, 0), (3, 0), (2, 1), (2, 0)):
        for dy in (odd, odd + 2):
            for dc in (0, 1):
                if (dx, dy, dc) in moves:
                    moves[dx, dy, dc].wait_recv()
        unpack(((x + 4 - dx) % 4) * 2 + (y + odd) % 2)
    for move in moves.values():
        move.wait_send()


def lines(coefficients, cols, occ):
    wh, wl = line_table()
    hbm = pl.BlockSpec(memory_space=pltpu.HBM)
    dma = pltpu.SemaphoreType.DMA
    n = len(TARGETS)
    return pl.pallas_call(
        lines_kernel,
        out_shape=jax.ShapeDtypeStruct((NCOLS, 128), F32),
        in_specs=[hbm, hbm, pl.BlockSpec(memory_space=pltpu.SMEM), hbm, hbm],
        out_specs=pl.BlockSpec(memory_space=pltpu.VMEM),
        scratch_shapes=[
            pltpu.VMEM((1, 2, KZ, LC), F32),
            pltpu.VMEM((1, NCOLS), jnp.int32),
            pltpu.VMEM((2 * KZ, 384), BF16),
            pltpu.VMEM((2 * KZ, 384), BF16),
            pltpu.VMEM((3, LC, 128), F32),
            pltpu.VMEM((n, 56, 128), F32),
            pltpu.VMEM((32, 56, 128), F32),
            dma((4,)), dma((n,)), dma((n,)),
        ],
        compiler_params=pltpu.CompilerParams(
            collective_id=1, has_side_effects=True, vmem_limit_bytes=24 * 2**20
        ),
    )(coefficients, cols, occ, jnp.asarray(wh), jnp.asarray(wl))


def planes_kernel(
    rows_ref, cols_ref, ch_hbm, cl_hbm, sh_hbm, sl_hbm, t2_hbm, m3_hbm,
    out_ref, grid_ref, g_ref, hall_ref, ch_ref, cl_ref, sh_ref, sl_ref, t2_ref, m3_ref, load,
):
    loads = load_tables(
        (
            (ch_hbm, ch_ref), (cl_hbm, cl_ref), (sh_hbm, sh_ref),
            (sl_hbm, sl_ref), (t2_hbm, t2_ref), (m3_hbm, m3_ref),
        ),
        load,
    )

    def scatter(i, carry):
        for u in range(16):
            n = i * 16 + u
            grid_ref[pl.ds(cols_ref[n], 1), :] = rows_ref[pl.ds(n, 1), :]
        return carry

    lax.fori_loop(0, NCOLS // 16, scatter, 0)

    def turn(i, carry):
        for u in range(8):
            k0 = i * 8 + u
            t = grid_ref[pl.ds(pl.multiple_of(k0 * KZ, 8), 128), :].T
            g_ref[pl.ds(k0, 40, stride=KZ), :] = t[0:40]
        return carry

    lax.fori_loop(0, KZ // 8, turn, 0)

    for one in loads:
        one.wait()
    ch, cl, sh, sl = ch_ref[...], cl_ref[...], sh_ref[...], sl_ref[...]
    rows = 5 * KZ
    for h in range(4):
        hall_ref[:, HALF * h + 5 * NC : HALF * (h + 1)] = jnp.zeros((NC, HALF - 5 * NC), F32)
        base = 10 * h * KZ
        re_h, re_l = split(g_ref[base : base + rows, 0:KZ])
        im_h, im_l = split(g_ref[base + rows : base + 2 * rows, 0:KZ])
        half_re = (dot(re_h, ch) + dot(re_l, ch) + dot(re_h, cl)) - (
            dot(im_h, sh) + dot(im_l, sh) + dot(im_h, sl)
        )
        half_im = (dot(re_h, sh) + dot(re_l, sh) + dot(re_h, sl)) + (
            dot(im_h, ch) + dot(im_l, ch) + dot(im_h, cl)
        )
        for u in range(5):
            at = HALF * h + NC * u
            hall_ref[0:KZ, at : at + NC] = half_re[KZ * u : KZ * (u + 1)]
            hall_ref[KZ : 2 * KZ, at : at + NC] = half_im[KZ * u : KZ * (u + 1)]

    row = lax.broadcasted_iota(jnp.int32, (8, 128), 0)
    for t in range(3):
        total = 0.0
        for h in range(4):
            field = [hall_ref[:, HALF * h + 128 * i : HALF * h + 128 * (i + 1)] for i in (t, t + 3)]
            hh, hl = split(jnp.concatenate(field, axis=1))
            psi = dot(t2_ref[...], jnp.concatenate([hh, hl, hh], axis=0))
            re, im = psi[0:NC], psi[NC : 2 * NC]
            total = total + (re * re + im * im)
        dh, dl = split(total)
        both = dot(m3_ref[...], jnp.concatenate([dh, dl, dh], axis=0))
        left, right = both[:, 0:128].reshape(8, 5, 8, 128), both[:, 128:256].reshape(8, 5, 8, 128)
        for p in range(4):
            out_ref[:, 6 * p + t] = left[:, p]
            out_ref[:, 6 * p + t + 3] = right[:, p]
        out_ref[:, 24 + t] = jnp.where(row[None] < 4, left[:, 4], right[:, 4])


def planes(rows, cols):
    ch, cl, sh, sl = second_tables()
    tables = (ch, cl, sh, sl, first_table(), owner_rows())
    vmem = pl.BlockSpec(memory_space=pltpu.VMEM)
    return pl.pallas_call(
        planes_kernel,
        out_shape=jax.ShapeDtypeStruct((8, 27, 8, 128), F32),
        in_specs=[vmem, pl.BlockSpec(memory_space=pltpu.SMEM)] + [pl.BlockSpec(memory_space=pltpu.HBM)] * 6,
        out_specs=vmem,
        scratch_shapes=[
            pltpu.VMEM((NCOLS + 56, 128), F32),
            pltpu.VMEM((40 * KZ, 128), F32),
            pltpu.VMEM((NC, 4 * HALF), F32),
            *(pltpu.VMEM(t.shape, BF16) for t in tables),
            pltpu.SemaphoreType.DMA((6,)),
        ],
        compiler_params=pltpu.CompilerParams(vmem_limit_bytes=32 * 2**20),
    )(rows, cols, *(jnp.asarray(t) for t in tables))


ALONE = {0: (0, 1, 2), 1: (3, 4)}


def sums_kernel(
    part_ref, mh_hbm, ml_hbm, out_ref,
    held, sent, acc, fin, left, fine, packed, given, got, turned, mh_ref, ml_ref,
    load, ring_s, ring_r, quad_s, quad_r, got_s, got_r,
):
    loads = load_tables(((mh_hbm, mh_ref), (ml_hbm, ml_ref)), load)
    band = lax.axis_index("band")
    me = lax.axis_index("fft")
    y, zc, c = band // 16, (band // 2) % 8, band % 2
    quarter = 2 * y + c

    def at(yy, zz, cc):
        return {"band": yy * 16 + zz * 2 + cc, "fft": me}

    ring_to = (at(y, (zc + 7) % 8, c), at(y, (zc + 1) % 8, c))
    others = ((1 - y, c), (1 - y, 1 - c), (y, 1 - c))
    quad = [at(yy, zc, cc) for yy, cc in others]
    peers = [{"band": band, "fft": (me + k) % 8} for k in range(1, 8)]

    barrier = pltpu.get_barrier_semaphore()
    everyone = [*ring_to, *quad, *peers]
    for device in everyone:
        pl.semaphore_signal(barrier, inc=1, device_id=device, device_id_type=MESH)
    pl.semaphore_wait(barrier, len(everyone))

    def copy(src, dst, send, recv, device):
        made = pltpu.make_async_remote_copy(
            src_ref=src, dst_ref=dst, send_sem=send, recv_sem=recv, device_id=device, device_id_type=MESH
        )
        made.start()
        return made

    started = []
    group = (
        pl.ds(24, 3),
        *(pl.ds(6 * (2 * yy + cc), 6) for yy, cc in others),
        pl.ds(6 * quarter, 6),
    )

    ring = {}
    for step in range(4):
        away = 4 - step
        for lg in range(5):
            for way in range(2):
                if step == 0 and lg not in ALONE[way]:
                    continue
                owner = (zc + (8 - away if way == 0 else away)) % 8
                before = ring.get((way, step - 1, lg))
                if before is None:
                    src = part_ref.at[owner, group[lg]]
                else:
                    before.wait_recv()
                    sent[way, step, group[lg]] = part_ref[owner, group[lg]] + held[way, step - 1, group[lg]]
                    src = sent.at[way, step, group[lg]]
                ring[way, step, lg] = copy(
                    src, held.at[way, step, group[lg]],
                    ring_s.at[way, step, lg], ring_r.at[way, step, lg], ring_to[way],
                )
                started.append(ring[way, step, lg])
    over = []
    for lg in range(5):
        for way in range(2):
            ring[way, 3, lg].wait_recv()
        acc[group[lg]] = part_ref[zc, group[lg]] + held[0, 3, group[lg]] + held[1, 3, group[lg]]
        for i in range(3):
            if lg == 0:
                there = fin.at[quarter, pl.ds(6, 3)]
            elif lg == i + 1:
                there = fin.at[quarter, pl.ds(0, 6)]
            else:
                continue
            k = 2 * i + (lg > 0)
            over.append(copy(acc.at[group[lg]], there, quad_s.at[k], quad_r.at[k], quad[i]))
    started += over
    fin[quarter, pl.ds(0, 6)] = acc[group[4]]
    fin[quarter, pl.ds(6, 3)] = acc[group[0]]
    for one in over:
        one.wait_recv()

    for s in range(4):
        main = jnp.concatenate([fin[s, t] for t in range(6)], axis=1)
        ninth = jnp.concatenate(
            [fin[s, 6 + t, pl.ds(quarter, 1), :] for t in range(3)]
            + [fin[s, 6 + t, pl.ds(4 + quarter, 1), :] for t in range(3)],
            axis=1,
        )
        for u in range(COUNT[s]):
            z = FIRST[s] + u
            left[8 * z : 8 * z + 8, :] = main[:, NC * u : NC * (u + 1)]
            left[NC + z : NC + z + 1, :] = ninth[:, NC * u : NC * (u + 1)]
    for one in loads:
        one.wait()
    lh, ll = split(left[...])
    mh, ml = mh_ref[...], ml_ref[...]
    value = dot(lh, mh) + dot(ll, mh) + dot(lh, ml)
    for t in range(3):
        fine[t, :, 0 : min(128, NF - 128 * t)] = value[:, 128 * t : min(128 * (t + 1), NF)]
    for g in range(9):
        here = pl.ds(g, NP, stride=8) if g < 8 else pl.ds(NC, NP)
        rows = jnp.concatenate([fine[t, here, :] for t in range(3)], axis=1)
        for j in range(8):
            packed[j, 0:NP, 36 * g : 36 * g + 36] = rows[:, 36 * j : 36 * j + 36]
    for j in range(8):
        for t in range(3):
            given[j, NP * t : NP * (t + 1), :] = packed[j, 0:NP, 128 * t : 128 * (t + 1)]
    moves = []
    for k in range(1, 8):
        moves.append(
            copy(given.at[(me + k) % 8], got.at[me], got_s.at[k], got_r.at[k], peers[k - 1])
        )
    started += moves
    got[me] = given[me]
    for one in moves:
        one.wait_recv()
    for j in range(8):
        for t in range(3):
            turned[NP * j : NP * (j + 1), 128 * t : 128 * (t + 1)] = got[j, NP * t : NP * (t + 1), :]
    rh, rl = split(turned[...].T)
    for g in range(9):
        a, b = rh[36 * g : 36 * g + 36], rl[36 * g : 36 * g + 36]
        out_ref[g] = dot(a, mh) + dot(b, mh) + dot(a, ml)
    for one in started:
        one.wait_send()


def sums(part):
    mh, ml = hi_lo(interpolation().T)
    vmem = pl.BlockSpec(memory_space=pltpu.VMEM)
    dma = pltpu.SemaphoreType.DMA
    return pl.pallas_call(
        sums_kernel,
        out_shape=jax.ShapeDtypeStruct((9, 36, NF), F32),
        in_specs=[vmem] + [pl.BlockSpec(memory_space=pltpu.HBM)] * 2,
        out_specs=vmem,
        scratch_shapes=[
            pltpu.VMEM((2, 4, 27, 8, 128), F32),
            pltpu.VMEM((2, 4, 27, 8, 128), F32),
            pltpu.VMEM((27, 8, 128), F32),
            pltpu.VMEM((4, 9, 8, 128), F32),
            pltpu.VMEM((168, NC), F32),
            pltpu.VMEM((3, 168, 128), F32),
            pltpu.VMEM((8, 24, 384), F32),
            pltpu.VMEM((8, 56, 128), F32),
            pltpu.VMEM((8, 56, 128), F32),
            pltpu.VMEM((NC, 384), F32),
            pltpu.VMEM((NC, NF), BF16),
            pltpu.VMEM((NC, NF), BF16),
            dma((2,)),
            dma((2, 4, 5)), dma((2, 4, 5)),
            dma((6,)), dma((6,)),
            dma((8,)), dma((8,)),
        ],
        compiler_params=pltpu.CompilerParams(
            collective_id=0, has_side_effects=True, vmem_limit_bytes=24 * 2**20
        ),
    )(part, jnp.asarray(mh), jnp.asarray(ml))


def local(coefficients, col_index, occupation):
    rows = lines(coefficients, col_index[None, :], occupation)
    return sums(planes(rows, col_index))


def solution(mesh):
    return jax.shard_map(
        local,
        mesh=mesh,
        in_specs=(P("band", None, None, "fft"), P(), P("band")),
        out_specs=P("band", "fft", None),
        check_vma=False,
    )
```

time: 72.8 us -> 74.5 us (1.023)
  Pallas kernels: 67.2 us -> 69 us
  other arithmetic: 0.79 us -> 0 us
  local copies, waits for them, and re-layouts: 3.66 us -> 4.41 us
    pallas_call x1, Pallas kernels: 19.1 us -> 24.1 us  [lines(): pl.pallas_call(lines_kernel, out_shape=jax.ShapeDtypeStruct((NCOLS, 128),...]
    pallas_call x1, Pallas kernels: 34.8 us -> 31.7 us  [sums(): pl.pallas_call(sums_kernel, out_shape=jax.ShapeDtypeStruct((9, 36, NF), F...]
    convert_element_type x1 -> x0, other arithmetic: 0.79 us -> none  [local(): radial = (k0 * k0 + k1 * k1).astype(F32)[None, :]]
    broadcast_in_dim x1, local copies, waits for them, and re-layouts: 0.01 us -> 0.75 us  [local(): rows = lines(coefficients, col_index[None, :], occupation)]
where the time goes in v3:
time: 74.5 us; the launch traced here: 74.3 us
  Pallas kernels  69 us (93%)
  local copies, waits for them, and re-layouts  4.41 us (6%)
  between operations  0.81 us (1%)
    pallas_call x1, Pallas kernels, sums(): pl.pallas_call(sums_kernel, out_shape=jax.ShapeDtypeStruct((9, 36, NF), F...  31.7 us
    pallas_call x1, Pallas kernels, lines(): pl.pallas_call(lines_kernel, out_shape=jax.ShapeDtypeStruct((NCOLS, 128),...  24.1 us
    pallas_call x1, Pallas kernels, planes(): pl.pallas_call(planes_kernel, out_shape=jax.ShapeDtypeStruct((8, 27, 8, 1...  13.2 us
    unnamed x25, local copies, waits for them, and re-layouts  3.65 us

profile of v3, /device:TPU:1, one launch (start us, length us, event | category | flops | bytes accessed | tf_op | source)
XLA Modules:
  0.0 74.3 jit_solution(14644899151057124827)
XLA Ops:
  0.0 0.0 copy-start.7
  0.7 0.8 %broadcast_in_dim.3.cols_hbm = s32[1,5184]{1,0:T(1,128)S(1)} reshape(s32[5184]{0:T(1024)} %cols_ref.1) | data formatting | bytes 41472 | tf_op jit(solution)/shard_map/broadcast_in_dim | solution.py:474
  1.4 0.0 copy-start
  1.4 1.0 %copy-done = f32[1,2,72,648]{3,2,1,0:T(8,128)S(1)} copy-done((f32[1,2,72,648]{3,2,1,0:T(8,128)S(1)}, f32[1,2,72,648]{3,2,1,0:T(8,128)}, u32[]{:S(2)}) %copy-start) | copy-done | bytes 373272
  2.4 0.0 copy-start.5
  2.4 0.9 %copy-done.5 = bf16[144,384]{1,0:T(8,128)(2,1)S(1)} copy-done((bf16[144,384]{1,0:T(8,128)(2,1)S(1)}, bf16[144,384]{1,0:T(8,128)(2,1)}, u32[]{:S(2)}) %copy-start.5) | copy-done | bytes 110616
  3.3 0.0 copy-start.6
  3.3 0.9 %copy-done.6 = bf16[144,384]{1,0:T(8,128)(2,1)S(1)} copy-done((bf16[144,384]{1,0:T(8,128)(2,1)S(1)}, bf16[144,384]{1,0:T(8,128)(2,1)}, u32[]{:S(2)}) %copy-start.6) | copy-done | bytes 110616
  4.2 0.0 copy-start.1
  4.2 0.0 copy-start.2
  4.2 0.0 copy-start.8
  4.2 0.0 copy-start.9
  4.2 0.0 copy-start.10
  4.3 0.0 copy-start.11
  4.3 24.1 %shard_map.127.rows_ref = f32[5184,128]{1,0:T(8,128)S(1)} custom-call(f32[1,2,72,648]{3,2,1,0:T(8,128)S(1)} %copy-done, s32[1,5184]{1,0:T(1,128)S(1)} %broadcast_in_dim.3.cols_hbm, s32[1]{0:T(128)S(6)} %copy.15.occ_ref, bf16[144,384]{1,0:T(8,128)(2,1)S(1)} %copy-done.6, bf16[144,384]{1,0:T(8,128)(2,1)S(1)} %copy-done.5), custom_call_target="tpu_custom_call" | custom-call | tf_op jit(solution)/shard_map/pallas_call | solution.py:204
  28.3 0.0 copy-done.7
  28.4 0.0 copy-done.1
  28.4 0.0 copy-done.2
  28.4 0.0 copy-done.8
  28.4 0.0 copy-done.9
  28.4 0.0 copy-done.10
  28.4 0.0 copy-done.11
  28.4 0.0 copy-start.3
  28.4 0.0 copy-start.4
  28.4 13.2 %shard_map.128.part_ref = f32[8,27,8,128]{3,2,1,0:T(8,128)S(1)} custom-call(f32[5184,128]{1,0:T(8,128)S(1)} %shard_map.127.rows_ref, s32[5184]{0:T(1024)S(1)} %copy-done.7, bf16[72,144]{1,0:T(8,128)(2,1)S(1)} %copy-done.11, bf16[72,144]{1,0:T(8,128)(2,1)S(1)} %copy-done.10, bf16[72,144]{1,0:T(8,128)(2,1)S(1)} %copy-done.9, bf16[72,144]{1,0:T(8,128)(2,1)S(1)} %copy-done.8, ...), custom_call_target="tpu_custom_call" | custom-call | tf_op jit(solution)/shard_map/pallas_call | solution.py:296
  41.7 0.0 copy-done.3
  41.7 0.0 copy-done.4
  41.7 31.7 %shard_map.129 = f32[9,36,288]{2,1,0:T(8,128)S(1)} custom-call(f32[8,27,8,128]{3,2,1,0:T(8,128)S(1)} %shard_map.128.part_ref, bf16[144,288]{1,0:T(8,128)(2,1)S(1)} %copy-done.4, bf16[144,288]{1,0:T(8,128)(2,1)S(1)} %copy-done.3), custom_call_target="tpu_custom_call" | custom-call | tf_op jit(solution)/shard_map/pallas_call | solution.py:444
  73.5 0.8 %copy.16 = f32[9,36,288]{2,1,0:T(8,128)} copy(f32[9,36,288]{2,1,0:T(8,128)S(1)} %shard_map.129) | data formatting | bytes 746496
Async XLA Ops:
  0.0 28.3 %copy-start.7 = (s32[5184]{0:T(1024)S(1)}, s32[5184]{0:T(1024)}, u32[]{:S(2)}) copy-start(s32[5184]{0:T(1024)} %cols_ref.1) | copy-start | bytes 62212
  1.4 1.0 %copy-start = (f32[1,2,72,648]{3,2,1,0:T(8,128)S(1)}, f32[1,2,72,648]{3,2,1,0:T(8,128)}, u32[]{:S(2)}) copy-start(f32[1,2,72,648]{3,2,1,0:T(8,128)} %coef_hbm.1) | copy-start | bytes 1119748
  2.4 0.9 %copy-start.5 = (bf16[144,384]{1,0:T(8,128)(2,1)S(1)}, bf16[144,384]{1,0:T(8,128)(2,1)}, u32[]{:S(2)}) copy-start(bf16[144,384]{1,0:T(8,128)(2,1)} %constant.21.clone.wl_hbm) | copy-start | bytes 331780
  3.3 0.9 %copy-start.6 = (bf16[144,384]{1,0:T(8,128)(2,1)S(1)}, bf16[144,384]{1,0:T(8,128)(2,1)}, u32[]{:S(2)}) copy-start(bf16[144,384]{1,0:T(8,128)(2,1)} %constant.20.clone.wh_hbm) | copy-start | bytes 331780
  4.2 24.1 %copy-start.1 = (bf16[320,432]{1,0:T(8,128)(2,1)S(1)}, bf16[320,432]{1,0:T(8,128)(2,1)}, u32[]{:S(2)}) copy-start(bf16[320,432]{1,0:T(8,128)(2,1)} %constant.27.clone.m3_hbm) | copy-start | bytes 829444
  4.2 24.1 %copy-start.2 = (bf16[288,432]{1,0:T(8,128)(2,1)S(1)}, bf16[288,432]{1,0:T(8,128)(2,1)}, u32[]{:S(2)}) copy-start(bf16[288,432]{1,0:T(8,128)(2,1)} %constant.26.clone.t2_hbm) | copy-start | bytes 746500
  4.2 24.1 %copy-start.8 = (bf16[72,144]{1,0:T(8,128)(2,1)S(1)}, bf16[72,144]{1,0:T(8,128)(2,1)}, u32[]{:S(2)}) copy-start(bf16[72,144]{1,0:T(8,128)(2,1)} %constant.25.clone.sl_hbm) | copy-start | bytes 62212
  4.2 24.2 %copy-start.9 = (bf16[72,144]{1,0:T(8,128)(2,1)S(1)}, bf16[72,144]{1,0:T(8,128)(2,1)}, u32[]{:S(2)}) copy-start(bf16[72,144]{1,0:T(8,128)(2,1)} %constant.24.clone.sh_hbm) | copy-start | bytes 62212
  4.2 24.2 %copy-start.10 = (bf16[72,144]{1,0:T(8,128)(2,1)S(1)}, bf16[72,144]{1,0:T(8,128)(2,1)}, u32[]{:S(2)}) copy-start(bf16[72,144]{1,0:T(8,128)(2,1)} %constant.23.clone.cl_hbm) | copy-start | bytes 62212
  4.3 24.2 %copy-start.11 = (bf16[72,144]{1,0:T(8,128)(2,1)S(1)}, bf16[72,144]{1,0:T(8,128)(2,1)}, u32[]{:S(2)}) copy-start(bf16[72,144]{1,0:T(8,128)(2,1)} %constant.22.clone.ch_hbm) | copy-start | bytes 62212
  28.4 13.3 %copy-start.3 = (bf16[144,288]{1,0:T(8,128)(2,1)S(1)}, bf16[144,288]{1,0:T(8,128)(2,1)}, u32[]{:S(2)}) copy-start(bf16[144,288]{1,0:T(8,128)(2,1)} %constant.29.clone.ml_hbm) | copy-start | bytes 248836
  28.4 13.3 %copy-start.4 = (bf16[144,288]{1,0:T(8,128)(2,1)S(1)}, bf16[144,288]{1,0:T(8,128)(2,1)}, u32[]{:S(2)}) copy-start(bf16[144,288]{1,0:T(8,128)(2,1)} %constant.28.clone.mh_hbm) | copy-start | bytes 248836

commit v4 on v3

v4 whole, which is shorter than its diff:
```python
import functools
import math

import jax
import jax.numpy as jnp
import numpy as np
from jax import lax
from jax.experimental import pallas as pl
from jax.experimental.pallas import tpu as pltpu
from jax.sharding import PartitionSpec as P

NC = 144
NF = 288
KZ = 72
R = 36
NCOLS = 5184
LC = 648
NP = 18
HALF = 768
FIRST = (0, 5, 9, 14)
COUNT = (5, 4, 5, 4)
LINES_VMEM = 32 * 2**20
GRID_VMEM = 16 * 2**20
DENSITY_VMEM = 32 * 2**20
BF16 = jnp.bfloat16
F32 = jnp.float32
MESH = pl.DeviceIdType.MESH


def hi_lo(table):
    table = np.asarray(table, np.float64)
    hi = table.astype(np.float32).astype(jnp.bfloat16)
    lo = (table - hi.astype(np.float64)).astype(np.float32).astype(jnp.bfloat16)
    return hi, lo


def phases(points):
    k = np.arange(KZ) - R
    ang = 2.0 * np.pi * ((k[:, None] * np.arange(points)[None, :]) % points) / points
    return np.cos(ang), np.sin(ang)


def interpolation():
    d = np.arange(NF)[:, None] - 2 * np.arange(NC)[None, :]
    k = np.arange(1, NC // 2)
    ang = 2.0 * np.pi * ((d[:, :, None] * k) % NF) / NF
    return (1.0 + 2.0 * np.cos(ang).sum(axis=2)) / NC


def line_table():
    cos, sin = phases(NC)
    w = np.zeros((2, KZ, 3, 128))
    for d in range(32):
        n, z = COUNT[d % 4], NP * (d // 4) + FIRST[d % 4]
        c, s = cos[:, z : z + n], sin[:, z : z + n]
        t, lane = d // 12, 10 * (d % 12)
        w[0, :, t, lane : lane + n] = c
        w[1, :, t, lane : lane + n] = -s
        w[0, :, t, lane + 5 : lane + 5 + n] = s
        w[1, :, t, lane + 5 : lane + 5 + n] = c
    return np.concatenate(hi_lo(w.reshape(2 * KZ, 384)), axis=0)


def stacked(table):
    hi, lo = hi_lo(table)
    return np.concatenate([hi, hi, lo], axis=1)


def first_table():
    cos, sin = phases(NC)
    return stacked(np.block([[cos.T, -sin.T], [sin.T, cos.T]]))


def second_tables():
    cos, sin = phases(NC)
    ch, cl = hi_lo(cos)
    sh, sl = hi_lo(sin)
    return ch, cl, sh, sl


def owner_rows():
    m = interpolation()
    rows = np.zeros((8, 5, 8, NC))
    for zc in range(8):
        for y in range(2):
            for c in range(2):
                g = NC * y + 18 * zc + 9 * c
                rows[zc, 2 * y + c] = m[g : g + 8]
                rows[zc, 4, 2 * y + c] = rows[zc, 4, 4 + 2 * y + c] = m[g + 8]
    return stacked(rows.reshape(320, NC))


def split(x):
    hi = x.astype(BF16)
    lo = (x - hi.astype(F32)).astype(BF16)
    return hi, lo


def dot(a, b):
    return jnp.dot(a, b, preferred_element_type=F32)


CHIPS = sorted(
    ((dx, dy) for dx in range(4) for dy in range(4)),
    key=lambda d: (-min(d[0], 4 - d[0]) - min(d[1], 4 - d[1]), d),
)
TARGETS = [(dx, dy, dc) for dx, dy in CHIPS for dc in (1, 0) if (dx, dy, dc) != (0, 0, 0)]


def load_tables(pairs, sems):
    loads = [pltpu.make_async_copy(src, dst, sems.at[i]) for i, (src, dst) in enumerate(pairs)]
    for one in loads:
        one.start()
    return loads


def lines_kernel(
    coef_hbm, cols_hbm, occ_ref, w_hbm, out_ref,
    coef, cols, w, lanes, given, got, load, give_s, got_r,
):
    loads = load_tables(((cols_hbm, cols), (coef_hbm, coef), (w_hbm, w)), load)
    band, me = lax.axis_index("band"), lax.axis_index("fft")
    yh, zc, c = band // 16, (band // 2) % 8, band % 2
    x, y = me // 2, 2 * yh + me % 2
    slot = 4 * me + 2 * yh + c

    def device(xx, yy, cc):
        return {"band": (yy // 2) * 16 + zc * 2 + cc, "fft": 2 * xx + yy % 2}

    targets = [((x + dx) % 4, (y + dy) % 4, (c + dc) % 2) for dx, dy, dc in TARGETS]
    barrier = pltpu.get_barrier_semaphore()
    for target in targets:
        pl.semaphore_signal(barrier, inc=1, device_id=device(*target), device_id_type=MESH)

    loads[0].wait()
    window = cols[:, pl.ds(pl.multiple_of(640 * me, 128), 704)]
    window = jnp.concatenate([window, window[:, 0:64]], axis=1)
    box = pltpu.roll(window, lax.rem(768 - 8 * me, 768), 1)[:, 0:LC].astype(F32)
    k0 = jnp.floor((box + 0.5) * (1.0 / KZ))
    k1 = box - KZ * k0 - R
    k0 = k0 - R
    k = lax.broadcasted_iota(jnp.int32, (KZ, LC), 0).astype(F32) - R
    inside = k * k + (k0 * k0 + k1 * k1) <= float(R * R)
    scale = jnp.sqrt(jnp.full((1, LC), occ_ref[0].astype(F32) * (1.0 / 32.0)))
    scale = jnp.where(inside, scale, 0.0)
    for one in loads[1:]:
        one.wait()
    xt = jnp.concatenate([coef[0, 0] * scale, coef[0, 1] * scale], axis=0).T
    hi, lo = split(xt)
    wh, wl = w[0 : 2 * KZ], w[2 * KZ : 4 * KZ]
    value = dot(hi, wh) + dot(lo, wh) + dot(hi, wl)
    for t in range(3):
        lanes[t] = value[:, 128 * t : 128 * (t + 1)]
    lane = lax.broadcasted_iota(jnp.int32, (56, 128), 1)
    pieces = [(q, 56 if q < 11 else 32) for q in range(12)]

    group = jnp.zeros((56, 128), jnp.int32)
    for q in range(1, 12):
        group = group + (lane >= 10 * q).astype(jnp.int32)
    mine = 2 * yh + c

    def packed(d):
        t, e = d // 12, d % 12
        tile = lanes.at[t]
        result = None
        for q, n in pieces:
            m = lax.rem(q + mine, 12)
            turned = pltpu.roll(tile[56 * q : 56 * q + n, :], lax.rem(1280 + 10 * m - 10 * e, 128), 1)
            if n < 56:
                turned = jnp.concatenate([turned, jnp.zeros((56 - n, 128), F32)], axis=0)
            result = turned if result is None else jnp.where(group == m, turned, result)
        return result

    moves = {}
    for i, target in enumerate(targets):
        xx, yy, cc = target
        given[i] = packed(4 * (2 * xx + yy % 2) + 2 * (yy // 2) + cc)
        if i == 0:
            pl.semaphore_wait(barrier, len(targets))
        move = pltpu.make_async_remote_copy(
            src_ref=given.at[i], dst_ref=got.at[slot],
            send_sem=give_s.at[i], recv_sem=got_r.at[i], device_id=device(*target), device_id_type=MESH,
        )
        move.start()
        moves[TARGETS[i]] = move
    got[slot] = packed(slot)

    def unpack(f):
        base = pl.multiple_of(f * LC, 8)
        for q, n in pieces:
            blocks = [got[4 * f + i, 0:n, :] for i in range(4)]
            here = lane[0:n]
            straight = min(4, 12 - q)
            first = blocks[0]
            for i in range(1, straight):
                first = jnp.where(here >= 10 * (q + i), blocks[i], first)
            result = pltpu.roll(first, 128 - 10 * q, 1) if q else first
            if straight < 4:
                second = blocks[straight]
                for i in range(straight + 1, 4):
                    second = jnp.where(here >= 10 * (q + i - 12), blocks[i], second)
                second = pltpu.roll(second, 120 - 10 * q, 1) if q < 12 else second
                result = jnp.where(here >= 10 * straight, second, result)
            out_ref[pl.ds(base + 56 * q, n), :] = result

    for dx, odd in ((0, 1), (0, 0), (1, 1), (3, 1), (1, 0), (3, 0), (2, 1), (2, 0)):
        for dy in (odd, odd + 2):
            for dc in (0, 1):
                if (dx, dy, dc) in moves:
                    moves[dx, dy, dc].wait_recv()
        unpack(((x + 4 - dx) % 4) * 2 + (y + odd) % 2)
    for move in moves.values():
        move.wait_send()


def lines(coefficients, cols, occ):
    w = line_table()
    hbm = pl.BlockSpec(memory_space=pltpu.HBM)
    dma = pltpu.SemaphoreType.DMA
    n = len(TARGETS)
    return pl.pallas_call(
        lines_kernel,
        out_shape=jax.ShapeDtypeStruct((NCOLS, 128), F32),
        in_specs=[hbm, hbm, pl.BlockSpec(memory_space=pltpu.SMEM), hbm],
        out_specs=pl.BlockSpec(memory_space=pltpu.VMEM),
        scratch_shapes=[
            pltpu.VMEM((1, 2, KZ, LC), F32),
            pltpu.VMEM((1, NCOLS), jnp.int32),
            pltpu.VMEM((4 * KZ, 384), BF16),
            pltpu.VMEM((3, LC, 128), F32),
            pltpu.VMEM((n, 56, 128), F32),
            pltpu.VMEM((32, 56, 128), F32),
            dma((3,)), dma((n,)), dma((n,)),
        ],
        compiler_params=pltpu.CompilerParams(
            collective_id=1, has_side_effects=True, vmem_limit_bytes=LINES_VMEM
        ),
    )(coefficients, cols, occ, jnp.asarray(w))


def grid_kernel(rows_ref, cols_ref, out_ref, grid_ref):
    def scatter(i, carry):
        for u in range(16):
            n = i * 16 + u
            grid_ref[pl.ds(cols_ref[n], 1), :] = rows_ref[pl.ds(n, 1), :]
        return carry

    lax.fori_loop(0, NCOLS // 16, scatter, 0)

    def turn(i, carry):
        for u in range(8):
            k0 = i * 8 + u
            t = grid_ref[pl.ds(pl.multiple_of(k0 * KZ, 8), 128), :].T
            out_ref[pl.ds(k0, 40, stride=KZ), :] = t[0:40]
        return carry

    lax.fori_loop(0, KZ // 8, turn, 0)


def grid(rows, cols):
    vmem = pl.BlockSpec(memory_space=pltpu.VMEM)
    return pl.pallas_call(
        grid_kernel,
        out_shape=jax.ShapeDtypeStruct((40 * KZ, 128), F32),
        in_specs=[vmem, pl.BlockSpec(memory_space=pltpu.SMEM)],
        out_specs=vmem,
        scratch_shapes=[pltpu.VMEM((NCOLS + 56, 128), F32)],
        compiler_params=pltpu.CompilerParams(vmem_limit_bytes=GRID_VMEM),
    )(rows, cols)


def density_kernel(
    g_ref, ch_hbm, cl_hbm, sh_hbm, sl_hbm, t2_hbm, m3_hbm, mh_hbm, ml_hbm, out_ref,
    ch_ref, cl_ref, sh_ref, sl_ref, t2_ref, m3_ref, mh_ref, ml_ref,
    hall_ref, part, held, sent, acc, left, fine, packed, given, got, turned,
    load, ring_s, ring_r, got_s, got_r,
):
    loads = load_tables(
        (
            (ch_hbm, ch_ref), (cl_hbm, cl_ref), (sh_hbm, sh_ref), (sl_hbm, sl_ref),
            (t2_hbm, t2_ref), (m3_hbm, m3_ref), (mh_hbm, mh_ref), (ml_hbm, ml_ref),
        ),
        load,
    )
    band, me = lax.axis_index("band"), lax.axis_index("fft")
    yh, zc, c = band // 16, (band // 2) % 8, band % 2
    x, y = me // 2, 2 * yh + me % 2
    slot = 4 * me + 2 * yh + c

    def device(xx, yy, cc):
        return {"band": (yy // 2) * 16 + zc * 2 + cc, "fft": 2 * xx + yy % 2}

    ring_to = [{"band": yh * 16 + ((zc + d) % 8) * 2 + c, "fft": me} for d in (7, 1)]
    targets = [((x + dx) % 4, (y + dy) % 4, (c + dc) % 2) for dx, dy, dc in TARGETS]
    barrier = pltpu.get_barrier_semaphore()
    for where in [*ring_to, *(device(*target) for target in targets)]:
        pl.semaphore_signal(barrier, inc=1, device_id=where, device_id_type=MESH)

    started = []

    def copy(src, dst, send, recv, where):
        made = pltpu.make_async_remote_copy(
            src_ref=src, dst_ref=dst, send_sem=send, recv_sem=recv, device_id=where, device_id_type=MESH
        )
        made.start()
        started.append(made)
        return made

    for one in loads:
        one.wait()
    ch, cl, sh, sl = ch_ref[...], cl_ref[...], sh_ref[...], sl_ref[...]
    rows = 5 * KZ
    for h in range(4):
        hall_ref[:, HALF * h + 5 * NC : HALF * (h + 1)] = jnp.zeros((NC, HALF - 5 * NC), F32)
        base = 10 * h * KZ
        re_h, re_l = split(g_ref[base : base + rows, 0:KZ])
        im_h, im_l = split(g_ref[base + rows : base + 2 * rows, 0:KZ])
        half_re = (dot(re_h, ch) + dot(re_l, ch) + dot(re_h, cl)) - (
            dot(im_h, sh) + dot(im_l, sh) + dot(im_h, sl)
        )
        half_im = (dot(re_h, sh) + dot(re_l, sh) + dot(re_h, sl)) + (
            dot(im_h, ch) + dot(im_l, ch) + dot(im_h, cl)
        )
        for u in range(5):
            at = HALF * h + NC * u
            hall_ref[0:KZ, at : at + NC] = half_re[KZ * u : KZ * (u + 1)]
            hall_ref[KZ : 2 * KZ, at : at + NC] = half_im[KZ * u : KZ * (u + 1)]

    row = lax.broadcasted_iota(jnp.int32, (8, 128), 0)

    def chunk(t):
        total = 0.0
        for h in range(4):
            field = [hall_ref[:, HALF * h + 128 * i : HALF * h + 128 * (i + 1)] for i in (t, t + 3)]
            hh, hl = split(jnp.concatenate(field, axis=1))
            psi = dot(t2_ref[...], jnp.concatenate([hh, hl, hh], axis=0))
            re, im = psi[0:NC], psi[NC : 2 * NC]
            total = total + (re * re + im * im)
        dh, dl = split(total)
        both = dot(m3_ref[...], jnp.concatenate([dh, dl, dh], axis=0))
        first, second = both[:, 0:128].reshape(8, 5, 8, 128), both[:, 128:256].reshape(8, 5, 8, 128)
        for p in range(4):
            part[:, t, 2 * p] = first[:, p]
            part[:, t, 2 * p + 1] = second[:, p]
        part[:, t, 8] = jnp.where(row[None] < 4, first[:, 4], second[:, 4])

    alone = (pl.ds(0, 4), pl.ds(4, 5))
    ring = {}

    def hop(step, t):
        for way in range(2):
            away = 4 - step
            owner = (zc + (8 - away if way == 0 else away)) % 8
            units = alone[way] if step == 0 else pl.ds(0, 9)
            if step == 0:
                src = part.at[owner, t, units]
            else:
                ring[way, step - 1, t].wait_recv()
                src = sent.at[way, step, t]
                if step == 1:
                    rest = alone[1 - way]
                    sent[way, step, t, rest] = part[owner, t, rest]
                    sent[way, step, t, alone[way]] = part[owner, t, alone[way]] + held[way, 0, t, alone[way]]
                else:
                    sent[way, step, t] = part[owner, t] + held[way, step - 1, t]
            ring[way, step, t] = copy(
                src, held.at[way, step, t, units], ring_s.at[way, step, t], ring_r.at[way, step, t], ring_to[way]
            )

    def final(t):
        for way in range(2):
            ring[way, 3, t].wait_recv()
        acc[t] = part[zc, t] + held[0, 3, t] + held[1, 3, t]

    chunk(0)
    pl.semaphore_wait(barrier, len(targets) + 2)
    hop(0, 0)
    chunk(1)
    hop(0, 1)
    hop(1, 0)
    chunk(2)
    hop(0, 2)
    hop(1, 1)
    hop(2, 0)
    hop(1, 2)
    hop(2, 1)
    hop(3, 0)
    hop(2, 2)
    hop(3, 1)
    hop(3, 2)
    for t in range(3):
        final(t)

    for o in range(4):
        main = jnp.concatenate([acc[t, 2 * o] for t in range(3)] + [acc[t, 2 * o + 1] for t in range(3)], axis=1)
        ninth = jnp.concatenate(
            [acc[t, 8, o : o + 1, :] for t in range(3)] + [acc[t, 8, 4 + o : 5 + o, :] for t in range(3)], axis=1
        )
        for u in range(5):
            n = 5 * o + u
            left[8 * n : 8 * n + 8, :] = main[:, NC * u : NC * (u + 1)]
            left[160 + n : 161 + n, :] = ninth[:, NC * u : NC * (u + 1)]
    lh, ll = split(left[...])
    mh, ml = mh_ref[...], ml_ref[...]
    value = dot(lh, mh) + dot(ll, mh) + dot(lh, ml)
    for t in range(3):
        fine[t, :, 0 : min(128, NF - 128 * t)] = value[:, 128 * t : min(128 * (t + 1), NF)]
    for o in range(4):
        for g in range(9):
            here = pl.ds(40 * o + g, 5, stride=8) if g < 8 else pl.ds(160 + 5 * o, 5)
            line = jnp.concatenate([fine[t, here, :] for t in range(3)], axis=1)
            for j in range(8):
                packed[j, o, 0:5, 36 * g : 36 * g + 36] = line[:, 36 * j : 36 * j + 36]
    for j in range(8):
        for o in range(4):
            for t in range(3):
                given[4 * j + o, 5 * t : 5 * t + 5, :] = packed[j, o, 0:5, 128 * t : 128 * (t + 1)]
    moves = []
    for i, target in enumerate(targets):
        xx, yy, cc = target
        to = 4 * (2 * xx + yy % 2) + 2 * (yy // 2) + cc
        moves.append(copy(given.at[to], got.at[slot], got_s.at[i], got_r.at[i], device(*target)))
    got[slot] = given[slot]
    for one in moves:
        one.wait_recv()
    for j in range(8):
        for o in range(4):
            z = NP * j + FIRST[o]
            for t in range(3):
                turned[z : z + COUNT[o], 128 * t : 128 * (t + 1)] = got[4 * j + o, 5 * t : 5 * t + COUNT[o], :]
    rh, rl = split(turned[...].T)
    for g in range(9):
        a, b = rh[36 * g : 36 * g + 36], rl[36 * g : 36 * g + 36]
        out_ref[g] = dot(a, mh) + dot(b, mh) + dot(a, ml)
    for one in started:
        one.wait_send()


def density(g):
    ch, cl, sh, sl = second_tables()
    mh, ml = hi_lo(interpolation().T)
    tables = (ch, cl, sh, sl, first_table(), owner_rows(), mh, ml)
    vmem = pl.BlockSpec(memory_space=pltpu.VMEM)
    dma = pltpu.SemaphoreType.DMA
    n = len(TARGETS)
    return pl.pallas_call(
        density_kernel,
        out_shape=jax.ShapeDtypeStruct((9, 36, NF), F32),
        in_specs=[vmem] + [pl.BlockSpec(memory_space=pltpu.HBM)] * 8,
        out_specs=vmem,
        scratch_shapes=[
            *(pltpu.VMEM(t.shape, BF16) for t in tables),
            pltpu.VMEM((NC, 4 * HALF), F32),
            pltpu.VMEM((8, 3, 9, 8, 128), F32),
            pltpu.VMEM((2, 4, 3, 9, 8, 128), F32),
            pltpu.VMEM((2, 4, 3, 9, 8, 128), F32),
            pltpu.VMEM((3, 9, 8, 128), F32),
            pltpu.VMEM((184, NC), F32),
            pltpu.VMEM((3, 184, 128), F32),
            pltpu.VMEM((8, 4, 8, 384), F32),
            pltpu.VMEM((32, 16, 128), F32),
            pltpu.VMEM((32, 16, 128), F32),
            pltpu.VMEM((NC, 384), F32),
            dma((8,)),
            dma((2, 4, 3)), dma((2, 4, 3)),
            dma((n,)), dma((n,)),
        ],
        compiler_params=pltpu.CompilerParams(
            collective_id=0, has_side_effects=True, vmem_limit_bytes=DENSITY_VMEM
        ),
    )(g, *(jnp.asarray(t) for t in tables))


def local(coefficients, col_index, occupation):
    rows = lines(coefficients, col_index[None, :], occupation)
    return density(grid(rows, col_index))


def solution(mesh):
    return jax.shard_map(
        local,
        mesh=mesh,
        in_specs=(P("band", None, None, "fft"), P(), P("band")),
        out_specs=P("band", "fft", None),
        check_vma=False,
    )
```

time: 74.5 us -> 69.4 us (0.932)
  Pallas kernels: 69 us -> 64.7 us
  local copies, waits for them, and re-layouts: 4.41 us -> 3.57 us
    pallas_call x2, Pallas kernels: 45 us -> 42.3 us  [the longest x1 34.2 us: density(): pl.pallas_call(density_kernel, out_shape=jax.ShapeDtypeStruct((9, 36, NF)...]
    pallas_call x1, Pallas kernels: 24.1 us -> 22.4 us  [lines(): pl.pallas_call(lines_kernel, out_shape=jax.ShapeDtypeStruct((NCOLS, 128),...]
    unnamed x25 -> x23, local copies, waits for them, and re-layouts: 3.65 us -> 2.81 us
where the time goes in v4:
time: 69.4 us; the launch traced here: 69.1 us
  Pallas kernels  64.7 us (93%)
  local copies, waits for them, and re-layouts  3.57 us (5%)
  between operations  0.82 us (1%)
    pallas_call x1, Pallas kernels, density(): pl.pallas_call(density_kernel, out_shape=jax.ShapeDtypeStruct((9, 36, NF)...  34.2 us
    pallas_call x1, Pallas kernels, lines(): pl.pallas_call(lines_kernel, out_shape=jax.ShapeDtypeStruct((NCOLS, 128),...  22.4 us
    pallas_call x1, Pallas kernels, grid(): pl.pallas_call(grid_kernel, out_shape=jax.ShapeDtypeStruct((40 * KZ, 128)...  8.1 us
    unnamed x23, local copies, waits for them, and re-layouts  2.81 us

profile of v4, /device:TPU:1, one launch (start us, length us, event | category | flops | bytes accessed | tf_op | source)
XLA Modules:
  0.0 69.1 jit_solution(4377901010294841502)
XLA Ops:
  0.0 0.0 copy-start.6
  0.7 0.8 %broadcast_in_dim.3.cols_hbm = s32[1,5184]{1,0:T(1,128)S(1)} reshape(s32[5184]{0:T(1024)} %cols_ref.1) | data formatting | bytes 41472 | tf_op jit(solution)/shard_map/broadcast_in_dim | solution.py:475
  1.4 0.0 copy-start
  1.4 1.0 %copy-done = f32[1,2,72,648]{3,2,1,0:T(8,128)S(1)} copy-done((f32[1,2,72,648]{3,2,1,0:T(8,128)S(1)}, f32[1,2,72,648]{3,2,1,0:T(8,128)}, u32[]{:S(2)}) %copy-start) | copy-done | bytes 373272
  2.4 0.0 copy-start.3
  2.4 0.9 %copy-done.3 = bf16[288,384]{1,0:T(8,128)(2,1)S(1)} copy-done((bf16[288,384]{1,0:T(8,128)(2,1)S(1)}, bf16[288,384]{1,0:T(8,128)(2,1)}, u32[]{:S(2)}) %copy-start.3) | copy-done | bytes 221208
  3.4 22.4 %shard_map.118.rows_ref = f32[5184,128]{1,0:T(8,128)S(1)} custom-call(f32[1,2,72,648]{3,2,1,0:T(8,128)S(1)} %copy-done, s32[1,5184]{1,0:T(1,128)S(1)} %broadcast_in_dim.3.cols_hbm, s32[1]{0:T(128)S(6)} %copy.14.occ_ref, bf16[288,384]{1,0:T(8,128)(2,1)S(1)} %copy-done.3), custom_call_target="tpu_custom_call" | custom-call | tf_op jit(solution)/shard_map/pallas_call | solution.py:221
  25.8 0.0 copy-done.6
  25.8 0.0 copy-start.1
  25.8 0.0 copy-start.2
  25.9 0.0 copy-start.4
  25.9 0.0 copy-start.5
  25.9 0.0 copy-start.7
  25.9 0.0 copy-start.8
  25.9 0.0 copy-start.9
  25.9 0.0 copy-start.10
  25.9 8.1 %shard_map.119.g_ref = f32[2880,128]{1,0:T(8,128)S(1)} custom-call(f32[5184,128]{1,0:T(8,128)S(1)} %shard_map.118.rows_ref, s32[5184]{0:T(1024)S(1)} %copy-done.6), custom_call_target="tpu_custom_call" | custom-call | tf_op jit(solution)/shard_map/pallas_call | solution.py:262
  34.0 0.0 copy-done.1
  34.1 0.0 copy-done.2
  34.1 0.0 copy-done.4
  34.1 0.0 copy-done.5
  34.1 0.0 copy-done.7
  34.1 0.0 copy-done.8
  34.1 0.0 copy-done.9
  34.1 0.0 copy-done.10
  34.1 34.2 %shard_map.120 = f32[9,36,288]{2,1,0:T(8,128)S(1)} custom-call(f32[2880,128]{1,0:T(8,128)S(1)} %shard_map.119.g_ref, bf16[72,144]{1,0:T(8,128)(2,1)S(1)} %copy-done.10, bf16[72,144]{1,0:T(8,128)(2,1)S(1)} %copy-done.9, bf16[72,144]{1,0:T(8,128)(2,1)S(1)} %copy-done.8, bf16[72,144]{1,0:T(8,128)(2,1)S(1)} %copy-done.7, bf16[288,432]{1,0:T(8,128)(2,1)S(1)} %copy-done.2, ...), custom_call_target="tpu_custom_call" | custom-call | tf_op jit(solution)/shard_map/pallas_call | solution.py:446
  68.3 0.8 %copy.15 = f32[9,36,288]{2,1,0:T(8,128)} copy(f32[9,36,288]{2,1,0:T(8,128)S(1)} %shard_map.120) | data formatting | bytes 746496
Async XLA Ops:
  0.0 25.8 %copy-start.6 = (s32[5184]{0:T(1024)S(1)}, s32[5184]{0:T(1024)}, u32[]{:S(2)}) copy-start(s32[5184]{0:T(1024)} %cols_ref.1) | copy-start | bytes 62212
  1.4 1.0 %copy-start = (f32[1,2,72,648]{3,2,1,0:T(8,128)S(1)}, f32[1,2,72,648]{3,2,1,0:T(8,128)}, u32[]{:S(2)}) copy-start(f32[1,2,72,648]{3,2,1,0:T(8,128)} %coef_hbm.1) | copy-start | bytes 1119748
  2.4 0.9 %copy-start.3 = (bf16[288,384]{1,0:T(8,128)(2,1)S(1)}, bf16[288,384]{1,0:T(8,128)(2,1)}, u32[]{:S(2)}) copy-start(bf16[288,384]{1,0:T(8,128)(2,1)} %constant.18.clone.w_hbm) | copy-start | bytes 663556
  25.8 8.2 %copy-start.1 = (bf16[320,432]{1,0:T(8,128)(2,1)S(1)}, bf16[320,432]{1,0:T(8,128)(2,1)}, u32[]{:S(2)}) copy-start(bf16[320,432]{1,0:T(8,128)(2,1)} %constant.24.clone.m3_hbm) | copy-start | bytes 829444
  25.8 8.2 %copy-start.2 = (bf16[288,432]{1,0:T(8,128)(2,1)S(1)}, bf16[288,432]{1,0:T(8,128)(2,1)}, u32[]{:S(2)}) copy-start(bf16[288,432]{1,0:T(8,128)(2,1)} %constant.23.clone.t2_hbm) | copy-start | bytes 746500
  25.9 8.2 %copy-start.4 = (bf16[144,288]{1,0:T(8,128)(2,1)S(1)}, bf16[144,288]{1,0:T(8,128)(2,1)}, u32[]{:S(2)}) copy-start(bf16[144,288]{1,0:T(8,128)(2,1)} %constant.26.clone.ml_hbm) | copy-start | bytes 248836
  25.9 8.2 %copy-start.5 = (bf16[144,288]{1,0:T(8,128)(2,1)S(1)}, bf16[144,288]{1,0:T(8,128)(2,1)}, u32[]{:S(2)}) copy-start(bf16[144,288]{1,0:T(8,128)(2,1)} %constant.25.clone.mh_hbm) | copy-start | bytes 248836
  25.9 8.2 %copy-start.7 = (bf16[72,144]{1,0:T(8,128)(2,1)S(1)}, bf16[72,144]{1,0:T(8,128)(2,1)}, u32[]{:S(2)}) copy-start(bf16[72,144]{1,0:T(8,128)(2,1)} %constant.22.clone.sl_hbm) | copy-start | bytes 62212
  25.9 8.2 %copy-start.8 = (bf16[72,144]{1,0:T(8,128)(2,1)S(1)}, bf16[72,144]{1,0:T(8,128)(2,1)}, u32[]{:S(2)}) copy-start(bf16[72,144]{1,0:T(8,128)(2,1)} %constant.21.clone.sh_hbm) | copy-start | bytes 62212
  25.9 8.2 %copy-start.9 = (bf16[72,144]{1,0:T(8,128)(2,1)S(1)}, bf16[72,144]{1,0:T(8,128)(2,1)}, u32[]{:S(2)}) copy-start(bf16[72,144]{1,0:T(8,128)(2,1)} %constant.20.clone.cl_hbm) | copy-start | bytes 62212
  25.9 8.2 %copy-start.10 = (bf16[72,144]{1,0:T(8,128)(2,1)S(1)}, bf16[72,144]{1,0:T(8,128)(2,1)}, u32[]{:S(2)}) copy-start(bf16[72,144]{1,0:T(8,128)(2,1)} %constant.19.clone.ch_hbm) | copy-start | bytes 62212

commit v5 on v4

--- a/solution.py
+++ b/solution.py
@@ -107,18 +107,10 @@
 TARGETS = [(dx, dy, dc) for dx, dy in CHIPS for dc in (1, 0) if (dx, dy, dc) != (0, 0, 0)]
 
 
-def load_tables(pairs, sems):
-    loads = [pltpu.make_async_copy(src, dst, sems.at[i]) for i, (src, dst) in enumerate(pairs)]
-    for one in loads:
-        one.start()
-    return loads
-
-
 def lines_kernel(
-    coef_hbm, cols_hbm, occ_ref, w_hbm, out_ref,
-    coef, cols, w, lanes, given, got, load, give_s, got_r,
+    coef, cols, occ_ref, w, out_ref,
+    lanes, given, got, give_s, got_r,
 ):
-    loads = load_tables(((cols_hbm, cols), (coef_hbm, coef), (w_hbm, w)), load)
     band, me = lax.axis_index("band"), lax.axis_index("fft")
     yh, zc, c = band // 16, (band // 2) % 8, band % 2
     x, y = me // 2, 2 * yh + me % 2
@@ -132,8 +124,7 @@
     for target in targets:
         pl.semaphore_signal(barrier, inc=1, device_id=device(*target), device_id_type=MESH)
 
-    loads[0].wait()
-    window = cols[:, pl.ds(pl.multiple_of(640 * me, 128), 704)]
+    window = cols[pl.ds(pl.multiple_of(640 * me, 128), 704)].reshape(1, 704)
     window = jnp.concatenate([window, window[:, 0:64]], axis=1)
     box = pltpu.roll(window, lax.rem(768 - 8 * me, 768), 1)[:, 0:LC].astype(F32)
     k0 = jnp.floor((box + 0.5) * (1.0 / KZ))
@@ -143,8 +134,6 @@
     inside = k * k + (k0 * k0 + k1 * k1) <= float(R * R)
     scale = jnp.sqrt(jnp.full((1, LC), occ_ref[0].astype(F32) * (1.0 / 32.0)))
     scale = jnp.where(inside, scale, 0.0)
-    for one in loads[1:]:
-        one.wait()
     xt = jnp.concatenate([coef[0, 0] * scale, coef[0, 1] * scale], axis=0).T
     hi, lo = split(xt)
     wh, wl = w[0 : 2 * KZ], w[2 * KZ : 4 * KZ]
@@ -215,22 +204,19 @@
 
 def lines(coefficients, cols, occ):
     w = line_table()
-    hbm = pl.BlockSpec(memory_space=pltpu.HBM)
+    vmem = pl.BlockSpec(memory_space=pltpu.VMEM)
     dma = pltpu.SemaphoreType.DMA
     n = len(TARGETS)
     return pl.pallas_call(
         lines_kernel,
         out_shape=jax.ShapeDtypeStruct((NCOLS, 128), F32),
-        in_specs=[hbm, hbm, pl.BlockSpec(memory_space=pltpu.SMEM), hbm],
-        out_specs=pl.BlockSpec(memory_space=pltpu.VMEM),
+        in_specs=[vmem, vmem, pl.BlockSpec(memory_space=pltpu.SMEM), vmem],
+        out_specs=vmem,
         scratch_shapes=[
-            pltpu.VMEM((1, 2, KZ, LC), F32),
-            pltpu.VMEM((1, NCOLS), jnp.int32),
-            pltpu.VMEM((4 * KZ, 384), BF16),
             pltpu.VMEM((3, LC, 128), F32),
             pltpu.VMEM((n, 56, 128), F32),
             pltpu.VMEM((32, 56, 128), F32),
-            dma((3,)), dma((n,)), dma((n,)),
+            dma((n,)), dma((n,)),
         ],
         compiler_params=pltpu.CompilerParams(
             collective_id=1, has_side_effects=True, vmem_limit_bytes=LINES_VMEM
@@ -240,12 +226,12 @@
 
 def grid_kernel(rows_ref, cols_ref, out_ref, grid_ref):
     def scatter(i, carry):
-        for u in range(16):
-            n = i * 16 + u
+        for u in range(144):
+            n = i * 144 + u
             grid_ref[pl.ds(cols_ref[n], 1), :] = rows_ref[pl.ds(n, 1), :]
         return carry
 
-    lax.fori_loop(0, NCOLS // 16, scatter, 0)
+    lax.fori_loop(0, NCOLS // 144, scatter, 0)
 
     def turn(i, carry):
         for u in range(8):
@@ -270,18 +256,10 @@
 
 
 def density_kernel(
-    g_ref, ch_hbm, cl_hbm, sh_hbm, sl_hbm, t2_hbm, m3_hbm, mh_hbm, ml_hbm, out_ref,
-    ch_ref, cl_ref, sh_ref, sl_ref, t2_ref, m3_ref, mh_ref, ml_ref,
+    g_ref, ch_ref, cl_ref, sh_ref, sl_ref, t2_ref, m3_ref, mh_ref, ml_ref, out_ref,
     hall_ref, part, held, sent, acc, left, fine, packed, given, got, turned,
-    load, ring_s, ring_r, got_s, got_r,
+    ring_s, ring_r, got_s, got_r,
 ):
-    loads = load_tables(
-        (
-            (ch_hbm, ch_ref), (cl_hbm, cl_ref), (sh_hbm, sh_ref), (sl_hbm, sl_ref),
-            (t2_hbm, t2_ref), (m3_hbm, m3_ref), (mh_hbm, mh_ref), (ml_hbm, ml_ref),
-        ),
-        load,
-    )
     band, me = lax.axis_index("band"), lax.axis_index("fft")
     yh, zc, c = band // 16, (band // 2) % 8, band % 2
     x, y = me // 2, 2 * yh + me % 2
@@ -290,7 +268,7 @@
     def device(xx, yy, cc):
         return {"band": (yy // 2) * 16 + zc * 2 + cc, "fft": 2 * xx + yy % 2}
 
-    ring_to = [{"band": yh * 16 + ((zc + d) % 8) * 2 + c, "fft": me} for d in (7, 1)]
+    ring_to = [{"band": yh * 16 + ((zc + d) % 8) * 2 + c, "fft": me} for d in (6, 7, 1, 2)]
     targets = [((x + dx) % 4, (y + dy) % 4, (c + dc) % 2) for dx, dy, dc in TARGETS]
     barrier = pltpu.get_barrier_semaphore()
     for where in [*ring_to, *(device(*target) for target in targets)]:
@@ -306,8 +284,6 @@
         started.append(made)
         return made
 
-    for one in loads:
-        one.wait()
     ch, cl, sh, sl = ch_ref[...], cl_ref[...], sh_ref[...], sl_ref[...]
     rows = 5 * KZ
     for h in range(4):
@@ -347,47 +323,53 @@
     alone = (pl.ds(0, 4), pl.ds(4, 5))
     ring = {}
 
-    def hop(step, t):
+    def owner(way, away):
+        return (zc + (8 - away if way == 0 else away)) % 8
+
+    def send(way, kind, t, src, units, hops):
+        to = {"band": yh * 16 + owner(way, hops) * 2 + c, "fft": me}
+        ring[way, kind, t] = copy(
+            src, held.at[way, kind, t, units], ring_s.at[way, kind, t], ring_r.at[way, kind, t], to
+        )
+
+    def early(t):
         for way in range(2):
-            away = 4 - step
-            owner = (zc + (8 - away if way == 0 else away)) % 8
-            units = alone[way] if step == 0 else pl.ds(0, 9)
-            if step == 0:
-                src = part.at[owner, t, units]
-            else:
-                ring[way, step - 1, t].wait_recv()
-                src = sent.at[way, step, t]
-                if step == 1:
-                    rest = alone[1 - way]
-                    sent[way, step, t, rest] = part[owner, t, rest]
-                    sent[way, step, t, alone[way]] = part[owner, t, alone[way]] + held[way, 0, t, alone[way]]
-                else:
-                    sent[way, step, t] = part[owner, t] + held[way, step - 1, t]
-            ring[way, step, t] = copy(
-                src, held.at[way, step, t, units], ring_s.at[way, step, t], ring_r.at[way, step, t], ring_to[way]
-            )
+            send(way, 0, t, part.at[owner(way, 4), t, alone[way]], alone[way], 2)
+        for way in range(2):
+            send(way, 1, t, part.at[owner(way, 3), t], pl.ds(0, 9), 1)
+
+    def near(t):
+        for way in range(2):
+            send(way, 2, t, part.at[owner(way, 1), t], pl.ds(0, 9), 1)
+
+    def joined(t):
+        for way in range(2):
+            ring[way, 0, t].wait_recv()
+            ring[way, 1, t].wait_recv()
+            mine, rest = alone[way], alone[1 - way]
+            sent[way, t, rest] = part[owner(way, 2), t, rest] + held[way, 1, t, rest]
+            sent[way, t, mine] = part[owner(way, 2), t, mine] + held[way, 1, t, mine] + held[way, 0, t, mine]
+            send(way, 3, t, sent.at[way, t], pl.ds(0, 9), 2)
 
     def final(t):
         for way in range(2):
+            ring[way, 2, t].wait_recv()
             ring[way, 3, t].wait_recv()
-        acc[t] = part[zc, t] + held[0, 3, t] + held[1, 3, t]
+        acc[t] = part[zc, t] + held[0, 2, t] + held[1, 2, t] + held[0, 3, t] + held[1, 3, t]
 
     chunk(0)
-    pl.semaphore_wait(barrier, len(targets) + 2)
-    hop(0, 0)
+    pl.semaphore_wait(barrier, len(targets) + 4)
+    early(0)
     chunk(1)
-    hop(0, 1)
-    hop(1, 0)
+    early(1)
     chunk(2)
-    hop(0, 2)
-    hop(1, 1)
-    hop(2, 0)
-    hop(1, 2)
-    hop(2, 1)
-    hop(3, 0)
-    hop(2, 2)
-    hop(3, 1)
-    hop(3, 2)
+    early(2)
+    near(0)
+    joined(0)
+    near(1)
+    joined(1)
+    near(2)
+    joined(2)
     for t in range(3):
         final(t)
 
@@ -446,14 +428,13 @@
     return pl.pallas_call(
         density_kernel,
         out_shape=jax.ShapeDtypeStruct((9, 36, NF), F32),
-        in_specs=[vmem] + [pl.BlockSpec(memory_space=pltpu.HBM)] * 8,
+        in_specs=[vmem] * 9,
         out_specs=vmem,
         scratch_shapes=[
-            *(pltpu.VMEM(t.shape, BF16) for t in tables),
             pltpu.VMEM((NC, 4 * HALF), F32),
             pltpu.VMEM((8, 3, 9, 8, 128), F32),
             pltpu.VMEM((2, 4, 3, 9, 8, 128), F32),
-            pltpu.VMEM((2, 4, 3, 9, 8, 128), F32),
+            pltpu.VMEM((2, 3, 9, 8, 128), F32),
             pltpu.VMEM((3, 9, 8, 128), F32),
             pltpu.VMEM((184, NC), F32),
             pltpu.VMEM((3, 184, 128), F32),
@@ -461,7 +442,6 @@
             pltpu.VMEM((32, 16, 128), F32),
             pltpu.VMEM((32, 16, 128), F32),
             pltpu.VMEM((NC, 384), F32),
-            dma((8,)),
             dma((2, 4, 3)), dma((2, 4, 3)),
             dma((n,)), dma((n,)),
         ],
@@ -472,7 +452,7 @@
 
 
 def local(coefficients, col_index, occupation):
-    rows = lines(coefficients, col_index[None, :], occupation)
+    rows = lines(coefficients, col_index, occupation)
     return density(grid(rows, col_index))
 
 

time: 69.4 us -> 64.2 us (0.925)
  Pallas kernels: 64.7 us -> 59.6 us
    pallas_call x1, Pallas kernels: 34.2 us -> 31 us  [density(): pl.pallas_call(density_kernel, out_shape=jax.ShapeDtypeStruct((9, 36, NF)...]
    pallas_call x1, Pallas kernels: 8.1 us -> 6.88 us  [grid(): pl.pallas_call(grid_kernel, out_shape=jax.ShapeDtypeStruct((40 * KZ, 128)...]
    broadcast_in_dim x1 -> x0, local copies, waits for them, and re-layouts: 0.75 us -> none  [local(): rows = lines(coefficients, col_index[None, :], occupation)]
    unnamed x23 -> x25, local copies, waits for them, and re-layouts: 2.81 us -> 3.55 us
    pallas_call x1, Pallas kernels: 22.4 us -> 21.7 us  [lines(): pl.pallas_call(lines_kernel, out_shape=jax.ShapeDtypeStruct((NCOLS, 128),...]
where the time goes in v5:
time: 64.2 us; the launch traced here: 63.9 us
  Pallas kernels  59.6 us (93%)
  local copies, waits for them, and re-layouts  3.55 us (6%)
  between operations  0.81 us (1%)
    pallas_call x1, Pallas kernels, density(): pl.pallas_call(density_kernel, out_shape=jax.ShapeDtypeStruct((9, 36, NF)...  31 us
    pallas_call x1, Pallas kernels, lines(): pl.pallas_call(lines_kernel, out_shape=jax.ShapeDtypeStruct((NCOLS, 128),...  21.7 us
    pallas_call x1, Pallas kernels, grid(): pl.pallas_call(grid_kernel, out_shape=jax.ShapeDtypeStruct((40 * KZ, 128)...  6.88 us
    unnamed x25, local copies, waits for them, and re-layouts  3.55 us

profile of v5, /device:TPU:1, one launch (start us, length us, event | category | flops | bytes accessed | tf_op | source)
XLA Modules:
  0.0 63.9 jit_solution(4687213417920851400)
XLA Ops:
  0.7 0.0 copy-start
  0.7 1.0 %copy-done = f32[1,2,72,648]{3,2,1,0:T(8,128)S(1)} copy-done((f32[1,2,72,648]{3,2,1,0:T(8,128)S(1)}, f32[1,2,72,648]{3,2,1,0:T(8,128)}, u32[]{:S(2)}) %copy-start) | copy-done | bytes 373272
  1.7 0.0 copy-start.3
  1.7 0.9 %copy-done.3 = bf16[288,384]{1,0:T(8,128)(2,1)S(1)} copy-done((bf16[288,384]{1,0:T(8,128)(2,1)S(1)}, bf16[288,384]{1,0:T(8,128)(2,1)}, u32[]{:S(2)}) %copy-start.3) | copy-done | bytes 221208
  2.6 0.0 copy-start.6
  2.6 0.7 %copy-done.6 = s32[5184]{0:T(1024)S(1)} copy-done((s32[5184]{0:T(1024)S(1)}, s32[5184]{0:T(1024)}, u32[]{:S(2)}) %copy-start.6) | copy-done | bytes 20760
  3.3 0.0 copy-start.7
  3.3 21.7 %shard_map.118.rows_ref = f32[5184,128]{1,0:T(8,128)S(1)} custom-call(f32[1,2,72,648]{3,2,1,0:T(8,128)S(1)} %copy-done, s32[5184]{0:T(1024)S(1)} %copy-done.6, s32[1]{0:T(128)S(6)} %copy.14.occ_ref, bf16[288,384]{1,0:T(8,128)(2,1)S(1)} %copy-done.3), custom_call_target="tpu_custom_call" | custom-call | tf_op jit(solution)/shard_map/pallas_call | solution.py:210
  25.1 0.0 copy-done.7
  25.1 0.0 copy-start.1
  25.1 0.0 copy-start.2
  25.1 0.0 copy-start.4
  25.1 0.0 copy-start.5
  25.1 0.0 copy-start.8
  25.1 0.0 copy-start.9
  25.2 0.0 copy-start.10
  25.2 0.0 copy-start.11
  25.2 6.9 %shard_map.119.g_ref = f32[2880,128]{1,0:T(8,128)S(1)} custom-call(f32[5184,128]{1,0:T(8,128)S(1)} %shard_map.118.rows_ref, s32[5184]{0:T(1024)S(1)} %copy-done.7), custom_call_target="tpu_custom_call" | custom-call | tf_op jit(solution)/shard_map/pallas_call | solution.py:248
  32.1 0.0 copy-done.1
  32.1 0.0 copy-done.2
  32.1 0.0 copy-done.4
  32.1 0.0 copy-done.5
  32.1 0.0 copy-done.8
  32.1 0.0 copy-done.9
  32.1 0.0 copy-done.10
  32.1 0.0 copy-done.11
  32.1 31.0 %shard_map.120 = f32[9,36,288]{2,1,0:T(8,128)S(1)} custom-call(f32[2880,128]{1,0:T(8,128)S(1)} %shard_map.119.g_ref, bf16[72,144]{1,0:T(8,128)(2,1)S(1)} %copy-done.11, bf16[72,144]{1,0:T(8,128)(2,1)S(1)} %copy-done.10, bf16[72,144]{1,0:T(8,128)(2,1)S(1)} %copy-done.9, bf16[72,144]{1,0:T(8,128)(2,1)S(1)} %copy-done.8, bf16[288,432]{1,0:T(8,128)(2,1)S(1)} %copy-done.2, ...), custom_call_target="tpu_custom_call" | custom-call | tf_op jit(solution)/shard_map/pallas_call | solution.py:428
  63.1 0.8 %copy.15 = f32[9,36,288]{2,1,0:T(8,128)} copy(f32[9,36,288]{2,1,0:T(8,128)S(1)} %shard_map.120) | data formatting | bytes 746496
Async XLA Ops:
  0.7 1.0 %copy-start = (f32[1,2,72,648]{3,2,1,0:T(8,128)S(1)}, f32[1,2,72,648]{3,2,1,0:T(8,128)}, u32[]{:S(2)}) copy-start(f32[1,2,72,648]{3,2,1,0:T(8,128)} %coef.1) | copy-start | bytes 1119748
  1.7 0.9 %copy-start.3 = (bf16[288,384]{1,0:T(8,128)(2,1)S(1)}, bf16[288,384]{1,0:T(8,128)(2,1)}, u32[]{:S(2)}) copy-start(bf16[288,384]{1,0:T(8,128)(2,1)} %constant.18.clone.w) | copy-start | bytes 663556
  2.6 0.7 %copy-start.6 = (s32[5184]{0:T(1024)S(1)}, s32[5184]{0:T(1024)}, u32[]{:S(2)}) copy-start(s32[5184]{0:T(1024)} %cols_ref.1) | copy-start | bytes 62212
  3.3 21.7 %copy-start.7 = (s32[5184]{0:T(1024)S(1)}, s32[5184]{0:T(1024)}, u32[]{:S(2)}) copy-start(s32[5184]{0:T(1024)} %cols_ref.1) | copy-start | bytes 62212
  25.1 7.0 %copy-start.1 = (bf16[320,432]{1,0:T(8,128)(2,1)S(1)}, bf16[320,432]{1,0:T(8,128)(2,1)}, u32[]{:S(2)}) copy-start(bf16[320,432]{1,0:T(8,128)(2,1)} %constant.24.clone.m3_ref) | copy-start | bytes 829444
  25.1 7.0 %copy-start.2 = (bf16[288,432]{1,0:T(8,128)(2,1)S(1)}, bf16[288,432]{1,0:T(8,128)(2,1)}, u32[]{:S(2)}) copy-start(bf16[288,432]{1,0:T(8,128)(2,1)} %constant.23.clone.t2_ref) | copy-start | bytes 746500
  25.1 7.0 %copy-start.4 = (bf16[144,288]{1,0:T(8,128)(2,1)S(1)}, bf16[144,288]{1,0:T(8,128)(2,1)}, u32[]{:S(2)}) copy-start(bf16[144,288]{1,0:T(8,128)(2,1)} %constant.26.clone.ml_ref) | copy-start | bytes 248836
  25.1 7.0 %copy-start.5 = (bf16[144,288]{1,0:T(8,128)(2,1)S(1)}, bf16[144,288]{1,0:T(8,128)(2,1)}, u32[]{:S(2)}) copy-start(bf16[144,288]{1,0:T(8,128)(2,1)} %constant.25.clone.mh_ref) | copy-start | bytes 248836
  25.1 7.0 %copy-start.8 = (bf16[72,144]{1,0:T(8,128)(2,1)S(1)}, bf16[72,144]{1,0:T(8,128)(2,1)}, u32[]{:S(2)}) copy-start(bf16[72,144]{1,0:T(8,128)(2,1)} %constant.22.clone.sl_ref) | copy-start | bytes 62212
  25.1 7.0 %copy-start.9 = (bf16[72,144]{1,0:T(8,128)(2,1)S(1)}, bf16[72,144]{1,0:T(8,128)(2,1)}, u32[]{:S(2)}) copy-start(bf16[72,144]{1,0:T(8,128)(2,1)} %constant.21.clone.sh_ref) | copy-start | bytes 62212
  25.2 7.0 %copy-start.10 = (bf16[72,144]{1,0:T(8,128)(2,1)S(1)}, bf16[72,144]{1,0:T(8,128)(2,1)}, u32[]{:S(2)}) copy-start(bf16[72,144]{1,0:T(8,128)(2,1)} %constant.20.clone.cl_ref) | copy-start | bytes 62212
  25.2 7.0 %copy-start.11 = (bf16[72,144]{1,0:T(8,128)(2,1)S(1)}, bf16[72,144]{1,0:T(8,128)(2,1)}, u32[]{:S(2)}) copy-start(bf16[72,144]{1,0:T(8,128)(2,1)} %constant.19.clone.ch_ref) | copy-start | bytes 62212

commit v6 on v5

--- a/solution.py
+++ b/solution.py
@@ -100,11 +100,14 @@
     return jnp.dot(a, b, preferred_element_type=F32)
 
 
-CHIPS = sorted(
-    ((dx, dy) for dx in range(4) for dy in range(4)),
-    key=lambda d: (-min(d[0], 4 - d[0]) - min(d[1], 4 - d[1]), d),
-)
-TARGETS = [(dx, dy, dc) for dx, dy in CHIPS for dc in (1, 0) if (dx, dy, dc) != (0, 0, 0)]
+GROUPS = ((0, 0), (1, 0), (3, 0), (0, 1), (1, 1), (3, 1), (2, 0), (2, 1))
+TARGETS = [
+    (dx, dy, dc)
+    for dx, odd in GROUPS
+    for dy in (odd + 2, odd)
+    for dc in (1, 0)
+    if (dx, dy, dc) != (0, 0, 0)
+]
 
 
 def lines_kernel(
@@ -192,9 +195,9 @@
                 result = jnp.where(here >= 10 * straight, second, result)
             out_ref[pl.ds(base + 56 * q, n), :] = result
 
-    for dx, odd in ((0, 1), (0, 0), (1, 1), (3, 1), (1, 0), (3, 0), (2, 1), (2, 0)):
-        for dy in (odd, odd + 2):
-            for dc in (0, 1):
+    for dx, odd in GROUPS:
+        for dy in (odd + 2, odd):
+            for dc in (1, 0):
                 if (dx, dy, dc) in moves:
                     moves[dx, dy, dc].wait_recv()
         unpack(((x + 4 - dx) % 4) * 2 + (y + odd) % 2)
@@ -225,13 +228,8 @@
 
 
 def grid_kernel(rows_ref, cols_ref, out_ref, grid_ref):
-    def scatter(i, carry):
-        for u in range(144):
-            n = i * 144 + u
-            grid_ref[pl.ds(cols_ref[n], 1), :] = rows_ref[pl.ds(n, 1), :]
-        return carry
-
-    lax.fori_loop(0, NCOLS // 144, scatter, 0)
+    for n in range(NCOLS):
+        grid_ref[pl.ds(cols_ref[n], 1), :] = rows_ref[pl.ds(n, 1), :]
 
     def turn(i, carry):
         for u in range(8):
@@ -285,30 +283,34 @@
         return made
 
     ch, cl, sh, sl = ch_ref[...], cl_ref[...], sh_ref[...], sl_ref[...]
-    rows = 5 * KZ
     for h in range(4):
         hall_ref[:, HALF * h + 5 * NC : HALF * (h + 1)] = jnp.zeros((NC, HALF - 5 * NC), F32)
-        base = 10 * h * KZ
-        re_h, re_l = split(g_ref[base : base + rows, 0:KZ])
-        im_h, im_l = split(g_ref[base + rows : base + 2 * rows, 0:KZ])
-        half_re = (dot(re_h, ch) + dot(re_l, ch) + dot(re_h, cl)) - (
-            dot(im_h, sh) + dot(im_l, sh) + dot(im_h, sl)
-        )
-        half_im = (dot(re_h, sh) + dot(re_l, sh) + dot(re_h, sl)) + (
-            dot(im_h, ch) + dot(im_l, ch) + dot(im_h, cl)
-        )
-        for u in range(5):
-            at = HALF * h + NC * u
-            hall_ref[0:KZ, at : at + NC] = half_re[KZ * u : KZ * (u + 1)]
-            hall_ref[KZ : 2 * KZ, at : at + NC] = half_im[KZ * u : KZ * (u + 1)]
+
+    def first_transform(start, count):
+        rows = count * KZ
+        for h in range(4):
+            base = (10 * h + start) * KZ
+            re_h, re_l = split(g_ref[base : base + rows, 0:KZ])
+            base += 5 * KZ
+            im_h, im_l = split(g_ref[base : base + rows, 0:KZ])
+            half_re = (dot(re_h, ch) + dot(re_l, ch) + dot(re_h, cl)) - (
+                dot(im_h, sh) + dot(im_l, sh) + dot(im_h, sl)
+            )
+            half_im = (dot(re_h, sh) + dot(re_l, sh) + dot(re_h, sl)) + (
+                dot(im_h, ch) + dot(im_l, ch) + dot(im_h, cl)
+            )
+            for u in range(count):
+                at = HALF * h + NC * (start + u)
+                hall_ref[0:KZ, at : at + NC] = half_re[KZ * u : KZ * (u + 1)]
+                hall_ref[KZ : 2 * KZ, at : at + NC] = half_im[KZ * u : KZ * (u + 1)]
 
     row = lax.broadcasted_iota(jnp.int32, (8, 128), 0)
 
     def chunk(t):
+        first_transform(2 * t, min(2, 5 - 2 * t))
         total = 0.0
         for h in range(4):
-            field = [hall_ref[:, HALF * h + 128 * i : HALF * h + 128 * (i + 1)] for i in (t, t + 3)]
-            hh, hl = split(jnp.concatenate(field, axis=1))
+            hh, hl = split(hall_ref[:, HALF * h + 256 * t : HALF * h + 256 * (t + 1)])
             psi = dot(t2_ref[...], jnp.concatenate([hh, hl, hh], axis=0))
             re, im = psi[0:NC], psi[NC : 2 * NC]
             total = total + (re * re + im * im)
@@ -374,9 +376,9 @@
         final(t)
 
     for o in range(4):
-        main = jnp.concatenate([acc[t, 2 * o] for t in range(3)] + [acc[t, 2 * o + 1] for t in range(3)], axis=1)
+        main = jnp.concatenate([acc[t, 2 * o + i] for t in range(3) for i in range(2)], axis=1)
         ninth = jnp.concatenate(
-            [acc[t, 8, o : o + 1, :] for t in range(3)] + [acc[t, 8, 4 + o : 5 + o, :] for t in range(3)], axis=1
+            [acc[t, 8, 4 * i + o : 4 * i + o + 1, :] for t in range(3) for i in range(2)], axis=1
         )
         for u in range(5):
             n = 5 * o + u

time: 64.2 us -> 62.6 us (0.975)
  Pallas kernels: 59.6 us -> 58 us
    pallas_call x1, Pallas kernels: 21.7 us -> 20.1 us  [lines(): pl.pallas_call(lines_kernel, out_shape=jax.ShapeDtypeStruct((NCOLS, 128),...]
    pallas_call x1, Pallas kernels: 31 us -> 32.6 us  [density(): pl.pallas_call(density_kernel, out_shape=jax.ShapeDtypeStruct((9, 36, NF)...]
    pallas_call x1, Pallas kernels: 6.88 us -> 5.39 us  [grid(): pl.pallas_call(grid_kernel, out_shape=jax.ShapeDtypeStruct((40 * KZ, 128)...]
where the time goes in v6:
time: 62.6 us; the launch traced here: 62.4 us
  Pallas kernels  58 us (93%)
  local copies, waits for them, and re-layouts  3.55 us (6%)
  between operations  0.81 us (1%)
    pallas_call x1, Pallas kernels, density(): pl.pallas_call(density_kernel, out_shape=jax.ShapeDtypeStruct((9, 36, NF)...  32.6 us
    pallas_call x1, Pallas kernels, lines(): pl.pallas_call(lines_kernel, out_shape=jax.ShapeDtypeStruct((NCOLS, 128),...  20.1 us
    pallas_call x1, Pallas kernels, grid(): pl.pallas_call(grid_kernel, out_shape=jax.ShapeDtypeStruct((40 * KZ, 128)...  5.39 us
    unnamed x25, local copies, waits for them, and re-layouts  3.55 us

profile of v6, /device:TPU:1, one launch (start us, length us, event | category | flops | bytes accessed | tf_op | source)
XLA Modules:
  0.0 62.4 jit_solution(10590760988021012238)
XLA Ops:
  0.7 0.0 copy-start
  0.7 1.0 %copy-done = f32[1,2,72,648]{3,2,1,0:T(8,128)S(1)} copy-done((f32[1,2,72,648]{3,2,1,0:T(8,128)S(1)}, f32[1,2,72,648]{3,2,1,0:T(8,128)}, u32[]{:S(2)}) %copy-start) | copy-done | bytes 373272
  1.7 0.0 copy-start.3
  1.7 0.9 %copy-done.3 = bf16[288,384]{1,0:T(8,128)(2,1)S(1)} copy-done((bf16[288,384]{1,0:T(8,128)(2,1)S(1)}, bf16[288,384]{1,0:T(8,128)(2,1)}, u32[]{:S(2)}) %copy-start.3) | copy-done | bytes 221208
  2.6 0.0 copy-start.6
  2.6 0.7 %copy-done.6 = s32[5184]{0:T(1024)S(1)} copy-done((s32[5184]{0:T(1024)S(1)}, s32[5184]{0:T(1024)}, u32[]{:S(2)}) %copy-start.6) | copy-done | bytes 20760
  3.3 0.0 copy-start.7
  3.3 20.1 %shard_map.118.rows_ref = f32[5184,128]{1,0:T(8,128)S(1)} custom-call(f32[1,2,72,648]{3,2,1,0:T(8,128)S(1)} %copy-done, s32[5184]{0:T(1024)S(1)} %copy-done.6, s32[1]{0:T(128)S(6)} %copy.14.occ_ref, bf16[288,384]{1,0:T(8,128)(2,1)S(1)} %copy-done.3), custom_call_target="tpu_custom_call" | custom-call | tf_op jit(solution)/shard_map/pallas_call | solution.py:213
  23.4 0.0 copy-done.7
  23.4 0.0 copy-start.1
  23.4 0.0 copy-start.2
  23.4 0.0 copy-start.4
  23.5 0.0 copy-start.5
  23.5 0.0 copy-start.8
  23.5 0.0 copy-start.9
  23.5 0.0 copy-start.10
  23.5 0.0 copy-start.11
  23.5 5.4 %shard_map.119.g_ref = f32[2880,128]{1,0:T(8,128)S(1)} custom-call(f32[5184,128]{1,0:T(8,128)S(1)} %shard_map.118.rows_ref, s32[5184]{0:T(1024)S(1)} %copy-done.7), custom_call_target="tpu_custom_call" | custom-call | tf_op jit(solution)/shard_map/pallas_call | solution.py:246
  28.9 0.0 copy-done.1
  28.9 0.0 copy-done.2
  28.9 0.0 copy-done.4
  28.9 0.0 copy-done.5
  29.0 0.0 copy-done.8
  29.0 0.0 copy-done.9
  29.0 0.0 copy-done.10
  29.0 0.0 copy-done.11
  29.0 32.6 %shard_map.120 = f32[9,36,288]{2,1,0:T(8,128)S(1)} custom-call(f32[2880,128]{1,0:T(8,128)S(1)} %shard_map.119.g_ref, bf16[72,144]{1,0:T(8,128)(2,1)S(1)} %copy-done.11, bf16[72,144]{1,0:T(8,128)(2,1)S(1)} %copy-done.10, bf16[72,144]{1,0:T(8,128)(2,1)S(1)} %copy-done.9, bf16[72,144]{1,0:T(8,128)(2,1)S(1)} %copy-done.8, bf16[288,432]{1,0:T(8,128)(2,1)S(1)} %copy-done.2, ...), custom_call_target="tpu_custom_call" | custom-call | tf_op jit(solution)/shard_map/pallas_call | solution.py:430
  61.6 0.8 %copy.15 = f32[9,36,288]{2,1,0:T(8,128)} copy(f32[9,36,288]{2,1,0:T(8,128)S(1)} %shard_map.120) | data formatting | bytes 746496
Async XLA Ops:
  0.7 1.0 %copy-start = (f32[1,2,72,648]{3,2,1,0:T(8,128)S(1)}, f32[1,2,72,648]{3,2,1,0:T(8,128)}, u32[]{:S(2)}) copy-start(f32[1,2,72,648]{3,2,1,0:T(8,128)} %coef.1) | copy-start | bytes 1119748
  1.7 0.9 %copy-start.3 = (bf16[288,384]{1,0:T(8,128)(2,1)S(1)}, bf16[288,384]{1,0:T(8,128)(2,1)}, u32[]{:S(2)}) copy-start(bf16[288,384]{1,0:T(8,128)(2,1)} %constant.18.clone.w) | copy-start | bytes 663556
  2.6 0.7 %copy-start.6 = (s32[5184]{0:T(1024)S(1)}, s32[5184]{0:T(1024)}, u32[]{:S(2)}) copy-start(s32[5184]{0:T(1024)} %cols_ref.1) | copy-start | bytes 62212
  3.3 20.1 %copy-start.7 = (s32[5184]{0:T(1024)S(1)}, s32[5184]{0:T(1024)}, u32[]{:S(2)}) copy-start(s32[5184]{0:T(1024)} %cols_ref.1) | copy-start | bytes 62212
  23.4 5.5 %copy-start.1 = (bf16[320,432]{1,0:T(8,128)(2,1)S(1)}, bf16[320,432]{1,0:T(8,128)(2,1)}, u32[]{:S(2)}) copy-start(bf16[320,432]{1,0:T(8,128)(2,1)} %constant.24.clone.m3_ref) | copy-start | bytes 829444
  23.4 5.5 %copy-start.2 = (bf16[288,432]{1,0:T(8,128)(2,1)S(1)}, bf16[288,432]{1,0:T(8,128)(2,1)}, u32[]{:S(2)}) copy-start(bf16[288,432]{1,0:T(8,128)(2,1)} %constant.23.clone.t2_ref) | copy-start | bytes 746500
  23.4 5.5 %copy-start.4 = (bf16[144,288]{1,0:T(8,128)(2,1)S(1)}, bf16[144,288]{1,0:T(8,128)(2,1)}, u32[]{:S(2)}) copy-start(bf16[144,288]{1,0:T(8,128)(2,1)} %constant.26.clone.ml_ref) | copy-start | bytes 248836
  23.5 5.5 %copy-start.5 = (bf16[144,288]{1,0:T(8,128)(2,1)S(1)}, bf16[144,288]{1,0:T(8,128)(2,1)}, u32[]{:S(2)}) copy-start(bf16[144,288]{1,0:T(8,128)(2,1)} %constant.25.clone.mh_ref) | copy-start | bytes 248836
  23.5 5.5 %copy-start.8 = (bf16[72,144]{1,0:T(8,128)(2,1)S(1)}, bf16[72,144]{1,0:T(8,128)(2,1)}, u32[]{:S(2)}) copy-start(bf16[72,144]{1,0:T(8,128)(2,1)} %constant.22.clone.sl_ref) | copy-start | bytes 62212
  23.5 5.5 %copy-start.9 = (bf16[72,144]{1,0:T(8,128)(2,1)S(1)}, bf16[72,144]{1,0:T(8,128)(2,1)}, u32[]{:S(2)}) copy-start(bf16[72,144]{1,0:T(8,128)(2,1)} %constant.21.clone.sh_ref) | copy-start | bytes 62212
  23.5 5.5 %copy-start.10 = (bf16[72,144]{1,0:T(8,128)(2,1)S(1)}, bf16[72,144]{1,0:T(8,128)(2,1)}, u32[]{:S(2)}) copy-start(bf16[72,144]{1,0:T(8,128)(2,1)} %constant.20.clone.cl_ref) | copy-start | bytes 62212
  23.5 5.5 %copy-start.11 = (bf16[72,144]{1,0:T(8,128)(2,1)S(1)}, bf16[72,144]{1,0:T(8,128)(2,1)}, u32[]{:S(2)}) copy-start(bf16[72,144]{1,0:T(8,128)(2,1)} %constant.19.clone.ch_ref) | copy-start | bytes 62212

commit v7 on v6

--- a/solution.py
+++ b/solution.py
@@ -47,20 +47,6 @@
     return (1.0 + 2.0 * np.cos(ang).sum(axis=2)) / NC
 
 
-def line_table():
-    cos, sin = phases(NC)
-    w = np.zeros((2, KZ, 3, 128))
-    for d in range(32):
-        n, z = COUNT[d % 4], NP * (d // 4) + FIRST[d % 4]
-        c, s = cos[:, z : z + n], sin[:, z : z + n]
-        t, lane = d // 12, 10 * (d % 12)
-        w[0, :, t, lane : lane + n] = c
-        w[1, :, t, lane : lane + n] = -s
-        w[0, :, t, lane + 5 : lane + 5 + n] = s
-        w[1, :, t, lane + 5 : lane + 5 + n] = c
-    return np.concatenate(hi_lo(w.reshape(2 * KZ, 384)), axis=0)
-
-
 def stacked(table):
     hi, lo = hi_lo(table)
     return np.concatenate([hi, hi, lo], axis=1)
@@ -110,8 +96,41 @@
 ]
 
 
+def line_table():
+    at = lax.broadcasted_iota(jnp.int32, (1, 384), 1).astype(F32)
+    tile = jnp.floor((at + 0.5) * (1.0 / 128))
+    at = at - 128 * tile
+    place = jnp.floor((at + 0.5) * 0.1)
+    part = at - 10 * place
+    imag = part >= 5
+    plane = jnp.where(imag, part - 5, part)
+    owner = 12 * tile + place
+    fft = jnp.floor((owner + 0.5) * 0.25)
+    quarter = owner - 4 * fft
+    first, count = jnp.zeros_like(at), jnp.zeros_like(at)
+    for i in range(4):
+        first = jnp.where(quarter == i, float(FIRST[i]), first)
+        count = jnp.where(quarter == i, float(COUNT[i]), count)
+    used = (plane < count) & (place < 12) & (fft < 8)
+    z = NP * fft + first + plane
+    k = lax.broadcasted_iota(jnp.int32, (KZ, 384), 0).astype(F32) - R
+    turns = k * z
+    turns = turns - NC * jnp.floor((turns + 0.5) * (1.0 / NC))
+    quad = jnp.floor((turns + 18.0) * (1.0 / 36))
+    a = (turns - 36 * quad) * (2.0 * np.pi / NC)
+    b = a * a
+    sin = a * (1 + b * (-1 / 6 + b * (1 / 120 + b * (-1 / 5040 + b * (1 / 362880)))))
+    cos = 1 + b * (-1 / 2 + b * (1 / 24 + b * (-1 / 720 + b * (1 / 40320 - b * (1 / 3628800)))))
+    odd = (quad == 1) | (quad == 3)
+    c, s = jnp.where(odd, sin, cos), jnp.where(odd, cos, sin)
+    c = jnp.where((quad == 1) | (quad == 2), -c, c)
+    s = jnp.where((quad == 2) | (quad == 3), -s, s)
+    c, s = jnp.where(used, c, 0.0), jnp.where(used, s, 0.0)
+    return jnp.concatenate([jnp.where(imag, s, c), jnp.where(imag, c, -s)], axis=0)
+
+
 def lines_kernel(
-    coef, cols, occ_ref, w, out_ref,
+    coef, cols, occ_ref, out_ref,
     lanes, given, got, give_s, got_r,
 ):
     band, me = lax.axis_index("band"), lax.axis_index("fft")
@@ -139,7 +158,7 @@
     scale = jnp.where(inside, scale, 0.0)
     xt = jnp.concatenate([coef[0, 0] * scale, coef[0, 1] * scale], axis=0).T
     hi, lo = split(xt)
-    wh, wl = w[0 : 2 * KZ], w[2 * KZ : 4 * KZ]
+    wh, wl = split(line_table())
     value = dot(hi, wh) + dot(lo, wh) + dot(hi, wl)
     for t in range(3):
         lanes[t] = value[:, 128 * t : 128 * (t + 1)]
@@ -206,14 +225,13 @@
 
 
 def lines(coefficients, cols, occ):
-    w = line_table()
     vmem = pl.BlockSpec(memory_space=pltpu.VMEM)
     dma = pltpu.SemaphoreType.DMA
     n = len(TARGETS)
     return pl.pallas_call(
         lines_kernel,
         out_shape=jax.ShapeDtypeStruct((NCOLS, 128), F32),
-        in_specs=[vmem, vmem, pl.BlockSpec(memory_space=pltpu.SMEM), vmem],
+        in_specs=[vmem, vmem, pl.BlockSpec(memory_space=pltpu.SMEM)],
         out_specs=vmem,
         scratch_shapes=[
             pltpu.VMEM((3, LC, 128), F32),
@@ -224,7 +242,7 @@
         compiler_params=pltpu.CompilerParams(
             collective_id=1, has_side_effects=True, vmem_limit_bytes=LINES_VMEM
         ),
-    )(coefficients, cols, occ, jnp.asarray(w))
+    )(coefficients, cols, occ)
 
 
 def grid_kernel(rows_ref, cols_ref, out_ref, grid_ref):
@@ -232,13 +250,13 @@
         grid_ref[pl.ds(cols_ref[n], 1), :] = rows_ref[pl.ds(n, 1), :]
 
     def turn(i, carry):
-        for u in range(8):
-            k0 = i * 8 + u
-            t = grid_ref[pl.ds(pl.multiple_of(k0 * KZ, 8), 128), :].T
-            out_ref[pl.ds(k0, 40, stride=KZ), :] = t[0:40]
+        for u in range(24):
+            k0 = i * 24 + u
+            t = grid_ref[pl.ds(pl.multiple_of(k0 * KZ, 8), KZ), :].T[0:40]
+            out_ref[pl.ds(k0, 40, stride=KZ), :] = jnp.concatenate([t, jnp.zeros((40, 128 - KZ), F32)], axis=1)
         return carry
 
-    lax.fori_loop(0, KZ // 8, turn, 0)
+    lax.fori_loop(0, KZ // 24, turn, 0)
 
 
 def grid(rows, cols):
@@ -251,6 +269,9 @@
         scratch_shapes=[pltpu.VMEM((NCOLS + 56, 128), F32)],
         compiler_params=pltpu.CompilerParams(vmem_limit_bytes=GRID_VMEM),
     )(rows, cols)
+
+
+RELAY = (0,)
 
 
 def density_kernel(
@@ -349,30 +370,52 @@
             ring[way, 0, t].wait_recv()
             ring[way, 1, t].wait_recv()
             mine, rest = alone[way], alone[1 - way]
-            sent[way, t, rest] = part[owner(way, 2), t, rest] + held[way, 1, t, rest]
-            sent[way, t, mine] = part[owner(way, 2), t, mine] + held[way, 1, t, mine] + held[way, 0, t, mine]
-            send(way, 3, t, sent.at[way, t], pl.ds(0, 9), 2)
+            sent[way, 3, t, rest] = part[owner(way, 2), t, rest] + held[way, 1, t, rest]
+            sent[way, 3, t, mine] = part[owner(way, 2), t, mine] + held[way, 1, t, mine] + held[way, 0, t, mine]
+            send(way, 3, t, sent.at[way, 3, t], pl.ds(0, 9), 2)
+
+    def hop(step, t):
+        for way in range(2):
+            src, units = part.at[owner(way, 4 - step), t], pl.ds(0, 9)
+            if step == 0:
+                src, units = part.at[owner(way, 4), t, alone[way]], alone[way]
+            else:
+                ring[way, step - 1, t].wait_recv()
+                mine, rest = alone[way], alone[1 - way]
+                here = owner(way, 4 - step)
+                if step == 1:
+                    sent[way, 1, t, rest] = part[here, t, rest]
+                    sent[way, 1, t, mine] = part[here, t, mine] + held[way, 0, t, mine]
+                else:
+                    sent[way, step, t] = part[here, t] + held[way, step - 1, t]
+                src = sent.at[way, step, t]
+            send(way, step, t, src, units, 1)
 
     def final(t):
         for way in range(2):
-            ring[way, 2, t].wait_recv()
+            if t not in RELAY:
+                ring[way, 2, t].wait_recv()
             ring[way, 3, t].wait_recv()
-        acc[t] = part[zc, t] + held[0, 2, t] + held[1, 2, t] + held[0, 3, t] + held[1, 3, t]
+        value = part[zc, t] + held[0, 3, t] + held[1, 3, t]
+        if t not in RELAY:
+            value = value + held[0, 2, t] + held[1, 2, t]
+        acc[t] = value
 
     chunk(0)
     pl.semaphore_wait(barrier, len(targets) + 4)
-    early(0)
+    hop(0, 0)
     chunk(1)
     early(1)
+    hop(1, 0)
     chunk(2)
     early(2)
-    near(0)
-    joined(0)
+    hop(2, 0)
     near(1)
     joined(1)
     near(2)
+    hop(3, 0)
     joined(2)
-    for t in range(3):
+    for t in (1, 0, 2):
         final(t)
 
     for o in range(4):
@@ -436,7 +479,7 @@
             pltpu.VMEM((NC, 4 * HALF), F32),
             pltpu.VMEM((8, 3, 9, 8, 128), F32),
             pltpu.VMEM((2, 4, 3, 9, 8, 128), F32),
-            pltpu.VMEM((2, 3, 9, 8, 128), F32),
+            pltpu.VMEM((2, 4, 3, 9, 8, 128), F32),
             pltpu.VMEM((3, 9, 8, 128), F32),
             pltpu.VMEM((184, NC), F32),
             pltpu.VMEM((3, 184, 128), F32),

time: 62.6 us -> 60.8 us (0.971)
  local copies, waits for them, and re-layouts: 3.55 us -> 2.6 us
  Pallas kernels: 58 us -> 57.2 us
    unnamed x25 -> x21, local copies, waits for them, and re-layouts: 3.55 us -> 2.6 us
    pallas_call x1, Pallas kernels: 5.39 us -> 4.65 us  [grid(): pl.pallas_call(grid_kernel, out_shape=jax.ShapeDtypeStruct((40 * KZ, 128)...]
where the time goes in v7:
time: 60.8 us; the launch traced here: 60.6 us
  Pallas kernels  57.2 us (94%)
  local copies, waits for them, and re-layouts  2.6 us (4%)
  between operations  0.81 us (1%)
    pallas_call x1, Pallas kernels, density(): pl.pallas_call(density_kernel, out_shape=jax.ShapeDtypeStruct((9, 36, NF)...  32.6 us
    pallas_call x1, Pallas kernels, lines(): pl.pallas_call(lines_kernel, out_shape=jax.ShapeDtypeStruct((NCOLS, 128),...  20 us
    pallas_call x1, Pallas kernels, grid(): pl.pallas_call(grid_kernel, out_shape=jax.ShapeDtypeStruct((40 * KZ, 128)...  4.65 us
    unnamed x21, local copies, waits for them, and re-layouts  2.6 us

profile of v7, /device:TPU:1, one launch (start us, length us, event | category | flops | bytes accessed | tf_op | source)
XLA Modules:
  0.0 60.6 jit_solution(11785699032829790950)
XLA Ops:
  0.7 0.0 copy-start
  0.7 1.0 %copy-done = f32[1,2,72,648]{3,2,1,0:T(8,128)S(1)} copy-done((f32[1,2,72,648]{3,2,1,0:T(8,128)S(1)}, f32[1,2,72,648]{3,2,1,0:T(8,128)}, u32[]{:S(2)}) %copy-start) | copy-done | bytes 373272
  1.7 0.0 copy-start.5
  1.7 0.7 %copy-done.5 = s32[5184]{0:T(1024)S(1)} copy-done((s32[5184]{0:T(1024)S(1)}, s32[5184]{0:T(1024)}, u32[]{:S(2)}) %copy-start.5) | copy-done | bytes 20760
  2.4 20.0 %shard_map.109.rows_ref = f32[5184,128]{1,0:T(8,128)S(1)} custom-call(f32[1,2,72,648]{3,2,1,0:T(8,128)S(1)} %copy-done, s32[5184]{0:T(1024)S(1)} %copy-done.5, s32[1]{0:T(128)S(6)} %copy.13.occ_ref), custom_call_target="tpu_custom_call" | custom-call | tf_op jit(solution)/shard_map/pallas_call | solution.py:231
  22.4 0.0 copy-start.1
  22.4 0.0 copy-start.2
  22.4 0.0 copy-start.3
  22.5 0.0 copy-start.4
  22.5 0.0 copy-start.6
  22.5 0.0 copy-start.7
  22.5 0.0 copy-start.8
  22.5 0.0 copy-start.9
  22.5 4.6 %shard_map.110.g_ref = f32[2880,128]{1,0:T(8,128)S(1)} custom-call(f32[5184,128]{1,0:T(8,128)S(1)} %shard_map.109.rows_ref, s32[5184]{0:T(1024)S(1)} %copy-done.5), custom_call_target="tpu_custom_call" | custom-call | tf_op jit(solution)/shard_map/pallas_call | solution.py:264
  27.2 0.0 copy-done.1
  27.2 0.0 copy-done.2
  27.2 0.0 copy-done.3
  27.2 0.0 copy-done.4
  27.2 0.0 copy-done.6
  27.2 0.0 copy-done.7
  27.2 0.0 copy-done.8
  27.2 0.0 copy-done.9
  27.3 32.6 %shard_map.111 = f32[9,36,288]{2,1,0:T(8,128)S(1)} custom-call(f32[2880,128]{1,0:T(8,128)S(1)} %shard_map.110.g_ref, bf16[72,144]{1,0:T(8,128)(2,1)S(1)} %copy-done.9, bf16[72,144]{1,0:T(8,128)(2,1)S(1)} %copy-done.8, bf16[72,144]{1,0:T(8,128)(2,1)S(1)} %copy-done.7, bf16[72,144]{1,0:T(8,128)(2,1)S(1)} %copy-done.6, bf16[288,432]{1,0:T(8,128)(2,1)S(1)} %copy-done.2, ...), custom_call_target="tpu_custom_call" | custom-call | tf_op jit(solution)/shard_map/pallas_call | solution.py:473
  59.8 0.8 %copy.14 = f32[9,36,288]{2,1,0:T(8,128)} copy(f32[9,36,288]{2,1,0:T(8,128)S(1)} %shard_map.111) | data formatting | bytes 746496
Async XLA Ops:
  0.7 1.0 %copy-start = (f32[1,2,72,648]{3,2,1,0:T(8,128)S(1)}, f32[1,2,72,648]{3,2,1,0:T(8,128)}, u32[]{:S(2)}) copy-start(f32[1,2,72,648]{3,2,1,0:T(8,128)} %coef.1) | copy-start | bytes 1119748
  1.7 0.7 %copy-start.5 = (s32[5184]{0:T(1024)S(1)}, s32[5184]{0:T(1024)}, u32[]{:S(2)}) copy-start(s32[5184]{0:T(1024)} %cols_ref.1) | copy-start | bytes 62212
  22.4 4.8 %copy-start.1 = (bf16[320,432]{1,0:T(8,128)(2,1)S(1)}, bf16[320,432]{1,0:T(8,128)(2,1)}, u32[]{:S(2)}) copy-start(bf16[320,432]{1,0:T(8,128)(2,1)} %constant.21.clone.m3_ref) | copy-start | bytes 829444
  22.4 4.8 %copy-start.2 = (bf16[288,432]{1,0:T(8,128)(2,1)S(1)}, bf16[288,432]{1,0:T(8,128)(2,1)}, u32[]{:S(2)}) copy-start(bf16[288,432]{1,0:T(8,128)(2,1)} %constant.20.clone.t2_ref) | copy-start | bytes 746500
  22.4 4.8 %copy-start.3 = (bf16[144,288]{1,0:T(8,128)(2,1)S(1)}, bf16[144,288]{1,0:T(8,128)(2,1)}, u32[]{:S(2)}) copy-start(bf16[144,288]{1,0:T(8,128)(2,1)} %constant.23.clone.ml_ref) | copy-start | bytes 248836
  22.5 4.8 %copy-start.4 = (bf16[144,288]{1,0:T(8,128)(2,1)S(1)}, bf16[144,288]{1,0:T(8,128)(2,1)}, u32[]{:S(2)}) copy-start(bf16[144,288]{1,0:T(8,128)(2,1)} %constant.22.clone.mh_ref) | copy-start | bytes 248836
  22.5 4.7 %copy-start.6 = (bf16[72,144]{1,0:T(8,128)(2,1)S(1)}, bf16[72,144]{1,0:T(8,128)(2,1)}, u32[]{:S(2)}) copy-start(bf16[72,144]{1,0:T(8,128)(2,1)} %constant.19.clone.sl_ref) | copy-start | bytes 62212
  22.5 4.7 %copy-start.7 = (bf16[72,144]{1,0:T(8,128)(2,1)S(1)}, bf16[72,144]{1,0:T(8,128)(2,1)}, u32[]{:S(2)}) copy-start(bf16[72,144]{1,0:T(8,128)(2,1)} %constant.18.clone.sh_ref) | copy-start | bytes 62212
  22.5 4.7 %copy-start.8 = (bf16[72,144]{1,0:T(8,128)(2,1)S(1)}, bf16[72,144]{1,0:T(8,128)(2,1)}, u32[]{:S(2)}) copy-start(bf16[72,144]{1,0:T(8,128)(2,1)} %constant.17.clone.cl_ref) | copy-start | bytes 62212
  22.5 4.7 %copy-start.9 = (bf16[72,144]{1,0:T(8,128)(2,1)S(1)}, bf16[72,144]{1,0:T(8,128)(2,1)}, u32[]{:S(2)}) copy-start(bf16[72,144]{1,0:T(8,128)(2,1)} %constant.16.clone.ch_ref) | copy-start | bytes 62212

commit v8 on v7

--- a/solution.py
+++ b/solution.py
@@ -250,13 +250,13 @@
         grid_ref[pl.ds(cols_ref[n], 1), :] = rows_ref[pl.ds(n, 1), :]
 
     def turn(i, carry):
-        for u in range(24):
-            k0 = i * 24 + u
+        for u in range(72):
+            k0 = i * 72 + u
             t = grid_ref[pl.ds(pl.multiple_of(k0 * KZ, 8), KZ), :].T[0:40]
             out_ref[pl.ds(k0, 40, stride=KZ), :] = jnp.concatenate([t, jnp.zeros((40, 128 - KZ), F32)], axis=1)
         return carry
 
-    lax.fori_loop(0, KZ // 24, turn, 0)
+    lax.fori_loop(0, KZ // 72, turn, 0)
 
 
 def grid(rows, cols):
@@ -443,8 +443,10 @@
             for t in range(3):
                 given[4 * j + o, 5 * t : 5 * t + 5, :] = packed[j, o, 0:5, 128 * t : 128 * (t + 1)]
     moves = []
-    for i, target in enumerate(targets):
-        xx, yy, cc = target
+    farthest = sorted(range(len(targets)), key=lambda i: -sum(min(v, 4 - v) for v in TARGETS[i][:2]))
+    for i in farthest:
+        xx, yy, cc = targets[i]
+        target = targets[i]
         to = 4 * (2 * xx + yy % 2) + 2 * (yy // 2) + cc
         moves.append(copy(given.at[to], got.at[slot], got_s.at[i], got_r.at[i], device(*target)))
     got[slot] = given[slot]
@@ -456,9 +458,9 @@
             for t in range(3):
                 turned[z : z + COUNT[o], 128 * t : 128 * (t + 1)] = got[4 * j + o, 5 * t : 5 * t + COUNT[o], :]
     rh, rl = split(turned[...].T)
+    value = dot(rh, mh) + dot(rl, mh) + dot(rh, ml)
     for g in range(9):
-        a, b = rh[36 * g : 36 * g + 36], rl[36 * g : 36 * g + 36]
-        out_ref[g] = dot(a, mh) + dot(b, mh) + dot(a, ml)
+        out_ref[g] = value[36 * g : 36 * g + 36]
     for one in started:
         one.wait_send()
 

time: 60.8 us -> 59.8 us (0.984)
  Pallas kernels: 57.2 us -> 56.2 us
    pallas_call x1, Pallas kernels: 32.6 us -> 31.9 us  [density(): pl.pallas_call(density_kernel, out_shape=jax.ShapeDtypeStruct((9, 36, NF)...]
where the time goes in v8:
time: 59.8 us; the launch traced here: 59.6 us
  Pallas kernels  56.2 us (94%)
  local copies, waits for them, and re-layouts  2.6 us (4%)
  between operations  0.81 us (1%)
    pallas_call x1, Pallas kernels, density(): pl.pallas_call(density_kernel, out_shape=jax.ShapeDtypeStruct((9, 36, NF)...  31.9 us
    pallas_call x1, Pallas kernels, lines(): pl.pallas_call(lines_kernel, out_shape=jax.ShapeDtypeStruct((NCOLS, 128),...  20 us
    pallas_call x1, Pallas kernels, grid(): pl.pallas_call(grid_kernel, out_shape=jax.ShapeDtypeStruct((40 * KZ, 128)...  4.35 us
    unnamed x21, local copies, waits for them, and re-layouts  2.6 us

profile of v8, /device:TPU:1, one launch (start us, length us, event | category | flops | bytes accessed | tf_op | source)
XLA Modules:
  0.0 59.6 jit_solution(6910246179967255039)
XLA Ops:
  0.7 0.0 copy-start
  0.7 1.0 %copy-done = f32[1,2,72,648]{3,2,1,0:T(8,128)S(1)} copy-done((f32[1,2,72,648]{3,2,1,0:T(8,128)S(1)}, f32[1,2,72,648]{3,2,1,0:T(8,128)}, u32[]{:S(2)}) %copy-start) | copy-done | bytes 373272
  1.7 0.0 copy-start.5
  1.7 0.7 %copy-done.5 = s32[5184]{0:T(1024)S(1)} copy-done((s32[5184]{0:T(1024)S(1)}, s32[5184]{0:T(1024)}, u32[]{:S(2)}) %copy-start.5) | copy-done | bytes 20760
  2.4 20.0 %shard_map.109.rows_ref = f32[5184,128]{1,0:T(8,128)S(1)} custom-call(f32[1,2,72,648]{3,2,1,0:T(8,128)S(1)} %copy-done, s32[5184]{0:T(1024)S(1)} %copy-done.5, s32[1]{0:T(128)S(6)} %copy.13.occ_ref), custom_call_target="tpu_custom_call" | custom-call | tf_op jit(solution)/shard_map/pallas_call | solution.py:231
  22.4 0.0 copy-start.1
  22.4 0.0 copy-start.2
  22.4 0.0 copy-start.3
  22.5 0.0 copy-start.4
  22.5 0.0 copy-start.6
  22.5 0.0 copy-start.7
  22.5 0.0 copy-start.8
  22.5 0.0 copy-start.9
  22.5 4.3 %shard_map.110.g_ref = f32[2880,128]{1,0:T(8,128)S(1)} custom-call(f32[5184,128]{1,0:T(8,128)S(1)} %shard_map.109.rows_ref, s32[5184]{0:T(1024)S(1)} %copy-done.5), custom_call_target="tpu_custom_call" | custom-call | tf_op jit(solution)/shard_map/pallas_call | solution.py:264
  26.9 0.0 copy-done.1
  26.9 0.0 copy-done.2
  26.9 0.0 copy-done.3
  26.9 0.0 copy-done.4
  26.9 0.0 copy-done.6
  26.9 0.0 copy-done.7
  26.9 0.0 copy-done.8
  26.9 0.0 copy-done.9
  27.0 31.9 %shard_map.111 = f32[9,36,288]{2,1,0:T(8,128)S(1)} custom-call(f32[2880,128]{1,0:T(8,128)S(1)} %shard_map.110.g_ref, bf16[72,144]{1,0:T(8,128)(2,1)S(1)} %copy-done.9, bf16[72,144]{1,0:T(8,128)(2,1)S(1)} %copy-done.8, bf16[72,144]{1,0:T(8,128)(2,1)S(1)} %copy-done.7, bf16[72,144]{1,0:T(8,128)(2,1)S(1)} %copy-done.6, bf16[288,432]{1,0:T(8,128)(2,1)S(1)} %copy-done.2, ...), custom_call_target="tpu_custom_call" | custom-call | tf_op jit(solution)/shard_map/pallas_call | solution.py:475
  58.8 0.8 %copy.14 = f32[9,36,288]{2,1,0:T(8,128)} copy(f32[9,36,288]{2,1,0:T(8,128)S(1)} %shard_map.111) | data formatting | bytes 746496
Async XLA Ops:
  0.7 1.0 %copy-start = (f32[1,2,72,648]{3,2,1,0:T(8,128)S(1)}, f32[1,2,72,648]{3,2,1,0:T(8,128)}, u32[]{:S(2)}) copy-start(f32[1,2,72,648]{3,2,1,0:T(8,128)} %coef.1) | copy-start | bytes 1119748
  1.7 0.7 %copy-start.5 = (s32[5184]{0:T(1024)S(1)}, s32[5184]{0:T(1024)}, u32[]{:S(2)}) copy-start(s32[5184]{0:T(1024)} %cols_ref.1) | copy-start | bytes 62212
  22.4 4.5 %copy-start.1 = (bf16[320,432]{1,0:T(8,128)(2,1)S(1)}, bf16[320,432]{1,0:T(8,128)(2,1)}, u32[]{:S(2)}) copy-start(bf16[320,432]{1,0:T(8,128)(2,1)} %constant.21.clone.m3_ref) | copy-start | bytes 829444
  22.4 4.5 %copy-start.2 = (bf16[288,432]{1,0:T(8,128)(2,1)S(1)}, bf16[288,432]{1,0:T(8,128)(2,1)}, u32[]{:S(2)}) copy-start(bf16[288,432]{1,0:T(8,128)(2,1)} %constant.20.clone.t2_ref) | copy-start | bytes 746500
  22.4 4.5 %copy-start.3 = (bf16[144,288]{1,0:T(8,128)(2,1)S(1)}, bf16[144,288]{1,0:T(8,128)(2,1)}, u32[]{:S(2)}) copy-start(bf16[144,288]{1,0:T(8,128)(2,1)} %constant.23.clone.ml_ref) | copy-start | bytes 248836
  22.5 4.5 %copy-start.4 = (bf16[144,288]{1,0:T(8,128)(2,1)S(1)}, bf16[144,288]{1,0:T(8,128)(2,1)}, u32[]{:S(2)}) copy-start(bf16[144,288]{1,0:T(8,128)(2,1)} %constant.22.clone.mh_ref) | copy-start | bytes 248836
  22.5 4.4 %copy-start.6 = (bf16[72,144]{1,0:T(8,128)(2,1)S(1)}, bf16[72,144]{1,0:T(8,128)(2,1)}, u32[]{:S(2)}) copy-start(bf16[72,144]{1,0:T(8,128)(2,1)} %constant.19.clone.sl_ref) | copy-start | bytes 62212
  22.5 4.4 %copy-start.7 = (bf16[72,144]{1,0:T(8,128)(2,1)S(1)}, bf16[72,144]{1,0:T(8,128)(2,1)}, u32[]{:S(2)}) copy-start(bf16[72,144]{1,0:T(8,128)(2,1)} %constant.18.clone.sh_ref) | copy-start | bytes 62212
  22.5 4.4 %copy-start.8 = (bf16[72,144]{1,0:T(8,128)(2,1)S(1)}, bf16[72,144]{1,0:T(8,128)(2,1)}, u32[]{:S(2)}) copy-start(bf16[72,144]{1,0:T(8,128)(2,1)} %constant.17.clone.cl_ref) | copy-start | bytes 62212
  22.5 4.4 %copy-start.9 = (bf16[72,144]{1,0:T(8,128)(2,1)S(1)}, bf16[72,144]{1,0:T(8,128)(2,1)}, u32[]{:S(2)}) copy-start(bf16[72,144]{1,0:T(8,128)(2,1)} %constant.16.clone.ch_ref) | copy-start | bytes 62212

commit v9 on v8

--- a/solution.py
+++ b/solution.py
@@ -90,8 +90,8 @@
 TARGETS = [
     (dx, dy, dc)
     for dx, odd in GROUPS
+    for dc in (1, 0)
     for dy in (odd + 2, odd)
-    for dc in (1, 0)
     if (dx, dy, dc) != (0, 0, 0)
 ]
 
@@ -276,7 +276,7 @@
 
 def density_kernel(
     g_ref, ch_ref, cl_ref, sh_ref, sl_ref, t2_ref, m3_ref, mh_ref, ml_ref, out_ref,
-    hall_ref, part, held, sent, acc, left, fine, packed, given, got, turned,
+    hall_ref, part, held, sent, acc, left, fine, packed, given, got,
     ring_s, ring_r, got_s, got_r,
 ):
     band, me = lax.axis_index("band"), lax.axis_index("fft")
@@ -456,11 +456,7 @@
         for o in range(4):
             z = NP * j + FIRST[o]
             for t in range(3):
-                turned[z : z + COUNT[o], 128 * t : 128 * (t + 1)] = got[4 * j + o, 5 * t : 5 * t + COUNT[o], :]
-    rh, rl = split(turned[...].T)
-    value = dot(rh, mh) + dot(rl, mh) + dot(rh, ml)
-    for g in range(9):
-        out_ref[g] = value[36 * g : 36 * g + 36]
+                out_ref[z : z + COUNT[o], 128 * t : 128 * (t + 1)] = got[4 * j + o, 5 * t : 5 * t + COUNT[o], :]
     for one in started:
         one.wait_send()
 
@@ -474,7 +470,7 @@
     n = len(TARGETS)
     return pl.pallas_call(
         density_kernel,
-        out_shape=jax.ShapeDtypeStruct((9, 36, NF), F32),
+        out_shape=jax.ShapeDtypeStruct((NC, 384), F32),
         in_specs=[vmem] * 9,
         out_specs=vmem,
         scratch_shapes=[
@@ -488,7 +484,6 @@
             pltpu.VMEM((8, 4, 8, 384), F32),
             pltpu.VMEM((32, 16, 128), F32),
             pltpu.VMEM((32, 16, 128), F32),
-            pltpu.VMEM((NC, 384), F32),
             dma((2, 4, 3)), dma((2, 4, 3)),
             dma((n,)), dma((n,)),
         ],
@@ -498,9 +493,29 @@
     )(g, *(jnp.asarray(t) for t in tables))
 
 
+def third_kernel(turned_ref, mh_ref, ml_ref, out_ref):
+    rh, rl = split(turned_ref[...].T)
+    mh, ml = mh_ref[...], ml_ref[...]
+    value = dot(rh, mh) + dot(rl, mh) + dot(rh, ml)
+    for g in range(9):
+        out_ref[g] = value[36 * g : 36 * g + 36]
+
+
+def third(turned):
+    mh, ml = hi_lo(interpolation().T)
+    vmem = pl.BlockSpec(memory_space=pltpu.VMEM)
+    return pl.pallas_call(
+        third_kernel,
+        out_shape=jax.ShapeDtypeStruct((9, 36, NF), F32),
+        in_specs=[vmem] * 3,
+        out_specs=vmem,
+        compiler_params=pltpu.CompilerParams(vmem_limit_bytes=GRID_VMEM),
+    )(turned, jnp.asarray(mh), jnp.asarray(ml))
+
+
 def local(coefficients, col_index, occupation):
     rows = lines(coefficients, col_index, occupation)
-    return density(grid(rows, col_index))
+    return third(density(grid(rows, col_index)))
 
 
 def solution(mesh):

time: 59.8 us -> 59.7 us (level)
  local copies, waits for them, and re-layouts: 2.6 us -> 1.8 us
  Pallas kernels: 56.2 us -> 56.9 us
    pallas_call x1 -> x2, Pallas kernels: 31.9 us -> 32.8 us  [the longest x1 31.5 us: density(): pl.pallas_call(density_kernel, out_shape=jax.ShapeDtypeStruct((NC, 384),...]
    unnamed x21 -> x20, local copies, waits for them, and re-layouts: 2.6 us -> 1.8 us
where the time goes in v9:
time: 59.7 us; the launch traced here: 59.5 us
  Pallas kernels  56.9 us (95%)
  local copies, waits for them, and re-layouts  1.8 us (3%)
  between operations  0.81 us (1%)
    pallas_call x1, Pallas kernels, density(): pl.pallas_call(density_kernel, out_shape=jax.ShapeDtypeStruct((NC, 384),...  31.5 us
    pallas_call x1, Pallas kernels, lines(): pl.pallas_call(lines_kernel, out_shape=jax.ShapeDtypeStruct((NCOLS, 128),...  19.7 us
    pallas_call x1, Pallas kernels, grid(): pl.pallas_call(grid_kernel, out_shape=jax.ShapeDtypeStruct((40 * KZ, 128)...  4.35 us
    unnamed x20, local copies, waits for them, and re-layouts  1.8 us
    pallas_call x1, Pallas kernels, third(): pl.pallas_call(third_kernel, out_shape=jax.ShapeDtypeStruct((9, 36, NF),...  1.32 us

profile of v9, /device:TPU:1, one launch (start us, length us, event | category | flops | bytes accessed | tf_op | source)
XLA Modules:
  0.0 59.5 jit_solution(2463818355242863296)
XLA Ops:
  0.7 0.0 copy-start
  0.7 1.0 %copy-done = f32[1,2,72,648]{3,2,1,0:T(8,128)S(1)} copy-done((f32[1,2,72,648]{3,2,1,0:T(8,128)S(1)}, f32[1,2,72,648]{3,2,1,0:T(8,128)}, u32[]{:S(2)}) %copy-start) | copy-done | bytes 373272
  1.7 0.0 copy-start.5
  1.7 0.7 %copy-done.5 = s32[5184]{0:T(1024)S(1)} copy-done((s32[5184]{0:T(1024)S(1)}, s32[5184]{0:T(1024)}, u32[]{:S(2)}) %copy-start.5) | copy-done | bytes 20760
  2.4 19.7 %shard_map.127.rows_ref = f32[5184,128]{1,0:T(8,128)S(1)} custom-call(f32[1,2,72,648]{3,2,1,0:T(8,128)S(1)} %copy-done, s32[5184]{0:T(1024)S(1)} %copy-done.5, s32[1]{0:T(128)S(6)} %copy.14.occ_ref), custom_call_target="tpu_custom_call" | custom-call | tf_op jit(solution)/shard_map/pallas_call | solution.py:231
  22.1 0.0 copy-start.1
  22.2 0.0 copy-start.2
  22.2 0.0 copy-start.3
  22.2 0.0 copy-start.4
  22.2 0.0 copy-start.6
  22.2 0.0 copy-start.7
  22.2 0.0 copy-start.8
  22.2 0.0 copy-start.9
  22.2 4.3 %shard_map.128.g_ref = f32[2880,128]{1,0:T(8,128)S(1)} custom-call(f32[5184,128]{1,0:T(8,128)S(1)} %shard_map.127.rows_ref, s32[5184]{0:T(1024)S(1)} %copy-done.5), custom_call_target="tpu_custom_call" | custom-call | tf_op jit(solution)/shard_map/pallas_call | solution.py:264
  26.6 0.0 copy-done.1
  26.6 0.0 copy-done.2
  26.6 0.0 copy-done.3
  26.6 0.0 copy-done.4
  26.6 0.0 copy-done.6
  26.6 0.0 copy-done.7
  26.7 0.0 copy-done.8
  26.7 0.0 copy-done.9
  26.7 31.5 %shard_map.129.turned_ref = f32[144,384]{1,0:T(8,128)S(1)} custom-call(f32[2880,128]{1,0:T(8,128)S(1)} %shard_map.128.g_ref, bf16[72,144]{1,0:T(8,128)(2,1)S(1)} %copy-done.9, bf16[72,144]{1,0:T(8,128)(2,1)S(1)} %copy-done.8, bf16[72,144]{1,0:T(8,128)(2,1)S(1)} %copy-done.7, bf16[72,144]{1,0:T(8,128)(2,1)S(1)} %copy-done.6, bf16[288,432]{1,0:T(8,128)(2,1)S(1)} %copy-done.4, ...), custom_call_target="tpu_custom_call" | custom-call | tf_op jit(solution)/shard_map/pallas_call | solution.py:471
  58.2 1.3 %shard_map.130 = f32[9,36,288]{2,1,0:T(8,128)} custom-call(f32[144,384]{1,0:T(8,128)S(1)} %shard_map.129.turned_ref, bf16[144,288]{1,0:T(8,128)(2,1)S(1)} %copy-done.2, bf16[144,288]{1,0:T(8,128)(2,1)S(1)} %copy-done.1), custom_call_target="tpu_custom_call" | custom-call | tf_op jit(solution)/shard_map/pallas_call | solution.py:507
Async XLA Ops:
  0.7 1.0 %copy-start = (f32[1,2,72,648]{3,2,1,0:T(8,128)S(1)}, f32[1,2,72,648]{3,2,1,0:T(8,128)}, u32[]{:S(2)}) copy-start(f32[1,2,72,648]{3,2,1,0:T(8,128)} %coef.1) | copy-start | bytes 1119748
  1.7 0.7 %copy-start.5 = (s32[5184]{0:T(1024)S(1)}, s32[5184]{0:T(1024)}, u32[]{:S(2)}) copy-start(s32[5184]{0:T(1024)} %cols_ref.1) | copy-start | bytes 62212
  22.1 4.5 %copy-start.1 = (bf16[144,288]{1,0:T(8,128)(2,1)S(1)}, bf16[144,288]{1,0:T(8,128)(2,1)}, u32[]{:S(2)}) copy-start(bf16[144,288]{1,0:T(8,128)(2,1)} %constant.23.clone.ml_ref) | copy-start | bytes 248836
  22.2 4.5 %copy-start.2 = (bf16[144,288]{1,0:T(8,128)(2,1)S(1)}, bf16[144,288]{1,0:T(8,128)(2,1)}, u32[]{:S(2)}) copy-start(bf16[144,288]{1,0:T(8,128)(2,1)} %constant.22.clone.mh_ref) | copy-start | bytes 248836
  22.2 4.5 %copy-start.3 = (bf16[320,432]{1,0:T(8,128)(2,1)S(1)}, bf16[320,432]{1,0:T(8,128)(2,1)}, u32[]{:S(2)}) copy-start(bf16[320,432]{1,0:T(8,128)(2,1)} %constant.21.clone.m3_ref) | copy-start | bytes 829444
  22.2 4.5 %copy-start.4 = (bf16[288,432]{1,0:T(8,128)(2,1)S(1)}, bf16[288,432]{1,0:T(8,128)(2,1)}, u32[]{:S(2)}) copy-start(bf16[288,432]{1,0:T(8,128)(2,1)} %constant.20.clone.t2_ref) | copy-start | bytes 746500
  22.2 4.4 %copy-start.6 = (bf16[72,144]{1,0:T(8,128)(2,1)S(1)}, bf16[72,144]{1,0:T(8,128)(2,1)}, u32[]{:S(2)}) copy-start(bf16[72,144]{1,0:T(8,128)(2,1)} %constant.19.clone.sl_ref) | copy-start | bytes 62212
  22.2 4.4 %copy-start.7 = (bf16[72,144]{1,0:T(8,128)(2,1)S(1)}, bf16[72,144]{1,0:T(8,128)(2,1)}, u32[]{:S(2)}) copy-start(bf16[72,144]{1,0:T(8,128)(2,1)} %constant.18.clone.sh_ref) | copy-start | bytes 62212
  22.2 4.4 %copy-start.8 = (bf16[72,144]{1,0:T(8,128)(2,1)S(1)}, bf16[72,144]{1,0:T(8,128)(2,1)}, u32[]{:S(2)}) copy-start(bf16[72,144]{1,0:T(8,128)(2,1)} %constant.17.clone.cl_ref) | copy-start | bytes 62212
  22.2 4.4 %copy-start.9 = (bf16[72,144]{1,0:T(8,128)(2,1)S(1)}, bf16[72,144]{1,0:T(8,128)(2,1)}, u32[]{:S(2)}) copy-start(bf16[72,144]{1,0:T(8,128)(2,1)} %constant.16.clone.ch_ref) | copy-start | bytes 62212
